TPU v7x, 512 devices: a whole 4x8x8 slice. The times are simulated.
512 devices in a mesh: lat: 64 (over z, y), lon: 8 (over x, core).
Axes of the slice: x: 4, y: 8, z: 8, core: 2. Of those that a mesh axis runs over, the one named last changes fastest.
Arguments:
- fields: bfloat16 [8192, 8, 1024], P('lat', 'lon'), may hold values from -6 to 6
- proj_x: bfloat16 [1024, 1024], P('lon'), may hold values from -0.1875 to 0.1875
- proj_z: bfloat16 [1024, 1024], P('lon'), may hold values from -0.1875 to 0.1875
- proj_bc: bfloat16 [1024, 128], P('lon'), may hold values from -0.1875 to 0.1875
- proj_dt: bfloat16 [1024, 16], P('lon'), may hold values from -1 to 1
- conv_x: float32 [4, 1024], replicated, may hold values from -3 to 3
- conv_bc: float32 [4, 128], replicated, may hold values from -3 to 3
- dt_bias: float32 [16], replicated, may hold values from -1 to 0.5
- log_rate: float32 [16], replicated, may hold values from -12 to -2.7
- norm_gain: float32 [1024], replicated, may hold values from 0.1 to 1.9
- proj_out: bfloat16 [1024, 1024], P('lon'), may hold values from -0.1875 to 0.1875
Outputs:
- mixer_out: bfloat16 [8192, 8, 1024], P('lat', 'lon')
All inputs are finite; a program needn't handle non-finite values.
Results may differ from a plain program's by a relative error of at most 0.012.
Values may be sent and summed in bfloat16 or wider, within the bound.
No kernel may reach another device: no remote copies, remote signals or barrier semaphores. Data moves between devices by JAX's collectives and lax.ppermute only.
A program may use at most 64 MiB of HBM per device.

v0:
```python
import jax
import jax.numpy as jnp
from jax import lax
from jax.experimental import pallas as pl
from jax.experimental.pallas import tpu as pltpu
from jax.sharding import Mesh
from jax.sharding import PartitionSpec as P


LAT = ("z", "y")
EPS = 1e-05
HIGHEST = lax.Precision.HIGHEST
F32 = jnp.float32
BF16 = jnp.bfloat16
HALO = 16
LANES = 128
SUB = 8
TILE = 256


def dot(a, b, **kw):
    return jnp.dot(a, b, preferred_element_type=F32, **kw)


def dot_nt(a, b):
    return lax.dot_general(a, b, (((1,), (1,)), ((), ())), preferred_element_type=F32)


def dot_tn(a, b):
    return lax.dot_general(a, b, (((0,), (0,)), ((), ())), preferred_element_type=F32)


def iota(shape, dim):
    return lax.broadcasted_iota(jnp.int32, shape, dim)


def silu(v):
    return v / (1.0 + jnp.exp(-v))


def halves(v):
    high = v.astype(BF16)
    return high, (v - high.astype(F32)).astype(BF16)


def spread(v, width):
    heads = v.shape[1]
    shape = (heads, width)
    pick = (iota(shape, 1) // (width // heads) == iota(shape, 0)).astype(BF16)
    high, low = halves(v)
    return dot(high, pick) + dot(low, pick)


def chunk(ref, index):
    return ref[:, pl.ds(pl.multiple_of(index * LANES, LANES), LANES)]


def ordered(ref, order, n):
    return jnp.concatenate([chunk(ref, order[j]) for j in range(n)], 1)


def stacked(refs, rows, columns):
    return jnp.concatenate([r[rows, columns] for r in refs], 0)


def pack_kernel(x_ref, bc_ref, dt_ref, out):
    k = x_ref.shape[0]
    blocks = x_ref.shape[1] // LANES
    part = k // blocks
    bc = jnp.concatenate([bc_ref[j * part : (j + 1) * part, :] for j in range(blocks)], 1)
    for i in range(out.shape[0]):
        out[i, :k, :] = x_ref[...]
        out[i, k : k + part, :] = bc
        out[i, k + part :, :LANES] = dt_ref[...]
        out[i, k + part :, LANES:] = jnp.zeros((part, x_ref.shape[1] - LANES), BF16)


def project_kernel(
    order, f_ref, halo_ref, wa, wb, conv_x, conv_bc, bias, rate,
    x_out, bc_out, dt_out, cum_out, msg_out, pre,
):
    rows, width = x_out.shape
    heads = bias.shape[1]
    half = width // 2
    k = LANES
    n = 2 * wa.shape[0]
    blocks = width // LANES
    part = k // blocks
    shards = [r.at[i] for r in (wa, wb) for i in range(n // 2)]
    src = jnp.concatenate([ordered(halo_ref, order, n), ordered(f_ref, order, n)], 0)
    first = HALO - conv_x.shape[0] + 1

    def conv(at, wide, taps):
        acc = taps[0:1, :] * pre[first : first + rows, at : at + wide]
        for i in range(1, conv_x.shape[0]):
            acc = acc + taps[i : i + 1, :] * pre[first + i : first + i + rows, at : at + wide]
        return silu(acc)

    w_dt = jnp.concatenate([r[i, k + part :, :LANES] for r in (wa, wb) for i in range(n // 2)], 1)
    dt_pre = dot_nt(src[HALO:], w_dt).astype(BF16).astype(F32)
    step = jax.nn.softplus(dt_pre + bias[...])
    log_step = -jnp.exp(rate[...]) * step
    lower = (iota((rows, rows), 0) >= iota((rows, rows), 1)).astype(F32)
    cum = dot(lower, log_step, precision=HIGHEST)
    dt_out[...] = step
    cum_out[...] = cum
    last = cum[rows - 1 : rows, :]
    weight = spread(jnp.exp(last - cum) * step, width)

    w_bc = jnp.concatenate(
        [
            r[i, k : k + part, j * LANES : (j + 1) * LANES]
            for r in (wa, wb)
            for i in range(n // 2)
            for j in range(blocks)
        ],
        0,
    )
    pre[:, width:] = dot(src, w_bc).astype(BF16).astype(F32)
    bc = conv(width, LANES, conv_bc[...])
    bc_out[...] = bc.astype(BF16)
    left = iota((rows, LANES), 1) < LANES // 2
    b0 = jnp.where(left, bc, 0.0)
    b = (b0.astype(BF16), pltpu.roll(b0, LANES // 2, 1).astype(BF16))

    def end(at, q):
        pre[:, at : at + TILE] = (
            dot(src, stacked(shards, slice(0, k), slice(at, at + TILE))).astype(BF16).astype(F32)
        )
        x = conv(at, TILE, conv_x[:, at : at + TILE]).astype(BF16)
        x_out[:, at : at + TILE] = x
        xw = (x.astype(F32) * weight[:, at : at + TILE]).astype(BF16)
        return dot_tn(xw, b[q])

    for at in range(0, half, TILE):
        t = end(at, 0) + end(half + at, 1)
        msg_out[at // SUB : (at + TILE) // SUB, :SUB, :] = t.reshape(TILE // SUB, SUB, LANES).astype(BF16)
    pairs = heads // 2
    mine = iota((pairs, heads), 1) % pairs == iota((pairs, heads), 0)
    pick = (iota((heads, LANES), 1) // (LANES // 2) == iota((heads, LANES), 0) // pairs).astype(BF16)
    high, low = (dot(jnp.where(mine, v.astype(F32), 0.0).astype(BF16), pick) for v in halves(last))
    row = iota((SUB, LANES), 0)
    each = msg_out.shape[0] // pairs
    for j in range(pairs):
        tail = jnp.where(row == 0, high[j : j + 1, :], jnp.where(row == 1, low[j : j + 1, :], 0.0))
        for i in range(each):
            msg_out[j * each + i, SUB:, :] = tail.astype(BF16)


def within_kernel(x_ref, bc_ref, dt_ref, cum_ref, y_out):
    rows, _ = x_ref.shape
    heads = dt_ref.shape[1]
    state = bc_ref.shape[1] // 2
    scores = dot_nt(bc_ref[:, state:], bc_ref[:, :state])
    causal = iota((rows, rows), 0) >= iota((rows, rows), 1)
    cum = cum_ref[...]
    cum_t = cum.T
    dt_t = dt_ref[...].T
    left = iota((rows, LANES), 1) < LANES // 2
    for pair in range(heads // 2):
        w = []
        for h in (2 * pair, 2 * pair + 1):
            gap = jnp.where(causal, cum[:, h : h + 1] - cum_t[h : h + 1, :], -jnp.inf)
            w.append((jnp.exp(gap) * (scores * dt_t[h : h + 1, :])).astype(BF16))
        xp = x_ref[:, pair * LANES : (pair + 1) * LANES]
        zero = jnp.zeros_like(xp)
        both = jnp.concatenate([jnp.where(left, xp, zero), jnp.where(left, zero, xp)], 0)
        y_out[:, pair * LANES : (pair + 1) * LANES] = dot(jnp.concatenate(w, 1), both)


def bands_kernel(r_ref, e_out):
    carry = jnp.zeros(e_out.shape[1:], F32)
    for b in range(e_out.shape[0]):
        e_out[b] = carry.astype(BF16)
        tail = r_ref[b, SUB:, :].astype(F32)
        carry = jnp.exp(tail[0:1, :] + tail[1:2, :]) * carry + r_ref[b, :SUB, :].astype(F32)


def gate_kernel(order, f_ref, *refs):
    shards, out = refs[:-1], refs[-1]
    src = ordered(f_ref, order, len(shards))
    for at in range(0, out.shape[1], TILE):
        w = stacked(shards, slice(0, LANES), slice(at, at + TILE))
        out[:, at : at + TILE] = silu(dot(src, w).astype(BF16).astype(F32))


def finish_kernel(order, y_ref, in_ref, bc_ref, cum_ref, gate_ref, gain, *refs):
    shards, (out, hidden) = refs[:-2], refs[-2:]
    rows, width = y_ref.shape
    half = width // 2
    bc = bc_ref[...].astype(F32)
    left = iota((rows, LANES), 1) < LANES // 2
    c1 = jnp.where(left, 0.0, bc)
    c = (pltpu.roll(c1, LANES // 2, 1).astype(BF16), c1.astype(BF16))
    grown = spread(jnp.exp(cum_ref[...]), width)
    square = jnp.zeros((rows, 1), F32)
    parts = []
    for at in range(0, width, TILE):
        inner = in_ref[at % half : at % half + TILE, :]
        y = y_ref[:, at : at + TILE] + dot_nt(c[at // half], inner) * grown[:, at : at + TILE]
        g = y * gate_ref[:, at : at + TILE]
        square = square + jnp.sum(g * g, -1, keepdims=True)
        parts.append(g)
    scale = lax.rsqrt(square / width + EPS)
    for i, at in enumerate(range(0, width, TILE)):
        hidden[:, at : at + TILE] = (parts[i] * scale * gain[:, at : at + TILE]).astype(BF16)
    src = ordered(hidden, order, len(shards))
    for at in range(0, out.shape[1], TILE):
        w = stacked(shards, slice(LANES, 2 * LANES), slice(at, at + TILE))
        out[:, at : at + TILE] = dot(src, w).astype(BF16)


def call(body, outs, args, smem=0, scratch=(), flops=0):
    vmem = pl.BlockSpec(memory_space=pltpu.VMEM)
    specs = [pl.BlockSpec(memory_space=pltpu.SMEM)] * smem + [vmem] * (len(args) - smem)
    nbytes = sum(a.size * a.dtype.itemsize for a in args)
    return pl.pallas_call(
        body,
        out_shape=outs,
        in_specs=specs,
        out_specs=jax.tree.map(lambda _: vmem, outs),
        scratch_shapes=list(scratch),
        compiler_params=pltpu.CompilerParams(vmem_limit_bytes=24 * 2**20),
        cost_estimate=pl.CostEstimate(flops=flops, bytes_accessed=nbytes, transcendentals=0),
    )(*args)


def other_core(block):
    return lax.ppermute(block, "c", [(0, 1), (1, 0)])


def local(
    fields, proj_x, proj_z, proj_bc, proj_dt, conv_x, conv_bc, dt_bias, log_rate, norm_gain, proj_out
):
    rows, _, depth = fields.shape
    heads = log_rate.shape[0]
    width = proj_x.shape[1]
    state = proj_bc.shape[1] // 2
    n_x = lax.axis_size("x")
    bands = lax.axis_size(LAT)
    f = fields.reshape(rows, depth)
    sds = jax.ShapeDtypeStruct

    k = proj_x.shape[0]
    first = call(
        pack_kernel,
        sds((n_x, k + 2 * k * LANES // width, width), BF16),
        [proj_x, proj_bc, proj_dt.T],
    )
    w1a = lax.all_to_all(first, "x", 0, 0)
    halo = lax.ppermute(f[rows - HALO :], LAT, [(i, i + 1) for i in range(bands - 1)])
    x_at, c_at = lax.axis_index("x"), lax.axis_index("c")
    x_all = jnp.arange(n_x)
    order = jnp.concatenate([x_all * 2 + c_at, x_all * 2 + 1 - c_at]).astype(jnp.int32)
    x_near = (x_at - x_all + n_x) % n_x
    order2 = jnp.concatenate([x_near * 2 + c_at, x_near * 2 + 1 - c_at]).astype(jnp.int32)
    second = jnp.concatenate([proj_z, proj_out], 0)
    w1a, halo, second, order, order2 = lax.optimization_barrier((w1a, halo, second, order, order2))
    w1b = other_core(w1a)
    w2a, w2b = [second], []
    for d in range(1, n_x):
        w2a.append(lax.ppermute(second, "x", [(i, (i + d) % n_x) for i in range(n_x)]))
    for d in range(n_x):
        w2b.append(other_core(w2a[d]))

    x_act, bc_act, step, cum, msg = call(
        project_kernel,
        (
            sds((rows, width), BF16),
            sds((rows, 2 * state), BF16),
            sds((rows, heads), F32),
            sds((rows, heads), F32),
            sds((bands, 2 * SUB, LANES), BF16),
        ),
        [order, f, halo, w1a, w1b, conv_x, conv_bc, dt_bias[None], log_rate[None]],
        smem=1,
        scratch=[pltpu.VMEM((HALO + rows, width + 2 * state), F32)],
        flops=2 * rows * depth * (width + 2 * LANES),
    )
    got = lax.all_to_all(msg, LAT, 0, 0)
    y = call(
        within_kernel,
        sds((rows, width), F32),
        [x_act, bc_act, step, cum],
        flops=2 * rows * rows * width * 2,
    )
    entering = call(
        bands_kernel, sds((bands, SUB, LANES), BF16), [got], flops=bands * SUB * LANES * 100
    )
    incoming = lax.all_to_all(entering, LAT, 0, 0)
    incoming = incoming.reshape(bands * SUB, LANES)
    gate = call(
        gate_kernel,
        sds((rows, width), F32),
        [order2, f, *w2a, *w2b],
        smem=1,
        flops=2 * rows * depth * width,
    )
    out = call(
        finish_kernel,
        sds((rows, depth), BF16),
        [order2, y, incoming, bc_act, cum, gate, norm_gain[None], *w2a, *w2b],
        smem=1,
        scratch=[pltpu.VMEM((rows, width), BF16)],
        flops=2 * rows * depth * width,
    )
    return out.reshape(rows, 1, depth)


def solution(mesh):
    finer = Mesh(mesh.devices.reshape(8, 8, 4, 2), ("z", "y", "x", "c"))
    lat, lon = P(LAT, ("x", "c"), None), P(("x", "c"), None)
    return jax.shard_map(
        local,
        mesh=finer,
        in_specs=(lat, lon, lon, lon, lon, P(), P(), P(), P(), P(), lon),
        out_specs=lat,
        check_vma=False,
    )
```

profile of v0, /device:TPU:2, one launch (start us, length us, event | category | flops | bytes accessed | tf_op | source)
XLA Modules:
  0.0 103.0 jit_solution(8859679500826271777)
XLA Ops:
  0.0 0.9 copy-done.10
  1.0 0.8 copy-done.19
  1.7 0.7 copy-done.21
  2.4 1.2 %shard_map.109 = bf16[4,160,1024]{2,1,0:T(8,128)(2,1)} custom-call(bf16[128,1024]{1,0:T(8,128)(2,1)S(1)} %copy-done.10, bf16[128,128]{1,0:T(8,128)(2,1)S(1)} %copy-done.19, bf16[16,128]{1,0:T(8,128)(2,1)S(1)} %bitcast.12), custom_call_target="tpu_custom_call" | custom-call | bytes 299008 | tf_op jit(solution)/shard_map/pallas_call | solution.py:217
  3.6 0.0 copy-start.24
  3.6 0.0 copy-start.25
  3.6 9.5 %all-to-all-start = ((bf16[4,160,1024]{2,1,0:T(8,128)(2,1)}), bf16[4,160,1024]{2,1,0:T(8,128)(2,1)S(1)}, u32[]{:S(2)}, u32[]{:S(2)}) async-start(bf16[4,160,1024]{2,1,0:T(8,128)(2,1)} %shard_map.109), calls=%async_computation | async-start | bytes 2621440 | tf_op jit(solution)/shard_map/all_to_all | solution.py:250
  13.2 0.8 slice_bitcast_fusion
  13.9 1.3 %collective-permute-start = (bf16[16,1024]{1,0:T(8,128)(2,1)S(1)}, bf16[16,1024]{1,0:T(8,128)(2,1)S(1)}, u32[]{:S(2)}, u32[]{:S(2)}) collective-permute-start(bf16[16,1024]{1,0:T(8,128)(2,1)S(1)} %slice_bitcast_fusion), channel_id=1, source_target_pairs={{0,8},{8,16},{16,24},{24,32},{32,40},{40,48},{48,56},{56,64},{64,7... | collective-permute-start | bytes 98312 | tf_op jit(solution)/shard_map/ppermute | solution.py:251
  15.2 0.1 pad_add_fusion.order
  15.4 0.1 pad_add_fusion.1.order
  15.4 1.3 %collective-permute-done.halo_ref = bf16[16,1024]{1,0:T(8,128)(2,1)S(1)} collective-permute-done((bf16[16,1024]{1,0:T(8,128)(2,1)S(1)}, bf16[16,1024]{1,0:T(8,128)(2,1)S(1)}, u32[]{:S(2)}, u32[]{:S(2)}) %collective-permute-start) | collective-permute-done | bytes 32800 | tf_op jit(solution)/shard_map/ppermute | solution.py:251
  16.8 8.3 %all-to-all-done.wa = bf16[4,160,1024]{2,1,0:T(8,128)(2,1)S(1)} async-done(((bf16[4,160,1024]{2,1,0:T(8,128)(2,1)}), bf16[4,160,1024]{2,1,0:T(8,128)(2,1)S(1)}, u32[]{:S(2)}, u32[]{:S(2)}) %all-to-all-start) | async-done | bytes 1310752 | tf_op jit(solution)/shard_map/all_to_all | solution.py:250
  25.0 1.9 %collective-permute-start.1 = (bf16[4,160,1024]{2,1,0:T(8,128)(2,1)S(1)}, bf16[4,160,1024]{2,1,0:T(8,128)(2,1)S(1)}, u32[]{:S(2)}, u32[]{:S(2)}) collective-permute-start(bf16[4,160,1024]{2,1,0:T(8,128)(2,1)S(1)} %all-to-all-done.wa), channel_id=1, source_target_pairs={{0,1},{1,0},{2,3},{3,2},{4,5},{5,4},{6,7},{7,6},{8,9},{9,8},{10,11... | collective-permute-start | bytes 3932168 | tf_op jit(solution)/shard_map/ppermute | solution.py:229
  27.0 1.9 %collective-permute-start.2 = (bf16[256,1024]{1,0:T(8,128)(2,1)S(1)}, bf16[256,1024]{1,0:T(8,128)(2,1)S(1)}, u32[]{:S(2)}, u32[]{:S(2)}) collective-permute-start(bf16[256,1024]{1,0:T(8,128)(2,1)S(1)} %pad_maximum_fusion.refs_0_), channel_id=1, source_target_pairs={{0,2},{2,4},{4,6},{6,0},{1,3},{3,5},{5,7},{7,1},{8,10},{10,12},{12... | collective-permute-start | bytes 1572872 | tf_op jit(solution)/shard_map/ppermute | solution.py:262
  28.9 5.4 %collective-permute-start.3 = (bf16[256,1024]{1,0:T(8,128)(2,1)S(1)}, bf16[256,1024]{1,0:T(8,128)(2,1)S(1)}, u32[]{:S(2)}, u32[]{:S(2)}) collective-permute-start(bf16[256,1024]{1,0:T(8,128)(2,1)S(1)} %pad_maximum_fusion.refs_0_), channel_id=1, source_target_pairs={{0,4},{2,6},{4,0},{6,2},{1,5},{3,7},{5,1},{7,3},{8,12},{10,14},{12... | collective-permute-start | bytes 1572872 | tf_op jit(solution)/shard_map/ppermute | solution.py:262
  34.3 2.5 %collective-permute-start.4 = (bf16[256,1024]{1,0:T(8,128)(2,1)S(1)}, bf16[256,1024]{1,0:T(8,128)(2,1)S(1)}, u32[]{:S(2)}, u32[]{:S(2)}) collective-permute-start(bf16[256,1024]{1,0:T(8,128)(2,1)S(1)} %pad_maximum_fusion.refs_0_), channel_id=1, source_target_pairs={{0,6},{2,0},{4,2},{6,4},{1,7},{3,1},{5,3},{7,5},{8,14},{10,8},{12,... | collective-permute-start | bytes 1572872 | tf_op jit(solution)/shard_map/ppermute | solution.py:262
  36.9 0.0 copy-start.4
  36.9 0.9 copy-done.4
  37.8 2.5 %shard_map.110 = (bf16[128,1024]{1,0:T(8,128)(2,1)S(1)}, bf16[128,128]{1,0:T(8,128)(2,1)S(1)}, f32[128,16]{1,0:T(8,128)S(1)}, f32[128,16]{1,0:T(8,128)S(1)}, bf16[64,16,128]{2,1,0:T(8,128)(2,1)S(1)}) custom-call(s32[8]{0:T(128)S(1)} %pad_add_fusion.order, bf16[128,1024]{1,0:T(8,128)(2,1)S(1)} %bitcast.9, bf16[16,1024]{1,0:T(8,128)(2,1)S(1)} %collective-permute-done.halo_ref, ...), custom_call_target="tpu_custom_call" | custom-call | flops 335544320 | bytes 2934944 | tf_op jit(solution)/shard_map/pallas_call | solution.py:217
  40.4 0.6 copy-done.7
  41.0 0.7 copy-done.11
  41.7 0.7 copy-done.12
  42.4 0.6 copy-done.14
  43.0 0.6 copy-done.17
  43.6 17.0 %all-to-all-start.1 = ((bf16[64,16,128]{2,1,0:T(8,128)(2,1)}), bf16[64,16,128]{2,1,0:T(8,128)(2,1)}, u32[]{:S(2)}, u32[]{:S(2)}) async-start(bf16[64,16,128]{2,1,0:T(8,128)(2,1)} %copy-done.11), calls=%async_computation.1 | async-start | bytes 524288 | tf_op jit(solution)/shard_map/all_to_all | solution.py:280
  60.6 1.9 %collective-permute-start.5 = (bf16[256,1024]{1,0:T(8,128)(2,1)S(1)}, bf16[256,1024]{1,0:T(8,128)(2,1)S(1)}, u32[]{:S(2)}, u32[]{:S(2)}) collective-permute-start(bf16[256,1024]{1,0:T(8,128)(2,1)S(1)} %pad_maximum_fusion.refs_0_), channel_id=1, source_target_pairs={{0,1},{1,0},{2,3},{3,2},{4,5},{5,4},{6,7},{7,6},{8,9},{9,8},{10,11... | collective-permute-start | bytes 1572872 | tf_op jit(solution)/shard_map/ppermute | solution.py:229
  62.5 0.0 collective-permute-done.2.refs_1_
  62.5 2.4 %collective-permute-start.6 = (bf16[256,1024]{1,0:T(8,128)(2,1)S(1)}, bf16[256,1024]{1,0:T(8,128)(2,1)S(1)}, u32[]{:S(2)}, u32[]{:S(2)}) collective-permute-start(bf16[256,1024]{1,0:T(8,128)(2,1)S(1)} %collective-permute-done.2.refs_1_), channel_id=1, source_target_pairs={{0,1},{1,0},{2,3},{3,2},{4,5},{5,4},{6,7},{7,6},{8,9},{9,8},{10,11... | collective-permute-start | bytes 1572872 | tf_op jit(solution)/shard_map/ppermute | solution.py:229
  65.0 0.0 collective-permute-done.3.refs_2_
  65.0 1.9 %collective-permute-start.7 = (bf16[256,1024]{1,0:T(8,128)(2,1)S(1)}, bf16[256,1024]{1,0:T(8,128)(2,1)}, u32[]{:S(2)}, u32[]{:S(2)}) collective-permute-start(bf16[256,1024]{1,0:T(8,128)(2,1)S(1)} %collective-permute-done.3.refs_2_), channel_id=1, source_target_pairs={{0,1},{1,0},{2,3},{3,2},{4,5},{5,4},{6,7},{7,6},{8,9},{9,8},{10,11... | collective-permute-start | bytes 1572872 | tf_op jit(solution)/shard_map/ppermute | solution.py:229
  66.9 2.4 %collective-permute-start.8 = (bf16[256,1024]{1,0:T(8,128)(2,1)S(1)}, bf16[256,1024]{1,0:T(8,128)(2,1)}, u32[]{:S(2)}, u32[]{:S(2)}) collective-permute-start(bf16[256,1024]{1,0:T(8,128)(2,1)S(1)} %collective-permute-done.4.refs_3_), channel_id=1, source_target_pairs={{0,1},{1,0},{2,3},{3,2},{4,5},{5,4},{6,7},{7,6},{8,9},{9,8},{10,11... | collective-permute-start | bytes 1572872 | tf_op jit(solution)/shard_map/ppermute | solution.py:229
  69.3 5.9 %all-to-all-done.1.r_ref = bf16[64,16,128]{2,1,0:T(8,128)(2,1)} async-done(((bf16[64,16,128]{2,1,0:T(8,128)(2,1)}), bf16[64,16,128]{2,1,0:T(8,128)(2,1)}, u32[]{:S(2)}, u32[]{:S(2)}) %all-to-all-start.1) | async-done | bytes 262176 | tf_op jit(solution)/shard_map/all_to_all | solution.py:280
  75.2 1.1 %shard_map.112 = bf16[64,8,128]{2,1,0:T(8,128)(2,1)S(1)} custom-call(bf16[64,16,128]{2,1,0:T(8,128)(2,1)} %all-to-all-done.1.r_ref), custom_call_target="tpu_custom_call" | custom-call | flops 6553600 | bytes 262144 | tf_op jit(solution)/shard_map/pallas_call | solution.py:217
  76.3 0.6 copy-done.6
  76.9 6.8 %all-to-all-start.2 = ((bf16[64,8,128]{2,1,0:T(8,128)(2,1)}), bf16[64,8,128]{2,1,0:T(8,128)(2,1)S(1)}, u32[]{:S(2)}, u32[]{:S(2)}) async-start(bf16[64,8,128]{2,1,0:T(8,128)(2,1)} %copy-done.6), calls=%async_computation.2 | async-start | bytes 262144 | tf_op jit(solution)/shard_map/all_to_all | solution.py:290
  83.7 0.0 copy-start.13
  83.7 0.0 copy-start.22
  83.8 1.8 %shard_map.113.gate_ref = f32[128,1024]{1,0:T(8,128)S(1)} custom-call(s32[8]{0:T(128)S(1)} %pad_add_fusion.1.order, bf16[128,1024]{1,0:T(8,128)(2,1)S(1)} %bitcast.10, bf16[256,1024]{1,0:T(8,128)(2,1)S(1)} %pad_maximum_fusion.refs_0_, bf16[256,1024]{1,0:T(8,128)(2,1)S(1)} %collective-permute-done.2.refs_1_, ...), custom_call_target="tpu_custom_call" | custom-call | flops 268435456 | bytes 4456480 | tf_op jit(solution)/shard_map/pallas_call | solution.py:217
  85.6 0.8 copy-done
  86.4 0.6 shard_map.111.y_ref
  87.1 0.8 copy-done.2
  87.9 8.6 %all-to-all-done.2 = bf16[64,8,128]{2,1,0:T(8,128)(2,1)S(1)} async-done(((bf16[64,8,128]{2,1,0:T(8,128)(2,1)}), bf16[64,8,128]{2,1,0:T(8,128)(2,1)S(1)}, u32[]{:S(2)}, u32[]{:S(2)}) %all-to-all-start.2) | async-done | bytes 131104 | tf_op jit(solution)/shard_map/all_to_all | solution.py:290
  96.5 1.0 %copy-done.1 = f32[128,1024]{1,0:T(8,128)S(1)} copy-done((f32[128,1024]{1,0:T(8,128)S(1)}, f32[128,1024]{1,0:T(8,128)}, u32[]{:S(2)}) %copy-start.1) | copy-done | bytes 524312
  97.5 1.0 %copy-done.3 = f32[128,1024]{1,0:T(8,128)S(1)} copy-done((f32[128,1024]{1,0:T(8,128)S(1)}, f32[128,1024]{1,0:T(8,128)}, u32[]{:S(2)}) %copy-start.3) | copy-done | bytes 524312
  98.6 0.8 copy-done.9
  99.4 0.8 copy-done.16
  100.2 2.8 %shard_map.114 = bf16[128,1024]{1,0:T(8,128)(2,1)} custom-call(s32[8]{0:T(128)S(1)} %pad_add_fusion.1.order, f32[128,1024]{1,0:T(8,128)S(1)} %copy-done.3, bf16[512,128]{1,0:T(8,128)(2,1)S(1)} %bitcast.11, bf16[128,128]{1,0:T(8,128)(2,1)S(1)} %copy-done.16, f32[128,16]{1,0:T(8,128)S(1)} %copy-done.9, f32[128,1024]{1,0:T(8,128)S(1)} %copy-done.1, ...), custom_call_target="tpu_custom_call" | custom-call | flops 268435456 | bytes 5419040 | tf_op jit(solution)/shard_map/pallas_call | solution.py:217
  (44 shorter events, 0.1 us)
Async XLA Ops:
  0.0 0.9 copy-start.10
  1.0 0.8 copy-start.19
  1.7 0.7 copy-start.21
  3.6 11.7 %copy-start.26 = (bf16[128,1024]{1,0:T(8,128)(2,1)S(1)}, bf16[128,1024]{1,0:T(8,128)(2,1)}, u32[]{:S(2)}) copy-start(bf16[128,1024]{1,0:T(8,128)(2,1)} %param.21) | copy-start | bytes 786436
  3.6 11.7 %copy-start.27 = (bf16[128,1024]{1,0:T(8,128)(2,1)S(1)}, bf16[128,1024]{1,0:T(8,128)(2,1)}, u32[]{:S(2)}) copy-start(bf16[128,1024]{1,0:T(8,128)(2,1)} %param.13) | copy-start | bytes 786436
  3.6 33.2 %copy-start.20 = (f32[4,1024]{1,0:T(4,128)S(1)}, f32[4,1024]{1,0:T(4,128)}, u32[]{:S(2)}) copy-start(f32[4,1024]{1,0:T(4,128)} %conv_x.1) | copy-start | bytes 49156
  3.6 33.2 %copy-start.23 = (f32[4,128]{1,0:T(4,128)S(1)}, f32[4,128]{1,0:T(4,128)}, u32[]{:S(2)}) copy-start(f32[4,128]{1,0:T(4,128)} %conv_bc.1) | copy-start | bytes 6148
  3.6 33.2 %copy-start.24 = (f32[16]{0:T(128)S(1)}, f32[16]{0:T(128)}, u32[]{:S(2)}) copy-start(f32[16]{0:T(128)} %param.18) | copy-start | bytes 196
  3.6 33.2 %copy-start.25 = (f32[16]{0:T(128)S(1)}, f32[16]{0:T(128)}, u32[]{:S(2)}) copy-start(f32[16]{0:T(128)} %param.19) | copy-start | bytes 196
  3.6 21.4 %all-to-all-start = ((bf16[4,160,1024]{2,1,0:T(8,128)(2,1)}), bf16[4,160,1024]{2,1,0:T(8,128)(2,1)S(1)}, u32[]{:S(2)}, u32[]{:S(2)}) async-start(bf16[4,160,1024]{2,1,0:T(8,128)(2,1)} %shard_map.109), calls=%async_computation | async-start | bytes 2621440 | tf_op jit(solution)/shard_map/all_to_all | solution.py:250
  13.9 2.9 %collective-permute-start = (bf16[16,1024]{1,0:T(8,128)(2,1)S(1)}, bf16[16,1024]{1,0:T(8,128)(2,1)S(1)}, u32[]{:S(2)}, u32[]{:S(2)}) collective-permute-start(bf16[16,1024]{1,0:T(8,128)(2,1)S(1)} %slice_bitcast_fusion), channel_id=1, source_target_pairs={{0,8},{8,16},{16,24},{24,32},{32,40},{40,48},{48,56},{56,64},{64,7... | collective-permute-start | bytes 98312 | tf_op jit(solution)/shard_map/ppermute | solution.py:251
  25.0 11.8 %collective-permute-start.1 = (bf16[4,160,1024]{2,1,0:T(8,128)(2,1)S(1)}, bf16[4,160,1024]{2,1,0:T(8,128)(2,1)S(1)}, u32[]{:S(2)}, u32[]{:S(2)}) collective-permute-start(bf16[4,160,1024]{2,1,0:T(8,128)(2,1)S(1)} %all-to-all-done.wa), channel_id=1, source_target_pairs={{0,1},{1,0},{2,3},{3,2},{4,5},{5,4},{6,7},{7,6},{8,9},{9,8},{10,11... | collective-permute-start | bytes 3932168 | tf_op jit(solution)/shard_map/ppermute | solution.py:229
  27.0 35.6 %collective-permute-start.2 = (bf16[256,1024]{1,0:T(8,128)(2,1)S(1)}, bf16[256,1024]{1,0:T(8,128)(2,1)S(1)}, u32[]{:S(2)}, u32[]{:S(2)}) collective-permute-start(bf16[256,1024]{1,0:T(8,128)(2,1)S(1)} %pad_maximum_fusion.refs_0_), channel_id=1, source_target_pairs={{0,2},{2,4},{4,6},{6,0},{1,3},{3,5},{5,7},{7,1},{8,10},{10,12},{12... | collective-permute-start | bytes 1572872 | tf_op jit(solution)/shard_map/ppermute | solution.py:262
  28.9 36.1 %collective-permute-start.3 = (bf16[256,1024]{1,0:T(8,128)(2,1)S(1)}, bf16[256,1024]{1,0:T(8,128)(2,1)S(1)}, u32[]{:S(2)}, u32[]{:S(2)}) collective-permute-start(bf16[256,1024]{1,0:T(8,128)(2,1)S(1)} %pad_maximum_fusion.refs_0_), channel_id=1, source_target_pairs={{0,4},{2,6},{4,0},{6,2},{1,5},{3,7},{5,1},{7,3},{8,12},{10,14},{12... | collective-permute-start | bytes 1572872 | tf_op jit(solution)/shard_map/ppermute | solution.py:262
  34.3 32.6 %collective-permute-start.4 = (bf16[256,1024]{1,0:T(8,128)(2,1)S(1)}, bf16[256,1024]{1,0:T(8,128)(2,1)S(1)}, u32[]{:S(2)}, u32[]{:S(2)}) collective-permute-start(bf16[256,1024]{1,0:T(8,128)(2,1)S(1)} %pad_maximum_fusion.refs_0_), channel_id=1, source_target_pairs={{0,6},{2,0},{4,2},{6,4},{1,7},{3,1},{5,3},{7,5},{8,14},{10,8},{12,... | collective-permute-start | bytes 1572872 | tf_op jit(solution)/shard_map/ppermute | solution.py:262
  36.9 1.0 copy-start.4
  40.4 0.6 copy-start.7
  41.0 0.7 copy-start.11
  41.7 0.7 copy-start.12
  42.4 0.6 copy-start.14
  43.0 0.6 copy-start.17
  43.6 40.2 %copy-start.5 = (bf16[128,1,1024]{2,0,1:T(8,128)(2,1)S(1)}, bf16[128,1,1024]{2,0,1:T(8,128)(2,1)}, u32[]{:S(2)}) copy-start(bf16[128,1,1024]{2,0,1:T(8,128)(2,1)} %param.11) | copy-start | bytes 786436
  43.6 31.6 %all-to-all-start.1 = ((bf16[64,16,128]{2,1,0:T(8,128)(2,1)}), bf16[64,16,128]{2,1,0:T(8,128)(2,1)}, u32[]{:S(2)}, u32[]{:S(2)}) async-start(bf16[64,16,128]{2,1,0:T(8,128)(2,1)} %copy-done.11), calls=%async_computation.1 | async-start | bytes 524288 | tf_op jit(solution)/shard_map/all_to_all | solution.py:280
  60.6 23.2 %collective-permute-start.5 = (bf16[256,1024]{1,0:T(8,128)(2,1)S(1)}, bf16[256,1024]{1,0:T(8,128)(2,1)S(1)}, u32[]{:S(2)}, u32[]{:S(2)}) collective-permute-start(bf16[256,1024]{1,0:T(8,128)(2,1)S(1)} %pad_maximum_fusion.refs_0_), channel_id=1, source_target_pairs={{0,1},{1,0},{2,3},{3,2},{4,5},{5,4},{6,7},{7,6},{8,9},{9,8},{10,11... | collective-permute-start | bytes 1572872 | tf_op jit(solution)/shard_map/ppermute | solution.py:229
  62.5 21.2 %collective-permute-start.6 = (bf16[256,1024]{1,0:T(8,128)(2,1)S(1)}, bf16[256,1024]{1,0:T(8,128)(2,1)S(1)}, u32[]{:S(2)}, u32[]{:S(2)}) collective-permute-start(bf16[256,1024]{1,0:T(8,128)(2,1)S(1)} %collective-permute-done.2.refs_1_), channel_id=1, source_target_pairs={{0,1},{1,0},{2,3},{3,2},{4,5},{5,4},{6,7},{7,6},{8,9},{9,8},{10,11... | collective-permute-start | bytes 1572872 | tf_op jit(solution)/shard_map/ppermute | solution.py:229
  65.0 18.8 %collective-permute-start.7 = (bf16[256,1024]{1,0:T(8,128)(2,1)S(1)}, bf16[256,1024]{1,0:T(8,128)(2,1)}, u32[]{:S(2)}, u32[]{:S(2)}) collective-permute-start(bf16[256,1024]{1,0:T(8,128)(2,1)S(1)} %collective-permute-done.3.refs_2_), channel_id=1, source_target_pairs={{0,1},{1,0},{2,3},{3,2},{4,5},{5,4},{6,7},{7,6},{8,9},{9,8},{10,11... | collective-permute-start | bytes 1572872 | tf_op jit(solution)/shard_map/ppermute | solution.py:229
  66.9 16.9 %collective-permute-start.8 = (bf16[256,1024]{1,0:T(8,128)(2,1)S(1)}, bf16[256,1024]{1,0:T(8,128)(2,1)}, u32[]{:S(2)}, u32[]{:S(2)}) collective-permute-start(bf16[256,1024]{1,0:T(8,128)(2,1)S(1)} %collective-permute-done.4.refs_3_), channel_id=1, source_target_pairs={{0,1},{1,0},{2,3},{3,2},{4,5},{5,4},{6,7},{7,6},{8,9},{9,8},{10,11... | collective-permute-start | bytes 1572872 | tf_op jit(solution)/shard_map/ppermute | solution.py:229
  76.3 0.6 copy-start.6
  76.9 19.6 %all-to-all-start.2 = ((bf16[64,8,128]{2,1,0:T(8,128)(2,1)}), bf16[64,8,128]{2,1,0:T(8,128)(2,1)S(1)}, u32[]{:S(2)}, u32[]{:S(2)}) async-start(bf16[64,8,128]{2,1,0:T(8,128)(2,1)} %copy-done.6), calls=%async_computation.2 | async-start | bytes 262144 | tf_op jit(solution)/shard_map/all_to_all | solution.py:290
  83.7 2.7 %copy-start.8 = (f32[128,16]{1,0:T(8,128)S(1)}, f32[128,16]{1,0:T(8,128)}, u32[]{:S(2)}) copy-start(f32[128,16]{1,0:T(8,128)} %copy-done.7) | copy-start | bytes 24580
  83.7 2.7 %copy-start.13 = (bf16[128,1024]{1,0:T(8,128)(2,1)S(1)}, bf16[128,1024]{1,0:T(8,128)(2,1)}, u32[]{:S(2)}) copy-start(bf16[128,1024]{1,0:T(8,128)(2,1)} %copy-done.12) | copy-start | bytes 786436
  83.7 2.7 %copy-start.15 = (bf16[128,128]{1,0:T(8,128)(2,1)S(1)}, bf16[128,128]{1,0:T(8,128)(2,1)}, u32[]{:S(2)}) copy-start(bf16[128,128]{1,0:T(8,128)(2,1)} %copy-done.14) | copy-start | bytes 98308
  83.7 2.7 %copy-start.18 = (f32[128,16]{1,0:T(8,128)S(1)}, f32[128,16]{1,0:T(8,128)}, u32[]{:S(2)}) copy-start(f32[128,16]{1,0:T(8,128)} %copy-done.17) | copy-start | bytes 24580
  83.7 12.7 %copy-start.22 = (f32[1024]{0:T(1024)S(1)}, f32[1024]{0:T(1024)}, u32[]{:S(2)}) copy-start(f32[1024]{0:T(1024)} %param.20) | copy-start | bytes 12292
  85.6 0.8 copy-start
  87.1 0.8 copy-start.2
  96.5 1.0 %copy-start.1 = (f32[128,1024]{1,0:T(8,128)S(1)}, f32[128,1024]{1,0:T(8,128)}, u32[]{:S(2)}) copy-start(f32[128,1024]{1,0:T(8,128)} %copy-done) | copy-start | bytes 1572868
  97.5 1.0 %copy-start.3 = (f32[128,1024]{1,0:T(8,128)S(1)}, f32[128,1024]{1,0:T(8,128)}, u32[]{:S(2)}) copy-start(f32[128,1024]{1,0:T(8,128)} %copy-done.2) | copy-start | bytes 1572868
  98.6 0.8 copy-start.9
  99.4 0.8 copy-start.16
where the time goes:
time: 104 us; the launch traced here: 103 us
  starting transfers between devices  55 us (53%)
  waiting for transfers between devices  24.1 us (23%)
  local copies, waits for them, and re-layouts  13.3 us (13%)
  Pallas kernels  10.1 us (10%)
    all_to_all x1, starting transfers between devices, local(): got = lax.all_to_all(msg, LAT, 0, 0)  17 us
    unnamed x56, local copies, waits for them, and re-layouts  12.6 us
    ppermute x5, starting transfers between devices, other_core(): return lax.ppermute(block, 'c', [(0, 1), (1, 0)])  10.6 us
    pallas_call x6, Pallas kernels, call(): pl.pallas_call(body, out_shape=outs, in_specs=specs, out_specs=jax.tree.m...  10.1 us
    ppermute x3, starting transfers between devices, local(): lax.ppermute(second, 'x', [(i, (i + d) % n_x) for i in range(n_x)])  9.82 us
    all_to_all x1, starting transfers between devices, local(): w1a = lax.all_to_all(first, 'x', 0, 0)  9.53 us
    all_to_all x1, waiting for transfers between devices, local(): incoming = lax.all_to_all(entering, LAT, 0, 0)  8.62 us
    all_to_all x1, waiting for transfers between devices, local(): w1a = lax.all_to_all(first, 'x', 0, 0)  8.26 us
  transfers between devices with their start and end apart: 12, of which 4 were waited for; matrix products, arithmetic and copies ran while one was open for 1% of the time, Pallas kernels for 6%

commit v1 on v0

--- a/solution.py
+++ b/solution.py
@@ -63,20 +63,39 @@
     return jnp.concatenate([r[rows, columns] for r in refs], 0)
 
 
-def pack_kernel(x_ref, bc_ref, dt_ref, out):
-    k = x_ref.shape[0]
-    blocks = x_ref.shape[1] // LANES
+def fetch(pairs, sems):
+    copies = [pltpu.make_async_copy(a, b, sems.at[i]) for i, (a, b) in enumerate(pairs)]
+    for c in copies:
+        c.start()
+    return copies
+
+
+def pack_kernel(x_ref, bc_ref, dt_ref, out, x, bc, dt, sems):
+    copies = fetch([(x_ref, x), (bc_ref, bc), (dt_ref, dt)], sems)
+    k, width = x.shape
+    blocks = width // LANES
     part = k // blocks
-    bc = jnp.concatenate([bc_ref[j * part : (j + 1) * part, :] for j in range(blocks)], 1)
+    for c in copies:
+        c.wait()
+    rest = jnp.zeros((part, width - LANES), BF16)
     for i in range(out.shape[0]):
-        out[i, :k, :] = x_ref[...]
-        out[i, k : k + part, :] = bc
-        out[i, k + part :, :LANES] = dt_ref[...]
-        out[i, k + part :, LANES:] = jnp.zeros((part, x_ref.shape[1] - LANES), BF16)
+        out[i, :k, :] = x[...]
+        for j in range(blocks):
+            out[i, k : k + part, j * LANES : (j + 1) * LANES] = bc[j * part : (j + 1) * part, :]
+        out[i, k + part :, :LANES] = dt[...]
+        out[i, k + part :, LANES:] = rest
+
+
+def source_kernel(order, f_ref, halo_ref, out):
+    n = out.shape[1] // LANES
+    for j in range(n):
+        at = slice(j * LANES, (j + 1) * LANES)
+        out[:HALO, at] = chunk(halo_ref, order[j])
+        out[HALO:, at] = chunk(f_ref, order[j])
 
 
 def project_kernel(
-    order, f_ref, halo_ref, wa, wb, conv_x, conv_bc, bias, rate,
+    src_ref, wa, wb, conv_x, conv_bc, bias, rate,
     x_out, bc_out, dt_out, cum_out, msg_out, pre,
 ):
     rows, width = x_out.shape
@@ -87,7 +106,7 @@
     blocks = width // LANES
     part = k // blocks
     shards = [r.at[i] for r in (wa, wb) for i in range(n // 2)]
-    src = jnp.concatenate([ordered(halo_ref, order, n), ordered(f_ref, order, n)], 0)
+    src = src_ref[...]
     first = HALO - conv_x.shape[0] + 1
 
     def conv(at, wide, taps):
@@ -177,15 +196,20 @@
 
 
 def gate_kernel(order, f_ref, *refs):
-    shards, out = refs[:-1], refs[-1]
+    shards, (out, w, sems) = refs[:-3], refs[-3:]
+    k = w.shape[0] // len(shards)
+    copies = fetch([(r.at[:k], w.at[pl.ds(i * k, k)]) for i, r in enumerate(shards)], sems)
     src = ordered(f_ref, order, len(shards))
+    for c in copies:
+        c.wait()
     for at in range(0, out.shape[1], TILE):
-        w = stacked(shards, slice(0, LANES), slice(at, at + TILE))
-        out[:, at : at + TILE] = silu(dot(src, w).astype(BF16).astype(F32))
+        out[:, at : at + TILE] = dot(src, w[:, at : at + TILE]).astype(BF16)
 
 
 def finish_kernel(order, y_ref, in_ref, bc_ref, cum_ref, gate_ref, gain, *refs):
-    shards, (out, hidden) = refs[:-2], refs[-2:]
+    shards, (out, hidden, w, sems) = refs[:-4], refs[-4:]
+    k = w.shape[0] // len(shards)
+    copies = fetch([(r.at[k:], w.at[pl.ds(i * k, k)]) for i, r in enumerate(shards)], sems)
     rows, width = y_ref.shape
     half = width // 2
     bc = bc_ref[...].astype(F32)
@@ -198,29 +222,39 @@
     for at in range(0, width, TILE):
         inner = in_ref[at % half : at % half + TILE, :]
         y = y_ref[:, at : at + TILE] + dot_nt(c[at // half], inner) * grown[:, at : at + TILE]
-        g = y * gate_ref[:, at : at + TILE]
+        g = y * silu(gate_ref[:, at : at + TILE].astype(F32))
         square = square + jnp.sum(g * g, -1, keepdims=True)
         parts.append(g)
     scale = lax.rsqrt(square / width + EPS)
     for i, at in enumerate(range(0, width, TILE)):
         hidden[:, at : at + TILE] = (parts[i] * scale * gain[:, at : at + TILE]).astype(BF16)
     src = ordered(hidden, order, len(shards))
+    for c in copies:
+        c.wait()
     for at in range(0, out.shape[1], TILE):
-        w = stacked(shards, slice(LANES, 2 * LANES), slice(at, at + TILE))
-        out[:, at : at + TILE] = dot(src, w).astype(BF16)
-
-
-def call(body, outs, args, smem=0, scratch=(), flops=0):
+        out[:, at : at + TILE] = dot(src, w[:, at : at + TILE]).astype(BF16)
+
+
+def call(body, outs, args, smem=0, hbm=0, scratch=(), flops=0):
     vmem = pl.BlockSpec(memory_space=pltpu.VMEM)
-    specs = [pl.BlockSpec(memory_space=pltpu.SMEM)] * smem + [vmem] * (len(args) - smem)
+    specs = (
+        [pl.BlockSpec(memory_space=pltpu.SMEM)] * smem
+        + [vmem] * (len(args) - smem - hbm)
+        + [pl.BlockSpec(memory_space=pltpu.MemorySpace.HBM)] * hbm
+    )
+    args = [
+        pltpu.with_memory_space_constraint(a, pltpu.MemorySpace.HBM) if i >= len(args) - hbm else a
+        for i, a in enumerate(args)
+    ]
+    scratch = list(scratch) + ([pltpu.SemaphoreType.DMA((hbm,))] if hbm else [])
     nbytes = sum(a.size * a.dtype.itemsize for a in args)
     return pl.pallas_call(
         body,
         out_shape=outs,
         in_specs=specs,
         out_specs=jax.tree.map(lambda _: vmem, outs),
-        scratch_shapes=list(scratch),
-        compiler_params=pltpu.CompilerParams(vmem_limit_bytes=24 * 2**20),
+        scratch_shapes=scratch,
+        compiler_params=pltpu.CompilerParams(vmem_limit_bytes=16 * 2**20),
         cost_estimate=pl.CostEstimate(flops=flops, bytes_accessed=nbytes, transcendentals=0),
     )(*args)
 
@@ -246,6 +280,12 @@
         pack_kernel,
         sds((n_x, k + 2 * k * LANES // width, width), BF16),
         [proj_x, proj_bc, proj_dt.T],
+        hbm=3,
+        scratch=[
+            pltpu.VMEM(proj_x.shape, BF16),
+            pltpu.VMEM(proj_bc.shape, BF16),
+            pltpu.VMEM(proj_dt.shape[::-1], BF16),
+        ],
     )
     w1a = lax.all_to_all(first, "x", 0, 0)
     halo = lax.ppermute(f[rows - HALO :], LAT, [(i, i + 1) for i in range(bands - 1)])
@@ -255,11 +295,14 @@
     x_near = (x_at - x_all + n_x) % n_x
     order2 = jnp.concatenate([x_near * 2 + c_at, x_near * 2 + 1 - c_at]).astype(jnp.int32)
     second = jnp.concatenate([proj_z, proj_out], 0)
-    w1a, halo, second, order, order2 = lax.optimization_barrier((w1a, halo, second, order, order2))
-    w1b = other_core(w1a)
+    src = call(
+        source_kernel, sds((HALO + rows, depth), BF16), [order, f, halo], smem=1, flops=10**6
+    )
     w2a, w2b = [second], []
     for d in range(1, n_x):
         w2a.append(lax.ppermute(second, "x", [(i, (i + d) % n_x) for i in range(n_x)]))
+    w1a, src, order2 = lax.optimization_barrier((w1a, src, order2))
+    w1b = other_core(w1a)
     for d in range(n_x):
         w2b.append(other_core(w2a[d]))
 
@@ -272,8 +315,7 @@
             sds((rows, heads), F32),
             sds((bands, 2 * SUB, LANES), BF16),
         ),
-        [order, f, halo, w1a, w1b, conv_x, conv_bc, dt_bias[None], log_rate[None]],
-        smem=1,
+        [src, w1a, w1b, conv_x, conv_bc, dt_bias[None], log_rate[None]],
         scratch=[pltpu.VMEM((HALO + rows, width + 2 * state), F32)],
         flops=2 * rows * depth * (width + 2 * LANES),
     )
@@ -291,9 +333,11 @@
     incoming = incoming.reshape(bands * SUB, LANES)
     gate = call(
         gate_kernel,
-        sds((rows, width), F32),
+        sds((rows, width), BF16),
         [order2, f, *w2a, *w2b],
         smem=1,
+        hbm=2 * n_x,
+        scratch=[pltpu.VMEM((depth, width), BF16)],
         flops=2 * rows * depth * width,
     )
     out = call(
@@ -301,7 +345,8 @@
         sds((rows, depth), BF16),
         [order2, y, incoming, bc_act, cum, gate, norm_gain[None], *w2a, *w2b],
         smem=1,
-        scratch=[pltpu.VMEM((rows, width), BF16)],
+        hbm=2 * n_x,
+        scratch=[pltpu.VMEM((rows, width), BF16), pltpu.VMEM((width, depth), BF16)],
         flops=2 * rows * depth * width,
     )
     return out.reshape(rows, 1, depth)

time: 104 us -> 95.9 us (0.922)
  the two profiles are of different devices: /device:TPU:2 before, /device:TPU:1 now
where the time goes in v1:
time: 95.9 us; the launch traced here: 95.2 us
  starting transfers between devices  61.5 us (64%)
  waiting for transfers between devices  19.4 us (20%)
  Pallas kernels  12.9 us (13%)
    ppermute x5, starting transfers between devices, other_core(): return lax.ppermute(block, 'c', [(0, 1), (1, 0)])  17.6 us
    all_to_all x1, starting transfers between devices, local(): got = lax.all_to_all(msg, LAT, 0, 0)  16.3 us
    pallas_call x7, Pallas kernels, call(): pl.pallas_call(body, out_shape=outs, in_specs=specs, out_specs=jax.tree.m...  12.9 us
    all_to_all x1, starting transfers between devices, local(): incoming = lax.all_to_all(entering, LAT, 0, 0)  10.9 us
    ppermute x3, starting transfers between devices, local(): lax.ppermute(second, 'x', [(i, (i + d) % n_x) for i in range(n_x)])  8.42 us
    all_to_all x1, waiting for transfers between devices, local(): incoming = lax.all_to_all(entering, LAT, 0, 0)  7.61 us
    all_to_all x1, waiting for transfers between devices, local(): w1a = lax.all_to_all(first, 'x', 0, 0)  7.17 us
    all_to_all x1, starting transfers between devices, local(): w1a = lax.all_to_all(first, 'x', 0, 0)  4.97 us
  transfers between devices with their start and end apart: 12, of which 4 were waited for; matrix products, arithmetic and copies ran while one was open for 0% of the time, Pallas kernels for 8%

profile of v1, /device:TPU:1, one launch (start us, length us, event | category | flops | bytes accessed | tf_op | source)
XLA Modules:
  0.0 95.2 jit_solution(16204591195287641346)
XLA Ops:
  0.0 2.2 %shard_map.109 = bf16[4,160,1024]{2,1,0:T(8,128)(2,1)} custom-call(bf16[128,1024]{1,0:T(8,128)(2,1)} %x_ref.1, bf16[128,128]{1,0:T(8,128)(2,1)} %bc_ref.1, bf16[16,128]{1,0:T(8,128)(2,1)} %bitcast.15), custom_call_target="tpu_custom_call" | custom-call | bytes 299008 | tf_op jit(solution)/shard_map/pallas_call | solution.py:251
  2.2 0.0 copy-start
  2.2 0.0 copy-start.9
  2.2 0.0 copy-start.10
  2.2 5.0 %all-to-all-start = ((bf16[4,160,1024]{2,1,0:T(8,128)(2,1)}), bf16[4,160,1024]{2,1,0:T(8,128)(2,1)S(1)}, u32[]{:S(2)}, u32[]{:S(2)}) async-start(bf16[4,160,1024]{2,1,0:T(8,128)(2,1)} %shard_map.109), calls=%async_computation | async-start | bytes 2621440 | tf_op jit(solution)/shard_map/all_to_all | solution.py:290
  7.2 0.0 copy-done
  7.2 0.0 copy-start.4
  7.2 0.0 copy-start.5
  7.2 3.3 %collective-permute-start = (bf16[16,1024]{1,0:T(8,128)(2,1)S(1)}, bf16[16,1024]{1,0:T(8,128)(2,1)S(1)}, u32[]{:S(2)}, u32[]{:S(2)}) collective-permute-start(bf16[16,1024]{1,0:T(8,128)(2,1)S(1)} %slice_bitcast_fusion), channel_id=1, source_target_pairs={{0,8},{8,16},{16,24},{24,32},{32,40},{40,48},{48,56},{56,64},{64,7... | collective-permute-start | bytes 98312 | tf_op jit(solution)/shard_map/ppermute | solution.py:291
  10.6 0.1 pad_add_fusion.order
  10.7 0.1 pad_add_fusion.1.order
  10.7 0.8 collective-permute-done.halo_ref
  11.6 0.6 shard_map.110.src_ref
  12.2 7.2 %all-to-all-done.wa = bf16[4,160,1024]{2,1,0:T(8,128)(2,1)S(1)} async-done(((bf16[4,160,1024]{2,1,0:T(8,128)(2,1)}), bf16[4,160,1024]{2,1,0:T(8,128)(2,1)S(1)}, u32[]{:S(2)}, u32[]{:S(2)}) %all-to-all-start) | async-done | bytes 1310752 | tf_op jit(solution)/shard_map/all_to_all | solution.py:290
  19.4 8.6 %collective-permute-start.1 = (bf16[4,160,1024]{2,1,0:T(8,128)(2,1)S(1)}, bf16[4,160,1024]{2,1,0:T(8,128)(2,1)S(1)}, u32[]{:S(2)}, u32[]{:S(2)}) collective-permute-start(bf16[4,160,1024]{2,1,0:T(8,128)(2,1)S(1)} %all-to-all-done.wa), channel_id=1, source_target_pairs={{0,1},{1,0},{2,3},{3,2},{4,5},{5,4},{6,7},{7,6},{8,9},{9,8},{10,11... | collective-permute-start | bytes 3932168 | tf_op jit(solution)/shard_map/ppermute | solution.py:263
  27.9 0.0 copy-done.9
  28.0 0.0 copy-done.10
  28.0 0.0 copy-start.6
  28.0 2.2 %collective-permute-start.2 = (bf16[256,1024]{1,0:T(8,128)(2,1)S(1)}, bf16[256,1024]{1,0:T(8,128)(2,1)S(1)}, u32[]{:S(2)}, u32[]{:S(2)}) collective-permute-start(bf16[256,1024]{1,0:T(8,128)(2,1)S(1)} %constant_dynamic-update-slice_fusion.refs_0_), channel_id=1, source_target_pairs={{0,2},{2,4},{4,6},{6,0},{1,3},{3,5},{5,7},{7,1},{8,10},{10,12},{12... | collective-permute-start | bytes 1572872 | tf_op jit(solution)/shard_map/ppermute | solution.py:303
  30.2 3.7 %collective-permute-start.3 = (bf16[256,1024]{1,0:T(8,128)(2,1)S(1)}, bf16[256,1024]{1,0:T(8,128)(2,1)}, u32[]{:S(2)}, u32[]{:S(2)}) collective-permute-start(bf16[256,1024]{1,0:T(8,128)(2,1)S(1)} %constant_dynamic-update-slice_fusion.refs_0_), channel_id=1, source_target_pairs={{0,4},{2,6},{4,0},{6,2},{1,5},{3,7},{5,1},{7,3},{8,12},{10,14},{12... | collective-permute-start | bytes 1572872 | tf_op jit(solution)/shard_map/ppermute | solution.py:303
  33.9 2.5 %collective-permute-start.4 = (bf16[256,1024]{1,0:T(8,128)(2,1)S(1)}, bf16[256,1024]{1,0:T(8,128)(2,1)}, u32[]{:S(2)}, u32[]{:S(2)}) collective-permute-start(bf16[256,1024]{1,0:T(8,128)(2,1)S(1)} %constant_dynamic-update-slice_fusion.refs_0_), channel_id=1, source_target_pairs={{0,6},{2,0},{4,2},{6,4},{1,7},{3,1},{5,3},{7,5},{8,14},{10,8},{12,... | collective-permute-start | bytes 1572872 | tf_op jit(solution)/shard_map/ppermute | solution.py:303
  36.5 0.0 collective-permute-done.1.wb
  36.5 0.0 copy-done.1
  36.5 0.0 copy-done.3
  36.5 0.0 copy-done.4
  36.5 2.7 %shard_map.111 = (bf16[128,1024]{1,0:T(8,128)(2,1)S(1)}, bf16[128,128]{1,0:T(8,128)(2,1)S(1)}, f32[128,16]{1,0:T(8,128)S(1)}, f32[128,16]{1,0:T(8,128)S(1)}, bf16[64,16,128]{2,1,0:T(8,128)(2,1)}) custom-call(bf16[144,1024]{1,0:T(8,128)(2,1)S(1)} %shard_map.110.src_ref, bf16[4,160,1024]{2,1,0:T(8,128)(2,1)S(1)} %all-to-all-done.wa, ...), custom_call_target="tpu_custom_call" | custom-call | flops 335544320 | bytes 2934912 | tf_op jit(solution)/shard_map/pallas_call | solution.py:251
  39.2 16.3 %all-to-all-start.1 = ((bf16[64,16,128]{2,1,0:T(8,128)(2,1)}), bf16[64,16,128]{2,1,0:T(8,128)(2,1)S(1)}, u32[]{:S(2)}, u32[]{:S(2)}) async-start(bf16[64,16,128]{2,1,0:T(8,128)(2,1)} %get-tuple-element.20), calls=%async_computation.1 | async-start | bytes 524288 | tf_op jit(solution)/shard_map/all_to_all | solution.py:322
  55.5 2.8 %collective-permute-start.5 = (bf16[256,1024]{1,0:T(8,128)(2,1)S(1)}, bf16[256,1024]{1,0:T(8,128)(2,1)S(1)}, u32[]{:S(2)}, u32[]{:S(2)}) collective-permute-start(bf16[256,1024]{1,0:T(8,128)(2,1)S(1)} %constant_dynamic-update-slice_fusion.refs_0_), channel_id=1, source_target_pairs={{0,1},{1,0},{2,3},{3,2},{4,5},{5,4},{6,7},{7,6},{8,9},{9,8},{10,11... | collective-permute-start | bytes 1572872 | tf_op jit(solution)/shard_map/ppermute | solution.py:263
  58.3 0.0 collective-permute-done.2.refs_1_
  58.3 0.0 copy-start.7
  58.3 1.9 %collective-permute-start.6 = (bf16[256,1024]{1,0:T(8,128)(2,1)S(1)}, bf16[256,1024]{1,0:T(8,128)(2,1)}, u32[]{:S(2)}, u32[]{:S(2)}) collective-permute-start(bf16[256,1024]{1,0:T(8,128)(2,1)S(1)} %collective-permute-done.2.refs_1_), channel_id=1, source_target_pairs={{0,1},{1,0},{2,3},{3,2},{4,5},{5,4},{6,7},{7,6},{8,9},{9,8},{10,11... | collective-permute-start | bytes 1572872 | tf_op jit(solution)/shard_map/ppermute | solution.py:263
  60.3 0.0 collective-permute-done.3.refs_2_
  60.3 2.4 %collective-permute-start.7 = (bf16[256,1024]{1,0:T(8,128)(2,1)}, bf16[256,1024]{1,0:T(8,128)(2,1)}, u32[]{:S(2)}, u32[]{:S(2)}) collective-permute-start(bf16[256,1024]{1,0:T(8,128)(2,1)} %collective-permute-done.3.refs_2_), channel_id=1, source_target_pairs={{0,1},{1,0},{2,3},{3,2},{4,5},{5,4},{6,7},{7,6},{8,9},{9,8},{10,11... | collective-permute-start | bytes 1572872 | tf_op jit(solution)/shard_map/ppermute | solution.py:263
  62.7 0.0 collective-permute-done.4.refs_3_
  62.7 1.9 %collective-permute-start.8 = (bf16[256,1024]{1,0:T(8,128)(2,1)}, bf16[256,1024]{1,0:T(8,128)(2,1)}, u32[]{:S(2)}, u32[]{:S(2)}) collective-permute-start(bf16[256,1024]{1,0:T(8,128)(2,1)} %collective-permute-done.4.refs_3_), channel_id=1, source_target_pairs={{0,1},{1,0},{2,3},{3,2},{4,5},{5,4},{6,7},{7,6},{8,9},{9,8},{10,11... | collective-permute-start | bytes 1572872 | tf_op jit(solution)/shard_map/ppermute | solution.py:263
  64.6 3.8 %all-to-all-done.1.r_ref = bf16[64,16,128]{2,1,0:T(8,128)(2,1)S(1)} async-done(((bf16[64,16,128]{2,1,0:T(8,128)(2,1)}), bf16[64,16,128]{2,1,0:T(8,128)(2,1)S(1)}, u32[]{:S(2)}, u32[]{:S(2)}) %all-to-all-start.1) | async-done | bytes 262176 | tf_op jit(solution)/shard_map/all_to_all | solution.py:322
  68.4 0.8 shard_map.113
  69.2 10.9 %all-to-all-start.2 = ((bf16[64,8,128]{2,1,0:T(8,128)(2,1)}), bf16[64,8,128]{2,1,0:T(8,128)(2,1)S(1)}, u32[]{:S(2)}, u32[]{:S(2)}) async-start(bf16[64,8,128]{2,1,0:T(8,128)(2,1)} %shard_map.113), calls=%async_computation.2 | async-start | bytes 262144 | tf_op jit(solution)/shard_map/all_to_all | solution.py:332
  80.1 0.0 copy-start.2
  80.1 0.0 collective-permute-done.5.refs_4_
  80.1 0.0 collective-permute-done.6.refs_5_
  80.1 0.0 collective-permute-done.7.refs_6_
  80.2 0.8 copy-done.8
  80.9 0.0 collective-permute-done.8.refs_7_
  80.9 2.6 %shard_map.114.gate_ref = bf16[128,1024]{1,0:T(8,128)(2,1)S(1)} custom-call(s32[8]{0:T(128)S(1)} %pad_add_fusion.1.order, bf16[128,1024]{1,0:T(8,128)(2,1)S(1)} %bitcast.10, bf16[256,1024]{1,0:T(8,128)(2,1)} %copy-done.6, bf16[256,1024]{1,0:T(8,128)(2,1)} %copy-done.7, bf16[256,1024]{1,0:T(8,128)(2,1)} %collective-permute-done.3.refs_2_, ...), custom_call_target="tpu_custom_call" | custom-call | flops 268435456 | bytes 4456480 | tf_op jit(solution)/shard_map/pallas_call | solution.py:251
  83.5 0.6 shard_map.112.y_ref
  84.1 7.6 %all-to-all-done.2 = bf16[64,8,128]{2,1,0:T(8,128)(2,1)S(1)} async-done(((bf16[64,8,128]{2,1,0:T(8,128)(2,1)}), bf16[64,8,128]{2,1,0:T(8,128)(2,1)S(1)}, u32[]{:S(2)}, u32[]{:S(2)}) %all-to-all-start.2) | async-done | bytes 131104 | tf_op jit(solution)/shard_map/all_to_all | solution.py:332
  91.8 3.5 %shard_map.115 = bf16[128,1024]{1,0:T(8,128)(2,1)} custom-call(s32[8]{0:T(128)S(1)} %pad_add_fusion.1.order, f32[128,1024]{1,0:T(8,128)S(1)} %shard_map.112.y_ref, bf16[512,128]{1,0:T(8,128)(2,1)S(1)} %bitcast.11, bf16[128,128]{1,0:T(8,128)(2,1)S(1)} %get-tuple-element.17.bc_ref, f32[128,16]{1,0:T(8,128)S(1)} %get-tuple-element.19.cum_ref, ...), custom_call_target="tpu_custom_call" | custom-call | flops 268435456 | bytes 5156896 | tf_op jit(solution)/shard_map/pallas_call | solution.py:251
  (12 shorter events, 0.1 us)
Async XLA Ops:
  2.2 5.0 %copy-start = (bf16[128,1,1024]{2,0,1:T(8,128)(2,1)S(1)}, bf16[128,1,1024]{2,0,1:T(8,128)(2,1)}, u32[]{:S(2)}) copy-start(bf16[128,1,1024]{2,0,1:T(8,128)(2,1)} %param.11) | copy-start | bytes 786436
  2.2 25.8 %copy-start.9 = (bf16[128,1024]{1,0:T(8,128)(2,1)S(1)}, bf16[128,1024]{1,0:T(8,128)(2,1)}, u32[]{:S(2)}) copy-start(bf16[128,1024]{1,0:T(8,128)(2,1)} %param.13) | copy-start | bytes 786436
  2.2 25.8 %copy-start.10 = (bf16[128,1024]{1,0:T(8,128)(2,1)S(1)}, bf16[128,1024]{1,0:T(8,128)(2,1)}, u32[]{:S(2)}) copy-start(bf16[128,1024]{1,0:T(8,128)(2,1)} %param.21) | copy-start | bytes 786436
  2.2 17.2 %all-to-all-start = ((bf16[4,160,1024]{2,1,0:T(8,128)(2,1)}), bf16[4,160,1024]{2,1,0:T(8,128)(2,1)S(1)}, u32[]{:S(2)}, u32[]{:S(2)}) async-start(bf16[4,160,1024]{2,1,0:T(8,128)(2,1)} %shard_map.109), calls=%async_computation | async-start | bytes 2621440 | tf_op jit(solution)/shard_map/all_to_all | solution.py:290
  7.2 29.3 %copy-start.1 = (f32[4,1024]{1,0:T(4,128)S(1)}, f32[4,1024]{1,0:T(4,128)}, u32[]{:S(2)}) copy-start(f32[4,1024]{1,0:T(4,128)} %conv_x.1) | copy-start | bytes 49156
  7.2 29.3 %copy-start.3 = (f32[4,128]{1,0:T(4,128)S(1)}, f32[4,128]{1,0:T(4,128)}, u32[]{:S(2)}) copy-start(f32[4,128]{1,0:T(4,128)} %conv_bc.1) | copy-start | bytes 6148
  7.2 29.3 %copy-start.4 = (f32[16]{0:T(128)S(1)}, f32[16]{0:T(128)}, u32[]{:S(2)}) copy-start(f32[16]{0:T(128)} %param.18) | copy-start | bytes 196
  7.2 29.3 %copy-start.5 = (f32[16]{0:T(128)S(1)}, f32[16]{0:T(128)}, u32[]{:S(2)}) copy-start(f32[16]{0:T(128)} %param.19) | copy-start | bytes 196
  7.2 4.3 %collective-permute-start = (bf16[16,1024]{1,0:T(8,128)(2,1)S(1)}, bf16[16,1024]{1,0:T(8,128)(2,1)S(1)}, u32[]{:S(2)}, u32[]{:S(2)}) collective-permute-start(bf16[16,1024]{1,0:T(8,128)(2,1)S(1)} %slice_bitcast_fusion), channel_id=1, source_target_pairs={{0,8},{8,16},{16,24},{24,32},{32,40},{40,48},{48,56},{56,64},{64,7... | collective-permute-start | bytes 98312 | tf_op jit(solution)/shard_map/ppermute | solution.py:291
  19.4 17.1 %collective-permute-start.1 = (bf16[4,160,1024]{2,1,0:T(8,128)(2,1)S(1)}, bf16[4,160,1024]{2,1,0:T(8,128)(2,1)S(1)}, u32[]{:S(2)}, u32[]{:S(2)}) collective-permute-start(bf16[4,160,1024]{2,1,0:T(8,128)(2,1)S(1)} %all-to-all-done.wa), channel_id=1, source_target_pairs={{0,1},{1,0},{2,3},{3,2},{4,5},{5,4},{6,7},{7,6},{8,9},{9,8},{10,11... | collective-permute-start | bytes 3932168 | tf_op jit(solution)/shard_map/ppermute | solution.py:263
  28.0 27.5 %copy-start.6 = (bf16[256,1024]{1,0:T(8,128)(2,1)}, bf16[256,1024]{1,0:T(8,128)(2,1)S(1)}, u32[]{:S(2)}) copy-start(bf16[256,1024]{1,0:T(8,128)(2,1)S(1)} %constant_dynamic-update-slice_fusion.refs_0_) | copy-start | bytes 1572868
  28.0 30.3 %collective-permute-start.2 = (bf16[256,1024]{1,0:T(8,128)(2,1)S(1)}, bf16[256,1024]{1,0:T(8,128)(2,1)S(1)}, u32[]{:S(2)}, u32[]{:S(2)}) collective-permute-start(bf16[256,1024]{1,0:T(8,128)(2,1)S(1)} %constant_dynamic-update-slice_fusion.refs_0_), channel_id=1, source_target_pairs={{0,2},{2,4},{4,6},{6,0},{1,3},{3,5},{5,7},{7,1},{8,10},{10,12},{12... | collective-permute-start | bytes 1572872 | tf_op jit(solution)/shard_map/ppermute | solution.py:303
  30.2 30.0 %collective-permute-start.3 = (bf16[256,1024]{1,0:T(8,128)(2,1)S(1)}, bf16[256,1024]{1,0:T(8,128)(2,1)}, u32[]{:S(2)}, u32[]{:S(2)}) collective-permute-start(bf16[256,1024]{1,0:T(8,128)(2,1)S(1)} %constant_dynamic-update-slice_fusion.refs_0_), channel_id=1, source_target_pairs={{0,4},{2,6},{4,0},{6,2},{1,5},{3,7},{5,1},{7,3},{8,12},{10,14},{12... | collective-permute-start | bytes 1572872 | tf_op jit(solution)/shard_map/ppermute | solution.py:303
  33.9 28.8 %collective-permute-start.4 = (bf16[256,1024]{1,0:T(8,128)(2,1)S(1)}, bf16[256,1024]{1,0:T(8,128)(2,1)}, u32[]{:S(2)}, u32[]{:S(2)}) collective-permute-start(bf16[256,1024]{1,0:T(8,128)(2,1)S(1)} %constant_dynamic-update-slice_fusion.refs_0_), channel_id=1, source_target_pairs={{0,6},{2,0},{4,2},{6,4},{1,7},{3,1},{5,3},{7,5},{8,14},{10,8},{12,... | collective-permute-start | bytes 1572872 | tf_op jit(solution)/shard_map/ppermute | solution.py:303
  39.2 29.2 %all-to-all-start.1 = ((bf16[64,16,128]{2,1,0:T(8,128)(2,1)}), bf16[64,16,128]{2,1,0:T(8,128)(2,1)S(1)}, u32[]{:S(2)}, u32[]{:S(2)}) async-start(bf16[64,16,128]{2,1,0:T(8,128)(2,1)} %get-tuple-element.20), calls=%async_computation.1 | async-start | bytes 524288 | tf_op jit(solution)/shard_map/all_to_all | solution.py:322
  55.5 24.6 %collective-permute-start.5 = (bf16[256,1024]{1,0:T(8,128)(2,1)S(1)}, bf16[256,1024]{1,0:T(8,128)(2,1)S(1)}, u32[]{:S(2)}, u32[]{:S(2)}) collective-permute-start(bf16[256,1024]{1,0:T(8,128)(2,1)S(1)} %constant_dynamic-update-slice_fusion.refs_0_), channel_id=1, source_target_pairs={{0,1},{1,0},{2,3},{3,2},{4,5},{5,4},{6,7},{7,6},{8,9},{9,8},{10,11... | collective-permute-start | bytes 1572872 | tf_op jit(solution)/shard_map/ppermute | solution.py:263
  58.3 22.6 %copy-start.7 = (bf16[256,1024]{1,0:T(8,128)(2,1)}, bf16[256,1024]{1,0:T(8,128)(2,1)S(1)}, u32[]{:S(2)}) copy-start(bf16[256,1024]{1,0:T(8,128)(2,1)S(1)} %collective-permute-done.2.refs_1_) | copy-start | bytes 1572868
  58.3 21.8 %collective-permute-start.6 = (bf16[256,1024]{1,0:T(8,128)(2,1)S(1)}, bf16[256,1024]{1,0:T(8,128)(2,1)}, u32[]{:S(2)}, u32[]{:S(2)}) collective-permute-start(bf16[256,1024]{1,0:T(8,128)(2,1)S(1)} %collective-permute-done.2.refs_1_), channel_id=1, source_target_pairs={{0,1},{1,0},{2,3},{3,2},{4,5},{5,4},{6,7},{7,6},{8,9},{9,8},{10,11... | collective-permute-start | bytes 1572872 | tf_op jit(solution)/shard_map/ppermute | solution.py:263
  60.3 19.9 %collective-permute-start.7 = (bf16[256,1024]{1,0:T(8,128)(2,1)}, bf16[256,1024]{1,0:T(8,128)(2,1)}, u32[]{:S(2)}, u32[]{:S(2)}) collective-permute-start(bf16[256,1024]{1,0:T(8,128)(2,1)} %collective-permute-done.3.refs_2_), channel_id=1, source_target_pairs={{0,1},{1,0},{2,3},{3,2},{4,5},{5,4},{6,7},{7,6},{8,9},{9,8},{10,11... | collective-permute-start | bytes 1572872 | tf_op jit(solution)/shard_map/ppermute | solution.py:263
  62.7 18.2 %collective-permute-start.8 = (bf16[256,1024]{1,0:T(8,128)(2,1)}, bf16[256,1024]{1,0:T(8,128)(2,1)}, u32[]{:S(2)}, u32[]{:S(2)}) collective-permute-start(bf16[256,1024]{1,0:T(8,128)(2,1)} %collective-permute-done.4.refs_3_), channel_id=1, source_target_pairs={{0,1},{1,0},{2,3},{3,2},{4,5},{5,4},{6,7},{7,6},{8,9},{9,8},{10,11... | collective-permute-start | bytes 1572872 | tf_op jit(solution)/shard_map/ppermute | solution.py:263
  69.2 22.5 %all-to-all-start.2 = ((bf16[64,8,128]{2,1,0:T(8,128)(2,1)}), bf16[64,8,128]{2,1,0:T(8,128)(2,1)S(1)}, u32[]{:S(2)}, u32[]{:S(2)}) async-start(bf16[64,8,128]{2,1,0:T(8,128)(2,1)} %shard_map.113), calls=%async_computation.2 | async-start | bytes 262144 | tf_op jit(solution)/shard_map/all_to_all | solution.py:332
  80.1 11.7 %copy-start.2 = (f32[1024]{0:T(1024)S(1)}, f32[1024]{0:T(1024)}, u32[]{:S(2)}) copy-start(f32[1024]{0:T(1024)} %param.20) | copy-start | bytes 12292
  80.1 0.8 copy-start.8

commit v2 on v1

--- a/solution.py
+++ b/solution.py
@@ -1,3 +1,5 @@
+import functools
+
 import jax
 import jax.numpy as jnp
 from jax import lax
@@ -70,20 +72,34 @@
     return copies
 
 
-def pack_kernel(x_ref, bc_ref, dt_ref, out, x, bc, dt, sems):
-    copies = fetch([(x_ref, x), (bc_ref, bc), (dt_ref, dt)], sems)
-    k, width = x.shape
+def pack_kernel(x_ref, bc_ref, dt_ref, z_ref, o_ref, f_ref, first, second, tail, fields, x, bc, dt, sems):
+    k, width = x_ref.shape
     blocks = width // LANES
     part = k // blocks
-    for c in copies:
+    rows = f_ref.shape[0]
+    copies = fetch(
+        [
+            (x_ref, x),
+            (bc_ref, bc),
+            (dt_ref, dt),
+            (f_ref.at[rows - HALO :], tail),
+            (z_ref, second.at[:k]),
+            (o_ref, second.at[k:]),
+            (f_ref, fields),
+        ],
+        sems,
+    )
+    for c in copies[:3]:
         c.wait()
     rest = jnp.zeros((part, width - LANES), BF16)
-    for i in range(out.shape[0]):
-        out[i, :k, :] = x[...]
+    for i in range(first.shape[0]):
+        first[i, :k, :] = x[...]
         for j in range(blocks):
-            out[i, k : k + part, j * LANES : (j + 1) * LANES] = bc[j * part : (j + 1) * part, :]
-        out[i, k + part :, :LANES] = dt[...]
-        out[i, k + part :, LANES:] = rest
+            first[i, k : k + part, j * LANES : (j + 1) * LANES] = bc[j * part : (j + 1) * part, :]
+        first[i, k + part :, :LANES] = dt[...]
+        first[i, k + part :, LANES:] = rest
+    for c in copies[3:]:
+        c.wait()
 
 
 def source_kernel(order, f_ref, halo_ref, out):
@@ -95,9 +111,12 @@
 
 
 def project_kernel(
-    src_ref, wa, wb, conv_x, conv_bc, bias, rate,
-    x_out, bc_out, dt_out, cum_out, msg_out, pre,
+    src_ref, wa, wb, taps_x, taps_bc, bias_ref, rate_ref,
+    x_out, bc_out, dt_out, cum_out, msg_out, pre, conv_x, conv_bc, bias, rate, sems,
 ):
+    copies = fetch(
+        [(taps_x, conv_x), (taps_bc, conv_bc), (bias_ref, bias), (rate_ref, rate)], sems
+    )
     rows, width = x_out.shape
     heads = bias.shape[1]
     half = width // 2
@@ -117,6 +136,8 @@
 
     w_dt = jnp.concatenate([r[i, k + part :, :LANES] for r in (wa, wb) for i in range(n // 2)], 1)
     dt_pre = dot_nt(src[HALO:], w_dt).astype(BF16).astype(F32)
+    for c in copies:
+        c.wait()
     step = jax.nn.softplus(dt_pre + bias[...])
     log_step = -jnp.exp(rate[...]) * step
     lower = (iota((rows, rows), 0) >= iota((rows, rows), 1)).astype(F32)
@@ -195,21 +216,33 @@
         carry = jnp.exp(tail[0:1, :] + tail[1:2, :]) * carry + r_ref[b, :SUB, :].astype(F32)
 
 
-def gate_kernel(order, f_ref, *refs):
-    shards, (out, w, sems) = refs[:-3], refs[-3:]
-    k = w.shape[0] // len(shards)
-    copies = fetch([(r.at[:k], w.at[pl.ds(i * k, k)]) for i, r in enumerate(shards)], sems)
-    src = ordered(f_ref, order, len(shards))
-    for c in copies:
+def gate_kernel(near, order, f_ref, *refs):
+    (out, w_out, w, sems) = refs[-4:]
+    near_refs, (z_ref, o_ref), far_refs = refs[:near], refs[near : near + 2], refs[near + 2 : -4]
+    k = z_ref.shape[0]
+    n = len(far_refs) + 1 + near
+    at = [pl.ds(i * k, k) for i in range(n)]
+    copies = fetch(
+        [(z_ref, w.at[at[0]])]
+        + [(r.at[:k], w.at[at[i]]) for i, r in enumerate(far_refs, 1)]
+        + [(o_ref, w_out.at[at[0]])]
+        + [(r.at[k:], w_out.at[at[i]]) for i, r in enumerate(far_refs, 1)],
+        sems,
+    )
+    for i, r in enumerate(near_refs, n - near):
+        w_out[i * k : (i + 1) * k, :] = r[k:, :]
+    src = ordered(f_ref, order, n)
+    for c in copies[: n - near]:
         c.wait()
-    for at in range(0, out.shape[1], TILE):
-        out[:, at : at + TILE] = dot(src, w[:, at : at + TILE]).astype(BF16)
-
-
-def finish_kernel(order, y_ref, in_ref, bc_ref, cum_ref, gate_ref, gain, *refs):
-    shards, (out, hidden, w, sems) = refs[:-4], refs[-4:]
-    k = w.shape[0] // len(shards)
-    copies = fetch([(r.at[k:], w.at[pl.ds(i * k, k)]) for i, r in enumerate(shards)], sems)
+    for j in range(0, out.shape[1], TILE):
+        cut = slice(j, j + TILE)
+        tile = jnp.concatenate([w[: (n - near) * k, cut]] + [r[:k, cut] for r in near_refs], 0)
+        out[:, cut] = dot(src, tile).astype(BF16)
+    for c in copies[n - near :]:
+        c.wait()
+
+
+def finish_kernel(order, y_ref, in_ref, bc_ref, cum_ref, gate_ref, gain, w, out, hidden):
     rows, width = y_ref.shape
     half = width // 2
     bc = bc_ref[...].astype(F32)
@@ -228,9 +261,7 @@
     scale = lax.rsqrt(square / width + EPS)
     for i, at in enumerate(range(0, width, TILE)):
         hidden[:, at : at + TILE] = (parts[i] * scale * gain[:, at : at + TILE]).astype(BF16)
-    src = ordered(hidden, order, len(shards))
-    for c in copies:
-        c.wait()
+    src = ordered(hidden, order, width // LANES)
     for at in range(0, out.shape[1], TILE):
         out[:, at : at + TILE] = dot(src, w[:, at : at + TILE]).astype(BF16)
 
@@ -246,7 +277,7 @@
         pltpu.with_memory_space_constraint(a, pltpu.MemorySpace.HBM) if i >= len(args) - hbm else a
         for i, a in enumerate(args)
     ]
-    scratch = list(scratch) + ([pltpu.SemaphoreType.DMA((hbm,))] if hbm else [])
+    scratch = list(scratch) + ([pltpu.SemaphoreType.DMA((2 * hbm,))] if hbm else [])
     nbytes = sum(a.size * a.dtype.itemsize for a in args)
     return pl.pallas_call(
         body,
@@ -257,10 +288,6 @@
         compiler_params=pltpu.CompilerParams(vmem_limit_bytes=16 * 2**20),
         cost_estimate=pl.CostEstimate(flops=flops, bytes_accessed=nbytes, transcendentals=0),
     )(*args)
-
-
-def other_core(block):
-    return lax.ppermute(block, "c", [(0, 1), (1, 0)])
 
 
 def local(
@@ -276,35 +303,43 @@
     sds = jax.ShapeDtypeStruct
 
     k = proj_x.shape[0]
-    first = call(
+    x_at, c_at = lax.axis_index("x"), lax.axis_index("c")
+    each = jnp.arange(2 * n_x)
+    order = each % n_x * 2 + (c_at + each // n_x) % 2
+    late = jnp.array([0, 1, 3, 2, 4, 6, 5, 7])
+    order2 = (x_at - late + 2 * n_x) % n_x * 2 + (c_at + late // n_x) % 2
+    first, second, tail, f = call(
         pack_kernel,
-        sds((n_x, k + 2 * k * LANES // width, width), BF16),
-        [proj_x, proj_bc, proj_dt.T],
-        hbm=3,
+        (
+            sds((n_x, k + 2 * k * LANES // width, width), BF16),
+            sds((2 * k, width), BF16),
+            sds((HALO, depth), BF16),
+            sds((rows, depth), BF16),
+        ),
+        [proj_x, proj_bc, proj_dt.T, proj_z, proj_out, f],
+        hbm=6,
         scratch=[
             pltpu.VMEM(proj_x.shape, BF16),
             pltpu.VMEM(proj_bc.shape, BF16),
             pltpu.VMEM(proj_dt.shape[::-1], BF16),
         ],
     )
+
+    def across(block):
+        return lax.ppermute(block, "c", [(0, 1), (1, 0)])
+
     w1a = lax.all_to_all(first, "x", 0, 0)
-    halo = lax.ppermute(f[rows - HALO :], LAT, [(i, i + 1) for i in range(bands - 1)])
-    x_at, c_at = lax.axis_index("x"), lax.axis_index("c")
-    x_all = jnp.arange(n_x)
-    order = jnp.concatenate([x_all * 2 + c_at, x_all * 2 + 1 - c_at]).astype(jnp.int32)
-    x_near = (x_at - x_all + n_x) % n_x
-    order2 = jnp.concatenate([x_near * 2 + c_at, x_near * 2 + 1 - c_at]).astype(jnp.int32)
-    second = jnp.concatenate([proj_z, proj_out], 0)
+    halo = lax.ppermute(tail, LAT, [(i, i + 1) for i in range(bands - 1)])
+    w2a, w2b = [second], [across(second)]
     src = call(
         source_kernel, sds((HALO + rows, depth), BF16), [order, f, halo], smem=1, flops=10**6
     )
-    w2a, w2b = [second], []
+    w1a, src, second, order2 = lax.optimization_barrier((w1a, src, second, order2))
+    w1b = across(w1a)
     for d in range(1, n_x):
         w2a.append(lax.ppermute(second, "x", [(i, (i + d) % n_x) for i in range(n_x)]))
-    w1a, src, order2 = lax.optimization_barrier((w1a, src, order2))
-    w1b = other_core(w1a)
-    for d in range(n_x):
-        w2b.append(other_core(w2a[d]))
+    for d in range(1, n_x):
+        w2b.append(across(w2a[d]))
 
     x_act, bc_act, step, cum, msg = call(
         project_kernel,
@@ -316,7 +351,9 @@
             sds((bands, 2 * SUB, LANES), BF16),
         ),
         [src, w1a, w1b, conv_x, conv_bc, dt_bias[None], log_rate[None]],
-        scratch=[pltpu.VMEM((HALO + rows, width + 2 * state), F32)],
+        hbm=4,
+        scratch=[pltpu.VMEM((HALO + rows, width + 2 * state), F32)]
+        + [pltpu.VMEM(a.shape, F32) for a in (conv_x, conv_bc, dt_bias[None], log_rate[None])],
         flops=2 * rows * depth * (width + 2 * LANES),
     )
     got = lax.all_to_all(msg, LAT, 0, 0)
@@ -331,22 +368,22 @@
     )
     incoming = lax.all_to_all(entering, LAT, 0, 0)
     incoming = incoming.reshape(bands * SUB, LANES)
-    gate = call(
-        gate_kernel,
-        sds((rows, width), BF16),
-        [order2, f, *w2a, *w2b],
+    near = []
+    gate, w_out = call(
+        functools.partial(gate_kernel, len(near)),
+        (sds((rows, width), BF16), sds((width, depth), BF16)),
+        [order2, f, *near, proj_z, proj_out, w2a[1], w2a[3], w2a[2], w2b[0], w2b[2], w2b[1], w2b[3]],
         smem=1,
-        hbm=2 * n_x,
+        hbm=9,
         scratch=[pltpu.VMEM((depth, width), BF16)],
         flops=2 * rows * depth * width,
     )
     out = call(
         finish_kernel,
         sds((rows, depth), BF16),
-        [order2, y, incoming, bc_act, cum, gate, norm_gain[None], *w2a, *w2b],
+        [order2, y, incoming, bc_act, cum, gate, norm_gain[None], w_out],
         smem=1,
-        hbm=2 * n_x,
-        scratch=[pltpu.VMEM((rows, width), BF16), pltpu.VMEM((width, depth), BF16)],
+        scratch=[pltpu.VMEM((rows, width), BF16)],
         flops=2 * rows * depth * width,
     )
     return out.reshape(rows, 1, depth)

time: 95.9 us -> 93.5 us (0.975)
  starting transfers between devices: 61.5 us -> 60 us
  waiting for transfers between devices: 19.4 us -> 17.9 us
    all_to_all x1, starting transfers between devices: 10.9 us -> 9.1 us  [local(): incoming = lax.all_to_all(entering, LAT, 0, 0)]
    all_to_all x1, waiting for transfers between devices: 7.61 us -> 6.25 us  [local(): incoming = lax.all_to_all(entering, LAT, 0, 0)]
  transfers between devices with their start and end apart: 12 -> 12, of which waited for: 4 -> 4; matrix products, arithmetic and copies ran while one was open for 0% -> 0% of each run, Pallas kernels for 8% -> 9%
where the time goes in v2:
time: 93.5 us; the launch traced here: 92.9 us
  starting transfers between devices  60 us (64%)
  waiting for transfers between devices  17.9 us (19%)
  Pallas kernels  13 us (14%)
  local copies, waits for them, and re-layouts  1.77 us (2%)
    ppermute x5, starting transfers between devices, across(): return lax.ppermute(block, 'c', [(0, 1), (1, 0)])  17.9 us
    all_to_all x1, starting transfers between devices, local(): got = lax.all_to_all(msg, LAT, 0, 0)  16.3 us
    pallas_call x7, Pallas kernels, call(): pl.pallas_call(body, out_shape=outs, in_specs=specs, out_specs=jax.tree.m...  13 us
    all_to_all x1, starting transfers between devices, local(): incoming = lax.all_to_all(entering, LAT, 0, 0)  9.1 us
    ppermute x3, starting transfers between devices, local(): lax.ppermute(second, 'x', [(i, (i + d) % n_x) for i in range(n_x)])  8.72 us
    all_to_all x1, waiting for transfers between devices, local(): w1a = lax.all_to_all(first, 'x', 0, 0)  7.36 us
    all_to_all x1, waiting for transfers between devices, local(): incoming = lax.all_to_all(entering, LAT, 0, 0)  6.25 us
    all_to_all x1, starting transfers between devices, local(): w1a = lax.all_to_all(first, 'x', 0, 0)  4.84 us
  transfers between devices with their start and end apart: 12, of which 4 were waited for; matrix products, arithmetic and copies ran while one was open for 0% of the time, Pallas kernels for 9%

profile of v2, /device:TPU:1, one launch (start us, length us, event | category | flops | bytes accessed | tf_op | source)
XLA Modules:
  0.0 92.9 jit_solution(13294368135348271351)
XLA Ops:
  0.0 2.6 %shard_map.118 = (bf16[4,160,1024]{2,1,0:T(8,128)(2,1)}, bf16[256,1024]{1,0:T(8,128)(2,1)}, bf16[16,1024]{1,0:T(8,128)(2,1)S(1)}, bf16[128,1024]{1,0:T(8,128)(2,1)S(1)}) custom-call(bf16[128,1024]{1,0:T(8,128)(2,1)} %x_ref.1, bf16[128,128]{1,0:T(8,128)(2,1)} %bc_ref.1, bf16[16,128]{1,0:T(8,128)(2,1)} %bitcast.10, bf16[128,1024]{1,0:T(8,128)(2,1)} %refs_0_.1, ...), custom_call_target="tpu_custom_call" | custom-call | bytes 1085440 | tf_op jit(solution)/shard_map/pallas_call | solution.py:282
  2.6 0.0 copy-start.4
  2.6 0.0 copy-start.5
  2.6 4.8 %all-to-all-start = ((bf16[4,160,1024]{2,1,0:T(8,128)(2,1)}), bf16[4,160,1024]{2,1,0:T(8,128)(2,1)S(1)}, u32[]{:S(2)}, u32[]{:S(2)}) async-start(bf16[4,160,1024]{2,1,0:T(8,128)(2,1)} %get-tuple-element.20), calls=%async_computation | async-start | bytes 2621440 | tf_op jit(solution)/shard_map/all_to_all | solution.py:331
  7.5 3.2 %collective-permute-start = (bf16[16,1024]{1,0:T(8,128)(2,1)S(1)}, bf16[16,1024]{1,0:T(8,128)(2,1)S(1)}, u32[]{:S(2)}, u32[]{:S(2)}) collective-permute-start(bf16[16,1024]{1,0:T(8,128)(2,1)S(1)} %get-tuple-element.22), channel_id=1, source_target_pairs={{0,8},{8,16},{16,24},{24,32},{32,40},{40,48},{48,56},{56,64},{64,7... | collective-permute-start | bytes 98312 | tf_op jit(solution)/shard_map/ppermute | solution.py:332
  10.7 0.0 copy-done.4
  10.7 0.0 copy-done.5
  10.7 1.0 %collective-permute-done.halo_ref = bf16[16,1024]{1,0:T(8,128)(2,1)S(1)} collective-permute-done((bf16[16,1024]{1,0:T(8,128)(2,1)S(1)}, bf16[16,1024]{1,0:T(8,128)(2,1)S(1)}, u32[]{:S(2)}, u32[]{:S(2)}) %collective-permute-start) | collective-permute-done | bytes 32800 | tf_op jit(solution)/shard_map/ppermute | solution.py:332
  11.7 0.6 shard_map.119.src_ref
  12.3 7.4 %all-to-all-done.wa = bf16[4,160,1024]{2,1,0:T(8,128)(2,1)S(1)} async-done(((bf16[4,160,1024]{2,1,0:T(8,128)(2,1)}), bf16[4,160,1024]{2,1,0:T(8,128)(2,1)S(1)}, u32[]{:S(2)}, u32[]{:S(2)}) %all-to-all-start) | async-done | bytes 1310752 | tf_op jit(solution)/shard_map/all_to_all | solution.py:331
  19.7 8.6 %collective-permute-start.1 = (bf16[4,160,1024]{2,1,0:T(8,128)(2,1)S(1)}, bf16[4,160,1024]{2,1,0:T(8,128)(2,1)S(1)}, u32[]{:S(2)}, u32[]{:S(2)}) collective-permute-start(bf16[4,160,1024]{2,1,0:T(8,128)(2,1)S(1)} %all-to-all-done.wa), channel_id=1, source_target_pairs={{0,1},{1,0},{2,3},{3,2},{4,5},{5,4},{6,7},{7,6},{8,9},{9,8},{10,11... | collective-permute-start | bytes 3932168 | tf_op jit(solution)/shard_map/ppermute | solution.py:329
  28.2 2.2 %collective-permute-start.4 = (bf16[256,1024]{1,0:T(8,128)(2,1)}, bf16[256,1024]{1,0:T(8,128)(2,1)}, u32[]{:S(2)}, u32[]{:S(2)}) collective-permute-start(bf16[256,1024]{1,0:T(8,128)(2,1)} %get-tuple-element.32), channel_id=1, source_target_pairs={{0,4},{2,6},{4,0},{6,2},{1,5},{3,7},{5,1},{7,3},{8,12},{10,14},{12... | collective-permute-start | bytes 1572872 | tf_op jit(solution)/shard_map/ppermute | solution.py:340
  30.5 3.1 %collective-permute-start.2 = (bf16[256,1024]{1,0:T(8,128)(2,1)}, bf16[256,1024]{1,0:T(8,128)(2,1)}, u32[]{:S(2)}, u32[]{:S(2)}) collective-permute-start(bf16[256,1024]{1,0:T(8,128)(2,1)} %get-tuple-element.32), channel_id=1, source_target_pairs={{0,2},{2,4},{4,6},{6,0},{1,3},{3,5},{5,7},{7,1},{8,10},{10,12},{12... | collective-permute-start | bytes 1572872 | tf_op jit(solution)/shard_map/ppermute | solution.py:340
  33.5 3.4 %collective-permute-start.3 = (bf16[256,1024]{1,0:T(8,128)(2,1)}, bf16[256,1024]{1,0:T(8,128)(2,1)}, u32[]{:S(2)}, u32[]{:S(2)}) collective-permute-start(bf16[256,1024]{1,0:T(8,128)(2,1)} %get-tuple-element.32), channel_id=1, source_target_pairs={{0,6},{2,0},{4,2},{6,4},{1,7},{3,1},{5,3},{7,5},{8,14},{10,8},{12,... | collective-permute-start | bytes 1572872 | tf_op jit(solution)/shard_map/ppermute | solution.py:340
  37.0 0.0 collective-permute-done.1.wb
  37.0 3.3 %shard_map.120 = (bf16[128,1024]{1,0:T(8,128)(2,1)S(1)}, bf16[128,128]{1,0:T(8,128)(2,1)S(1)}, f32[128,16]{1,0:T(8,128)S(1)}, f32[128,16]{1,0:T(8,128)S(1)}, bf16[64,16,128]{2,1,0:T(8,128)(2,1)}) custom-call(bf16[144,1024]{1,0:T(8,128)(2,1)S(1)} %shard_map.119.src_ref, bf16[4,160,1024]{2,1,0:T(8,128)(2,1)S(1)} %all-to-all-done.wa, ...), custom_call_target="tpu_custom_call" | custom-call | flops 335544320 | bytes 2934912 | tf_op jit(solution)/shard_map/pallas_call | solution.py:282
  40.3 16.3 %all-to-all-start.1 = ((bf16[64,16,128]{2,1,0:T(8,128)(2,1)}), bf16[64,16,128]{2,1,0:T(8,128)(2,1)S(1)}, u32[]{:S(2)}, u32[]{:S(2)}) async-start(bf16[64,16,128]{2,1,0:T(8,128)(2,1)} %get-tuple-element.31), calls=%async_computation.1 | async-start | bytes 524288 | tf_op jit(solution)/shard_map/all_to_all | solution.py:359
  56.6 3.0 %collective-permute-start.5 = (bf16[256,1024]{1,0:T(8,128)(2,1)}, bf16[256,1024]{1,0:T(8,128)(2,1)S(1)}, u32[]{:S(2)}, u32[]{:S(2)}) collective-permute-start(bf16[256,1024]{1,0:T(8,128)(2,1)} %get-tuple-element.32), channel_id=1, source_target_pairs={{0,1},{1,0},{2,3},{3,2},{4,5},{5,4},{6,7},{7,6},{8,9},{9,8},{10,11... | collective-permute-start | bytes 1572872 | tf_op jit(solution)/shard_map/ppermute | solution.py:329
  59.6 0.0 collective-permute-done.4.refs_4_
  59.6 1.9 %collective-permute-start.6 = (bf16[256,1024]{1,0:T(8,128)(2,1)}, bf16[256,1024]{1,0:T(8,128)(2,1)S(1)}, u32[]{:S(2)}, u32[]{:S(2)}) collective-permute-start(bf16[256,1024]{1,0:T(8,128)(2,1)} %collective-permute-done.4.refs_4_), channel_id=1, source_target_pairs={{0,1},{1,0},{2,3},{3,2},{4,5},{5,4},{6,7},{7,6},{8,9},{9,8},{10,11... | collective-permute-start | bytes 1572872 | tf_op jit(solution)/shard_map/ppermute | solution.py:329
  61.6 0.0 collective-permute-done.2.refs_2_
  61.6 2.4 %collective-permute-start.7 = (bf16[256,1024]{1,0:T(8,128)(2,1)}, bf16[256,1024]{1,0:T(8,128)(2,1)S(1)}, u32[]{:S(2)}, u32[]{:S(2)}) collective-permute-start(bf16[256,1024]{1,0:T(8,128)(2,1)} %collective-permute-done.2.refs_2_), channel_id=1, source_target_pairs={{0,1},{1,0},{2,3},{3,2},{4,5},{5,4},{6,7},{7,6},{8,9},{9,8},{10,11... | collective-permute-start | bytes 1572872 | tf_op jit(solution)/shard_map/ppermute | solution.py:329
  64.0 0.0 collective-permute-done.3.refs_3_
  64.0 1.9 %collective-permute-start.8 = (bf16[256,1024]{1,0:T(8,128)(2,1)}, bf16[256,1024]{1,0:T(8,128)(2,1)}, u32[]{:S(2)}, u32[]{:S(2)}) collective-permute-start(bf16[256,1024]{1,0:T(8,128)(2,1)} %collective-permute-done.3.refs_3_), channel_id=1, source_target_pairs={{0,1},{1,0},{2,3},{3,2},{4,5},{5,4},{6,7},{7,6},{8,9},{9,8},{10,11... | collective-permute-start | bytes 1572872 | tf_op jit(solution)/shard_map/ppermute | solution.py:329
  65.9 3.3 %all-to-all-done.1.r_ref = bf16[64,16,128]{2,1,0:T(8,128)(2,1)S(1)} async-done(((bf16[64,16,128]{2,1,0:T(8,128)(2,1)}), bf16[64,16,128]{2,1,0:T(8,128)(2,1)S(1)}, u32[]{:S(2)}, u32[]{:S(2)}) %all-to-all-start.1) | async-done | bytes 262176 | tf_op jit(solution)/shard_map/all_to_all | solution.py:359
  69.3 0.8 shard_map.122
  70.1 9.1 %all-to-all-start.2 = ((bf16[64,8,128]{2,1,0:T(8,128)(2,1)}), bf16[64,8,128]{2,1,0:T(8,128)(2,1)S(1)}, u32[]{:S(2)}, u32[]{:S(2)}) async-start(bf16[64,8,128]{2,1,0:T(8,128)(2,1)} %shard_map.122), calls=%async_computation.2 | async-start | bytes 262144 | tf_op jit(solution)/shard_map/all_to_all | solution.py:369
  79.2 0.0 copy-start
  79.2 0.0 collective-permute-done.5.refs_5_
  79.2 0.0 copy-start.1
  79.2 0.0 collective-permute-done.6.refs_6_
  79.2 0.0 copy-start.2
  79.2 0.0 collective-permute-done.7.refs_7_
  79.2 0.8 copy-done.1
  80.0 0.2 copy-done.2
  80.2 0.0 copy-start.3
  80.2 0.8 copy-done.3
  81.0 0.0 collective-permute-done.8.refs_8_
  81.0 2.8 %shard_map.123 = (bf16[128,1024]{1,0:T(8,128)(2,1)S(1)}, bf16[1024,1024]{1,0:T(8,128)(2,1)S(1)}) custom-call(s32[8]{0:T(128)S(1)} %get-tuple-element.24.order, bf16[128,1024]{1,0:T(8,128)(2,1)S(1)} %get-tuple-element.21.f_ref, bf16[128,1024]{1,0:T(8,128)(2,1)} %refs_0_.1, bf16[128,1024]{1,0:T(8,128)(2,1)} %refs_1_.1, ...), custom_call_target="tpu_custom_call" | custom-call | flops 268435456 | bytes 4456480 | tf_op jit(solution)/shard_map/pallas_call | solution.py:282
  83.8 0.6 shard_map.121.y_ref
  84.5 6.2 %all-to-all-done.2 = bf16[64,8,128]{2,1,0:T(8,128)(2,1)S(1)} async-done(((bf16[64,8,128]{2,1,0:T(8,128)(2,1)}), bf16[64,8,128]{2,1,0:T(8,128)(2,1)S(1)}, u32[]{:S(2)}, u32[]{:S(2)}) %all-to-all-start.2) | async-done | bytes 131104 | tf_op jit(solution)/shard_map/all_to_all | solution.py:369
  90.7 0.0 copy-done
  90.7 2.2 %shard_map.124 = bf16[128,1024]{1,0:T(8,128)(2,1)} custom-call(s32[8]{0:T(128)S(1)} %get-tuple-element.24.order, f32[128,1024]{1,0:T(8,128)S(1)} %shard_map.121.y_ref, bf16[512,128]{1,0:T(8,128)(2,1)S(1)} %bitcast.7, bf16[128,128]{1,0:T(8,128)(2,1)S(1)} %get-tuple-element.28.bc_ref, f32[128,16]{1,0:T(8,128)S(1)} %get-tuple-element.30.cum_ref, ...), custom_call_target="tpu_custom_call" | custom-call | flops 268435456 | bytes 3059744 | tf_op jit(solution)/shard_map/pallas_call | solution.py:282
  (1 shorter events, 0.0 us)
Async XLA Ops:
  2.6 8.1 %copy-start.4 = (s32[8]{0:T(128)S(1)}, s32[8]{0:T(128)}, u32[]{:S(2)}) copy-start(s32[8]{0:T(128)} %constant.88) | copy-start | bytes 100
  2.6 8.1 %copy-start.5 = (s32[8]{0:T(128)S(1)}, s32[8]{0:T(128)}, u32[]{:S(2)}) copy-start(s32[8]{0:T(128)} %constant.74) | copy-start | bytes 100
  2.6 17.0 %all-to-all-start = ((bf16[4,160,1024]{2,1,0:T(8,128)(2,1)}), bf16[4,160,1024]{2,1,0:T(8,128)(2,1)S(1)}, u32[]{:S(2)}, u32[]{:S(2)}) async-start(bf16[4,160,1024]{2,1,0:T(8,128)(2,1)} %get-tuple-element.20), calls=%async_computation | async-start | bytes 2621440 | tf_op jit(solution)/shard_map/all_to_all | solution.py:331
  7.5 4.2 %collective-permute-start = (bf16[16,1024]{1,0:T(8,128)(2,1)S(1)}, bf16[16,1024]{1,0:T(8,128)(2,1)S(1)}, u32[]{:S(2)}, u32[]{:S(2)}) collective-permute-start(bf16[16,1024]{1,0:T(8,128)(2,1)S(1)} %get-tuple-element.22), channel_id=1, source_target_pairs={{0,8},{8,16},{16,24},{24,32},{32,40},{40,48},{48,56},{56,64},{64,7... | collective-permute-start | bytes 98312 | tf_op jit(solution)/shard_map/ppermute | solution.py:332
  19.7 17.3 %collective-permute-start.1 = (bf16[4,160,1024]{2,1,0:T(8,128)(2,1)S(1)}, bf16[4,160,1024]{2,1,0:T(8,128)(2,1)S(1)}, u32[]{:S(2)}, u32[]{:S(2)}) collective-permute-start(bf16[4,160,1024]{2,1,0:T(8,128)(2,1)S(1)} %all-to-all-done.wa), channel_id=1, source_target_pairs={{0,1},{1,0},{2,3},{3,2},{4,5},{5,4},{6,7},{7,6},{8,9},{9,8},{10,11... | collective-permute-start | bytes 3932168 | tf_op jit(solution)/shard_map/ppermute | solution.py:329
  28.2 31.4 %collective-permute-start.4 = (bf16[256,1024]{1,0:T(8,128)(2,1)}, bf16[256,1024]{1,0:T(8,128)(2,1)}, u32[]{:S(2)}, u32[]{:S(2)}) collective-permute-start(bf16[256,1024]{1,0:T(8,128)(2,1)} %get-tuple-element.32), channel_id=1, source_target_pairs={{0,4},{2,6},{4,0},{6,2},{1,5},{3,7},{5,1},{7,3},{8,12},{10,14},{12... | collective-permute-start | bytes 1572872 | tf_op jit(solution)/shard_map/ppermute | solution.py:340
  30.5 31.1 %collective-permute-start.2 = (bf16[256,1024]{1,0:T(8,128)(2,1)}, bf16[256,1024]{1,0:T(8,128)(2,1)}, u32[]{:S(2)}, u32[]{:S(2)}) collective-permute-start(bf16[256,1024]{1,0:T(8,128)(2,1)} %get-tuple-element.32), channel_id=1, source_target_pairs={{0,2},{2,4},{4,6},{6,0},{1,3},{3,5},{5,7},{7,1},{8,10},{10,12},{12... | collective-permute-start | bytes 1572872 | tf_op jit(solution)/shard_map/ppermute | solution.py:340
  33.5 30.5 %collective-permute-start.3 = (bf16[256,1024]{1,0:T(8,128)(2,1)}, bf16[256,1024]{1,0:T(8,128)(2,1)}, u32[]{:S(2)}, u32[]{:S(2)}) collective-permute-start(bf16[256,1024]{1,0:T(8,128)(2,1)} %get-tuple-element.32), channel_id=1, source_target_pairs={{0,6},{2,0},{4,2},{6,4},{1,7},{3,1},{5,3},{7,5},{8,14},{10,8},{12,... | collective-permute-start | bytes 1572872 | tf_op jit(solution)/shard_map/ppermute | solution.py:340
  40.3 29.0 %all-to-all-start.1 = ((bf16[64,16,128]{2,1,0:T(8,128)(2,1)}), bf16[64,16,128]{2,1,0:T(8,128)(2,1)S(1)}, u32[]{:S(2)}, u32[]{:S(2)}) async-start(bf16[64,16,128]{2,1,0:T(8,128)(2,1)} %get-tuple-element.31), calls=%async_computation.1 | async-start | bytes 524288 | tf_op jit(solution)/shard_map/all_to_all | solution.py:359
  56.6 22.6 %collective-permute-start.5 = (bf16[256,1024]{1,0:T(8,128)(2,1)}, bf16[256,1024]{1,0:T(8,128)(2,1)S(1)}, u32[]{:S(2)}, u32[]{:S(2)}) collective-permute-start(bf16[256,1024]{1,0:T(8,128)(2,1)} %get-tuple-element.32), channel_id=1, source_target_pairs={{0,1},{1,0},{2,3},{3,2},{4,5},{5,4},{6,7},{7,6},{8,9},{9,8},{10,11... | collective-permute-start | bytes 1572872 | tf_op jit(solution)/shard_map/ppermute | solution.py:329
  59.6 19.6 %collective-permute-start.6 = (bf16[256,1024]{1,0:T(8,128)(2,1)}, bf16[256,1024]{1,0:T(8,128)(2,1)S(1)}, u32[]{:S(2)}, u32[]{:S(2)}) collective-permute-start(bf16[256,1024]{1,0:T(8,128)(2,1)} %collective-permute-done.4.refs_4_), channel_id=1, source_target_pairs={{0,1},{1,0},{2,3},{3,2},{4,5},{5,4},{6,7},{7,6},{8,9},{9,8},{10,11... | collective-permute-start | bytes 1572872 | tf_op jit(solution)/shard_map/ppermute | solution.py:329
  61.6 17.6 %collective-permute-start.7 = (bf16[256,1024]{1,0:T(8,128)(2,1)}, bf16[256,1024]{1,0:T(8,128)(2,1)S(1)}, u32[]{:S(2)}, u32[]{:S(2)}) collective-permute-start(bf16[256,1024]{1,0:T(8,128)(2,1)} %collective-permute-done.2.refs_2_), channel_id=1, source_target_pairs={{0,1},{1,0},{2,3},{3,2},{4,5},{5,4},{6,7},{7,6},{8,9},{9,8},{10,11... | collective-permute-start | bytes 1572872 | tf_op jit(solution)/shard_map/ppermute | solution.py:329
  64.0 17.0 %collective-permute-start.8 = (bf16[256,1024]{1,0:T(8,128)(2,1)}, bf16[256,1024]{1,0:T(8,128)(2,1)}, u32[]{:S(2)}, u32[]{:S(2)}) collective-permute-start(bf16[256,1024]{1,0:T(8,128)(2,1)} %collective-permute-done.3.refs_3_), channel_id=1, source_target_pairs={{0,1},{1,0},{2,3},{3,2},{4,5},{5,4},{6,7},{7,6},{8,9},{9,8},{10,11... | collective-permute-start | bytes 1572872 | tf_op jit(solution)/shard_map/ppermute | solution.py:329
  70.1 20.6 %all-to-all-start.2 = ((bf16[64,8,128]{2,1,0:T(8,128)(2,1)}), bf16[64,8,128]{2,1,0:T(8,128)(2,1)S(1)}, u32[]{:S(2)}, u32[]{:S(2)}) async-start(bf16[64,8,128]{2,1,0:T(8,128)(2,1)} %shard_map.122), calls=%async_computation.2 | async-start | bytes 262144 | tf_op jit(solution)/shard_map/all_to_all | solution.py:369
  79.2 11.5 %copy-start = (f32[1024]{0:T(1024)S(1)}, f32[1024]{0:T(1024)}, u32[]{:S(2)}) copy-start(f32[1024]{0:T(1024)} %param.21) | copy-start | bytes 12292
  79.2 0.8 copy-start.1
  79.2 1.0 %copy-start.2 = (bf16[256,1024]{1,0:T(8,128)(2,1)}, bf16[256,1024]{1,0:T(8,128)(2,1)S(1)}, u32[]{:S(2)}) copy-start(bf16[256,1024]{1,0:T(8,128)(2,1)S(1)} %collective-permute-done.6.refs_6_) | copy-start | bytes 1572868
  80.2 0.8 copy-start.3

commit v3 on v2

--- a/solution.py
+++ b/solution.py
@@ -72,24 +72,14 @@
     return copies
 
 
-def pack_kernel(x_ref, bc_ref, dt_ref, z_ref, o_ref, f_ref, first, second, tail, fields, x, bc, dt, sems):
+def pack_kernel(x_ref, bc_ref, dt_ref, f_ref, first, tail, x, bc, dt, sems):
     k, width = x_ref.shape
     blocks = width // LANES
     part = k // blocks
-    rows = f_ref.shape[0]
     copies = fetch(
-        [
-            (x_ref, x),
-            (bc_ref, bc),
-            (dt_ref, dt),
-            (f_ref.at[rows - HALO :], tail),
-            (z_ref, second.at[:k]),
-            (o_ref, second.at[k:]),
-            (f_ref, fields),
-        ],
-        sems,
-    )
-    for c in copies[:3]:
+        [(x_ref, x), (bc_ref, bc), (dt_ref, dt), (f_ref.at[f_ref.shape[0] - HALO :], tail)], sems
+    )
+    for c in copies:
         c.wait()
     rest = jnp.zeros((part, width - LANES), BF16)
     for i in range(first.shape[0]):
@@ -98,27 +88,46 @@
             first[i, k : k + part, j * LANES : (j + 1) * LANES] = bc[j * part : (j + 1) * part, :]
         first[i, k + part :, :LANES] = dt[...]
         first[i, k + part :, LANES:] = rest
-    for c in copies[3:]:
-        c.wait()
-
-
-def source_kernel(order, f_ref, halo_ref, out):
+
+
+def source_kernel(order, halo_ref, *refs):
+    z_ref, o_ref, f_ref = refs[:3]
+    small_refs = refs[3:7]
+    out, second, fields = refs[7:10]
+    small, sems = refs[10:14], refs[14]
+    k = z_ref.shape[0]
+    copies = fetch(
+        [(f_ref, fields), (z_ref, second.at[:k]), (o_ref, second.at[k:])]
+        + list(zip(small_refs, small)),
+        sems,
+    )
     n = out.shape[1] // LANES
+    copies[0].wait()
     for j in range(n):
         at = slice(j * LANES, (j + 1) * LANES)
         out[:HALO, at] = chunk(halo_ref, order[j])
-        out[HALO:, at] = chunk(f_ref, order[j])
+        out[HALO:, at] = chunk(fields, order[j])
+    for c in copies[1:]:
+        c.wait()
+
+
+def tail_rows(high, low):
+    row = iota((SUB, LANES), 0)
+    return jnp.where(row == 0, high, jnp.where(row == 1, low, 0.0)).astype(BF16)
+
+
+def part_of(ref, b):
+    size = ref.shape[1] - SUB
+    tail = ref[b, size:, :].astype(F32)
+    return ref[b, :size, :].astype(F32), tail[0:1, :] + tail[1:2, :]
 
 
 def project_kernel(
-    src_ref, wa, wb, taps_x, taps_bc, bias_ref, rate_ref,
-    x_out, bc_out, dt_out, cum_out, msg_out, pre, conv_x, conv_bc, bias, rate, sems,
+    src_ref, wa, wb, conv_x, conv_bc, bias, rate, x_out, bc_out, dt_out, cum_out, msg_out, pre
 ):
-    copies = fetch(
-        [(taps_x, conv_x), (taps_bc, conv_bc), (bias_ref, bias), (rate_ref, rate)], sems
-    )
     rows, width = x_out.shape
     heads = bias.shape[1]
+    per = width // heads
     half = width // 2
     k = LANES
     n = 2 * wa.shape[0]
@@ -136,8 +145,6 @@
 
     w_dt = jnp.concatenate([r[i, k + part :, :LANES] for r in (wa, wb) for i in range(n // 2)], 1)
     dt_pre = dot_nt(src[HALO:], w_dt).astype(BF16).astype(F32)
-    for c in copies:
-        c.wait()
     step = jax.nn.softplus(dt_pre + bias[...])
     log_step = -jnp.exp(rate[...]) * step
     lower = (iota((rows, rows), 0) >= iota((rows, rows), 1)).astype(F32)
@@ -174,17 +181,14 @@
 
     for at in range(0, half, TILE):
         t = end(at, 0) + end(half + at, 1)
-        msg_out[at // SUB : (at + TILE) // SUB, :SUB, :] = t.reshape(TILE // SUB, SUB, LANES).astype(BF16)
+        for i in range(0, TILE, per):
+            msg_out[(at + i) // per, :per, :] = t[i : i + per].astype(BF16)
     pairs = heads // 2
     mine = iota((pairs, heads), 1) % pairs == iota((pairs, heads), 0)
     pick = (iota((heads, LANES), 1) // (LANES // 2) == iota((heads, LANES), 0) // pairs).astype(BF16)
     high, low = (dot(jnp.where(mine, v.astype(F32), 0.0).astype(BF16), pick) for v in halves(last))
-    row = iota((SUB, LANES), 0)
-    each = msg_out.shape[0] // pairs
     for j in range(pairs):
-        tail = jnp.where(row == 0, high[j : j + 1, :], jnp.where(row == 1, low[j : j + 1, :], 0.0))
-        for i in range(each):
-            msg_out[j * each + i, SUB:, :] = tail.astype(BF16)
+        msg_out[j, per:, :] = tail_rows(high[j : j + 1, :], low[j : j + 1, :])
 
 
 def within_kernel(x_ref, bc_ref, dt_ref, cum_ref, y_out):
@@ -208,12 +212,29 @@
         y_out[:, pair * LANES : (pair + 1) * LANES] = dot(jnp.concatenate(w, 1), both)
 
 
-def bands_kernel(r_ref, e_out):
-    carry = jnp.zeros(e_out.shape[1:], F32)
+def row_kernel(r_ref, before, decay, msg_out):
+    state = jnp.zeros(before.shape[1:], F32)
+    total = jnp.zeros((1, LANES), F32)
+    for b in range(r_ref.shape[0]):
+        before[b] = state
+        decay[b : b + 1, :] = total
+        own, step = part_of(r_ref, b)
+        state = jnp.exp(step) * state + own
+        total = total + step
+    high, low = (v.astype(F32) for v in halves(total))
+    tail = tail_rows(high, low)
+    for z in range(msg_out.shape[0]):
+        msg_out[z, : state.shape[0], :] = state.astype(BF16)
+        msg_out[z, state.shape[0] :, :] = tail
+
+
+def enter_kernel(place, r_ref, before, decay, e_out):
+    state = jnp.zeros(before.shape[1:], F32)
+    for z in range(r_ref.shape[0]):
+        own, step = part_of(r_ref, z)
+        state = jnp.where(z < place[0], jnp.exp(step) * state + own, state)
     for b in range(e_out.shape[0]):
-        e_out[b] = carry.astype(BF16)
-        tail = r_ref[b, SUB:, :].astype(F32)
-        carry = jnp.exp(tail[0:1, :] + tail[1:2, :]) * carry + r_ref[b, :SUB, :].astype(F32)
+        e_out[b] = (before[b] + jnp.exp(decay[b : b + 1, :]) * state).astype(BF16)
 
 
 def gate_kernel(near, order, f_ref, *refs):
@@ -298,7 +319,8 @@
     width = proj_x.shape[1]
     state = proj_bc.shape[1] // 2
     n_x = lax.axis_size("x")
-    bands = lax.axis_size(LAT)
+    n_z, n_y = lax.axis_size("z"), lax.axis_size("y")
+    bands = n_z * n_y
     f = fields.reshape(rows, depth)
     sds = jax.ShapeDtypeStruct
 
@@ -308,16 +330,11 @@
     order = each % n_x * 2 + (c_at + each // n_x) % 2
     late = jnp.array([0, 1, 3, 2, 4, 6, 5, 7])
     order2 = (x_at - late + 2 * n_x) % n_x * 2 + (c_at + late // n_x) % 2
-    first, second, tail, f = call(
+    first, tail = call(
         pack_kernel,
-        (
-            sds((n_x, k + 2 * k * LANES // width, width), BF16),
-            sds((2 * k, width), BF16),
-            sds((HALO, depth), BF16),
-            sds((rows, depth), BF16),
-        ),
-        [proj_x, proj_bc, proj_dt.T, proj_z, proj_out, f],
-        hbm=6,
+        (sds((n_x, k + 2 * k * LANES // width, width), BF16), sds((HALO, depth), BF16)),
+        [proj_x, proj_bc, proj_dt.T, f],
+        hbm=4,
         scratch=[
             pltpu.VMEM(proj_x.shape, BF16),
             pltpu.VMEM(proj_bc.shape, BF16),
@@ -330,11 +347,20 @@
 
     w1a = lax.all_to_all(first, "x", 0, 0)
     halo = lax.ppermute(tail, LAT, [(i, i + 1) for i in range(bands - 1)])
+    small = [conv_x, conv_bc, dt_bias[None], log_rate[None]]
+    src, second, f, *small = call(
+        source_kernel,
+        [sds((HALO + rows, depth), BF16), sds((2 * k, width), BF16), sds((rows, depth), BF16)]
+        + [sds(a.shape, F32) for a in small],
+        [order, halo, proj_z, proj_out, f, *small],
+        smem=1,
+        hbm=7,
+        flops=10**6,
+    )
     w2a, w2b = [second], [across(second)]
-    src = call(
-        source_kernel, sds((HALO + rows, depth), BF16), [order, f, halo], smem=1, flops=10**6
-    )
-    w1a, src, second, order2 = lax.optimization_barrier((w1a, src, second, order2))
+    w1a, src, second, order2, w2b[0] = lax.optimization_barrier(
+        (w1a, src, second, order2, w2b[0])
+    )
     w1b = across(w1a)
     for d in range(1, n_x):
         w2a.append(lax.ppermute(second, "x", [(i, (i + d) % n_x) for i in range(n_x)]))
@@ -348,26 +374,40 @@
             sds((rows, 2 * state), BF16),
             sds((rows, heads), F32),
             sds((rows, heads), F32),
-            sds((bands, 2 * SUB, LANES), BF16),
+            sds((n_y, width // heads + SUB, LANES), BF16),
         ),
-        [src, w1a, w1b, conv_x, conv_bc, dt_bias[None], log_rate[None]],
-        hbm=4,
-        scratch=[pltpu.VMEM((HALO + rows, width + 2 * state), F32)]
-        + [pltpu.VMEM(a.shape, F32) for a in (conv_x, conv_bc, dt_bias[None], log_rate[None])],
+        [src, w1a, w1b, *small],
+        scratch=[pltpu.VMEM((HALO + rows, width + 2 * state), F32)],
         flops=2 * rows * depth * (width + 2 * LANES),
     )
-    got = lax.all_to_all(msg, LAT, 0, 0)
+    got = lax.all_to_all(msg, "y", 0, 0)
     y = call(
         within_kernel,
         sds((rows, width), F32),
         [x_act, bc_act, step, cum],
         flops=2 * rows * rows * width * 2,
     )
+    per = width // heads
+    before, decay, msg = call(
+        row_kernel,
+        (
+            sds((n_y, per, LANES), F32),
+            sds((n_y, LANES), F32),
+            sds((n_z, per + SUB, LANES), BF16),
+        ),
+        [got],
+        flops=10**6,
+    )
+    got = lax.all_to_all(msg, "z", 0, 0)
     entering = call(
-        bands_kernel, sds((bands, SUB, LANES), BF16), [got], flops=bands * SUB * LANES * 100
-    )
-    incoming = lax.all_to_all(entering, LAT, 0, 0)
-    incoming = incoming.reshape(bands * SUB, LANES)
+        enter_kernel,
+        sds((n_y, per, LANES), BF16),
+        [lax.axis_index("z")[None], got, before, decay],
+        smem=1,
+        flops=10**6,
+    )
+    incoming = lax.all_to_all(entering, "y", 0, 0)
+    incoming = incoming.reshape(width // 2, LANES)
     near = []
     gate, w_out = call(
         functools.partial(gate_kernel, len(near)),

time: 93.5 us -> 99.5 us (1.064)
  the two profiles are of different devices: /device:TPU:1 before, /device:TPU:8 now
where the time goes in v3:
time: 99.5 us; the launch traced here: 98.8 us
  starting transfers between devices  52.8 us (53%)
  waiting for transfers between devices  29.4 us (30%)
  Pallas kernels  14.6 us (15%)
  local copies, waits for them, and re-layouts  1.79 us (2%)
    pallas_call x8, Pallas kernels, call(): pl.pallas_call(body, out_shape=outs, in_specs=specs, out_specs=jax.tree.m...  14.6 us
    all_to_all x1, starting transfers between devices, local(): got = lax.all_to_all(msg, 'z', 0, 0)  10.3 us
    ppermute x5, starting transfers between devices, across(): return lax.ppermute(block, 'c', [(0, 1), (1, 0)])  10.1 us
    all_to_all x1, waiting for transfers between devices, local(): got = lax.all_to_all(msg, 'z', 0, 0)  9.63 us
    ppermute x3, starting transfers between devices, local(): lax.ppermute(second, 'x', [(i, (i + d) % n_x) for i in range(n_x)])  9.53 us
    ppermute x3, waiting for transfers between devices, local(): lax.ppermute(second, 'x', [(i, (i + d) % n_x) for i in range(n_x)])  7.59 us
    all_to_all x1, starting transfers between devices, local(): incoming = lax.all_to_all(entering, 'y', 0, 0)  7.55 us
    all_to_all x1, starting transfers between devices, local(): got = lax.all_to_all(msg, 'y', 0, 0)  7.54 us
  transfers between devices with their start and end apart: 13, of which 6 were waited for; matrix products, arithmetic and copies ran while one was open for 0% of the time, Pallas kernels for 10%

profile of v3, /device:TPU:8, one launch (start us, length us, event | category | flops | bytes accessed | tf_op | source)
XLA Modules:
  0.0 98.8 jit_solution(1021977597510083685)
XLA Ops:
  0.0 2.2 %shard_map.118 = (bf16[4,160,1024]{2,1,0:T(8,128)(2,1)}, bf16[16,1024]{1,0:T(8,128)(2,1)S(1)}) custom-call(bf16[128,1024]{1,0:T(8,128)(2,1)} %x_ref.1, bf16[128,128]{1,0:T(8,128)(2,1)} %bc_ref.1, bf16[16,128]{1,0:T(8,128)(2,1)} %bitcast.12, bf16[128,1024]{1,0:T(8,128)(2,1)} %bitcast.10), custom_call_target="tpu_custom_call" | custom-call | bytes 561152 | tf_op jit(solution)/shard_map/pallas_call | solution.py:303
  2.2 0.0 copy-start.5
  2.2 0.0 copy-start.6
  2.2 4.3 %all-to-all-start = ((bf16[4,160,1024]{2,1,0:T(8,128)(2,1)}), bf16[4,160,1024]{2,1,0:T(8,128)(2,1)S(1)}, u32[]{:S(2)}, u32[]{:S(2)}) async-start(bf16[4,160,1024]{2,1,0:T(8,128)(2,1)} %get-tuple-element.29), calls=%async_computation | async-start | bytes 2621440 | tf_op jit(solution)/shard_map/all_to_all | solution.py:348
  6.6 3.5 %collective-permute-start = (bf16[16,1024]{1,0:T(8,128)(2,1)S(1)}, bf16[16,1024]{1,0:T(8,128)(2,1)S(1)}, u32[]{:S(2)}, u32[]{:S(2)}) collective-permute-start(bf16[16,1024]{1,0:T(8,128)(2,1)S(1)} %get-tuple-element.30), channel_id=1, source_target_pairs={{0,8},{8,16},{16,24},{24,32},{32,40},{40,48},{48,56},{56,64},{64,7... | collective-permute-start | bytes 98312 | tf_op jit(solution)/shard_map/ppermute | solution.py:349
  10.1 4.7 %collective-permute-done.halo_ref = bf16[16,1024]{1,0:T(8,128)(2,1)S(1)} collective-permute-done((bf16[16,1024]{1,0:T(8,128)(2,1)S(1)}, bf16[16,1024]{1,0:T(8,128)(2,1)S(1)}, u32[]{:S(2)}, u32[]{:S(2)}) %collective-permute-start) | collective-permute-done | bytes 32800 | tf_op jit(solution)/shard_map/ppermute | solution.py:349
  14.8 2.6 %shard_map.119 = (bf16[144,1024]{1,0:T(8,128)(2,1)S(1)}, bf16[256,1024]{1,0:T(8,128)(2,1)}, bf16[128,1024]{1,0:T(8,128)(2,1)S(1)}, f32[4,1024]{1,0:T(4,128)S(1)}...) custom-call(s32[8]{0:T(128)S(1)} %fusion.order, ...), custom_call_target="tpu_custom_call" | custom-call | flops 1000000 | bytes 837792 | tf_op jit(solution)/shard_map/pallas_call | solution.py:303
  17.4 1.9 %collective-permute-start.1 = (bf16[256,1024]{1,0:T(8,128)(2,1)}, bf16[256,1024]{1,0:T(8,128)(2,1)S(1)}, u32[]{:S(2)}, u32[]{:S(2)}) collective-permute-start(bf16[256,1024]{1,0:T(8,128)(2,1)} %get-tuple-element.49), channel_id=1, source_target_pairs={{0,1},{1,0},{2,3},{3,2},{4,5},{5,4},{6,7},{7,6},{8,9},{9,8},{10,11... | collective-permute-start | bytes 1572872 | tf_op jit(solution)/shard_map/ppermute | solution.py:346
  19.3 0.0 copy-done.5
  19.3 0.0 copy-done.6
  19.3 2.0 %collective-permute-done.1.refs_5_ = bf16[256,1024]{1,0:T(8,128)(2,1)S(1)} collective-permute-done((bf16[256,1024]{1,0:T(8,128)(2,1)}, bf16[256,1024]{1,0:T(8,128)(2,1)S(1)}, u32[]{:S(2)}, u32[]{:S(2)}) %collective-permute-start.1) | collective-permute-done | bytes 524320 | tf_op jit(solution)/shard_map/ppermute | solution.py:346
  21.4 0.0 copy-start.1
  21.4 3.1 %all-to-all-done.wa = bf16[4,160,1024]{2,1,0:T(8,128)(2,1)S(1)} async-done(((bf16[4,160,1024]{2,1,0:T(8,128)(2,1)}), bf16[4,160,1024]{2,1,0:T(8,128)(2,1)S(1)}, u32[]{:S(2)}, u32[]{:S(2)}) %all-to-all-start) | async-done | bytes 1310752 | tf_op jit(solution)/shard_map/all_to_all | solution.py:348
  24.5 1.9 %collective-permute-start.2 = (bf16[4,160,1024]{2,1,0:T(8,128)(2,1)S(1)}, bf16[4,160,1024]{2,1,0:T(8,128)(2,1)S(1)}, u32[]{:S(2)}, u32[]{:S(2)}) collective-permute-start(bf16[4,160,1024]{2,1,0:T(8,128)(2,1)S(1)} %all-to-all-done.wa), channel_id=1, source_target_pairs={{0,1},{1,0},{2,3},{3,2},{4,5},{5,4},{6,7},{7,6},{8,9},{9,8},{10,11... | collective-permute-start | bytes 3932168 | tf_op jit(solution)/shard_map/ppermute | solution.py:346
  26.4 2.5 %collective-permute-start.5 = (bf16[256,1024]{1,0:T(8,128)(2,1)}, bf16[256,1024]{1,0:T(8,128)(2,1)}, u32[]{:S(2)}, u32[]{:S(2)}) collective-permute-start(bf16[256,1024]{1,0:T(8,128)(2,1)} %get-tuple-element.49), channel_id=1, source_target_pairs={{0,4},{2,6},{4,0},{6,2},{1,5},{3,7},{5,1},{7,3},{8,12},{10,14},{12... | collective-permute-start | bytes 1572872 | tf_op jit(solution)/shard_map/ppermute | solution.py:366
  28.9 3.4 %collective-permute-start.3 = (bf16[256,1024]{1,0:T(8,128)(2,1)}, bf16[256,1024]{1,0:T(8,128)(2,1)}, u32[]{:S(2)}, u32[]{:S(2)}) collective-permute-start(bf16[256,1024]{1,0:T(8,128)(2,1)} %get-tuple-element.49), channel_id=1, source_target_pairs={{0,2},{2,4},{4,6},{6,0},{1,3},{3,5},{5,7},{7,1},{8,10},{10,12},{12... | collective-permute-start | bytes 1572872 | tf_op jit(solution)/shard_map/ppermute | solution.py:366
  32.2 3.7 %collective-permute-start.4 = (bf16[256,1024]{1,0:T(8,128)(2,1)}, bf16[256,1024]{1,0:T(8,128)(2,1)}, u32[]{:S(2)}, u32[]{:S(2)}) collective-permute-start(bf16[256,1024]{1,0:T(8,128)(2,1)} %get-tuple-element.49), channel_id=1, source_target_pairs={{0,6},{2,0},{4,2},{6,4},{1,7},{3,1},{5,3},{7,5},{8,14},{10,8},{12,... | collective-permute-start | bytes 1572872 | tf_op jit(solution)/shard_map/ppermute | solution.py:366
  35.9 0.0 collective-permute-done.2.wb
  35.9 0.0 copy-done.1
  35.9 2.7 %shard_map.120 = (bf16[128,1024]{1,0:T(8,128)(2,1)S(1)}, bf16[128,128]{1,0:T(8,128)(2,1)S(1)}, f32[128,16]{1,0:T(8,128)S(1)}, f32[128,16]{1,0:T(8,128)S(1)}, bf16[8,72,128]{2,1,0:T(8,128)(2,1)}) custom-call(bf16[144,1024]{1,0:T(8,128)(2,1)S(1)} %get-tuple-element.34.src_ref, bf16[4,160,1024]{2,1,0:T(8,128)(2,1)S(1)} %all-to-all-done.wa, ...), custom_call_target="tpu_custom_call" | custom-call | flops 335544320 | bytes 2934912 | tf_op jit(solution)/shard_map/pallas_call | solution.py:303
  38.6 7.5 %all-to-all-start.1 = ((bf16[8,72,128]{2,1,0:T(8,128)(2,1)}), bf16[8,72,128]{2,1,0:T(8,128)(2,1)S(1)}, u32[]{:S(2)}, u32[]{:S(2)}) async-start(bf16[8,72,128]{2,1,0:T(8,128)(2,1)} %get-tuple-element.44), calls=%async_computation.1 | async-start | bytes 294912 | tf_op jit(solution)/shard_map/all_to_all | solution.py:383
  46.1 0.0 collective-permute-done.5.refs_4_
  46.2 1.9 %collective-permute-start.6 = (bf16[256,1024]{1,0:T(8,128)(2,1)}, bf16[256,1024]{1,0:T(8,128)(2,1)S(1)}, u32[]{:S(2)}, u32[]{:S(2)}) collective-permute-start(bf16[256,1024]{1,0:T(8,128)(2,1)} %collective-permute-done.5.refs_4_), channel_id=1, source_target_pairs={{0,1},{1,0},{2,3},{3,2},{4,5},{5,4},{6,7},{7,6},{8,9},{9,8},{10,11... | collective-permute-start | bytes 1572872 | tf_op jit(solution)/shard_map/ppermute | solution.py:346
  48.1 7.6 %collective-permute-done.3.refs_2_ = bf16[256,1024]{1,0:T(8,128)(2,1)} collective-permute-done((bf16[256,1024]{1,0:T(8,128)(2,1)}, bf16[256,1024]{1,0:T(8,128)(2,1)}, u32[]{:S(2)}, u32[]{:S(2)}) %collective-permute-start.3) | collective-permute-done | bytes 524320 | tf_op jit(solution)/shard_map/ppermute | solution.py:366
  55.7 1.9 %collective-permute-start.7 = (bf16[256,1024]{1,0:T(8,128)(2,1)}, bf16[256,1024]{1,0:T(8,128)(2,1)S(1)}, u32[]{:S(2)}, u32[]{:S(2)}) collective-permute-start(bf16[256,1024]{1,0:T(8,128)(2,1)} %collective-permute-done.3.refs_2_), channel_id=1, source_target_pairs={{0,1},{1,0},{2,3},{3,2},{4,5},{5,4},{6,7},{7,6},{8,9},{9,8},{10,11... | collective-permute-start | bytes 1572872 | tf_op jit(solution)/shard_map/ppermute | solution.py:346
  57.6 0.0 collective-permute-done.4.refs_3_
  57.6 2.4 %collective-permute-start.8 = (bf16[256,1024]{1,0:T(8,128)(2,1)}, bf16[256,1024]{1,0:T(8,128)(2,1)S(1)}, u32[]{:S(2)}, u32[]{:S(2)}) collective-permute-start(bf16[256,1024]{1,0:T(8,128)(2,1)} %collective-permute-done.4.refs_3_), channel_id=1, source_target_pairs={{0,1},{1,0},{2,3},{3,2},{4,5},{5,4},{6,7},{7,6},{8,9},{9,8},{10,11... | collective-permute-start | bytes 1572872 | tf_op jit(solution)/shard_map/ppermute | solution.py:346
  60.0 0.0 all-to-all-done.1.r_ref
  60.0 0.7 shard_map.122
  60.7 10.3 %all-to-all-start.2 = ((bf16[8,72,128]{2,1,0:T(8,128)(2,1)}), bf16[8,72,128]{2,1,0:T(8,128)(2,1)S(1)}, u32[]{:S(2)}, u32[]{:S(2)}) async-start(bf16[8,72,128]{2,1,0:T(8,128)(2,1)} %get-tuple-element.45), calls=%async_computation.2 | async-start | bytes 294912 | tf_op jit(solution)/shard_map/all_to_all | solution.py:401
  71.0 9.6 %all-to-all-done.2.r_ref = bf16[8,72,128]{2,1,0:T(8,128)(2,1)S(1)} async-done(((bf16[8,72,128]{2,1,0:T(8,128)(2,1)}), bf16[8,72,128]{2,1,0:T(8,128)(2,1)S(1)}, u32[]{:S(2)}, u32[]{:S(2)}) %all-to-all-start.2) | async-done | bytes 147488 | tf_op jit(solution)/shard_map/all_to_all | solution.py:401
  80.7 0.7 shard_map.123
  81.4 7.5 %all-to-all-start.3 = ((bf16[8,64,128]{2,1,0:T(8,128)(2,1)}), bf16[8,64,128]{2,1,0:T(8,128)(2,1)S(1)}, u32[]{:S(2)}, u32[]{:S(2)}) async-start(bf16[8,64,128]{2,1,0:T(8,128)(2,1)} %shard_map.123), calls=%async_computation.3 | async-start | bytes 262144 | tf_op jit(solution)/shard_map/all_to_all | solution.py:409
  88.9 0.0 collective-permute-done.6.refs_6_
  88.9 0.0 copy-start.2
  88.9 0.0 collective-permute-done.7.refs_7_
  89.0 0.0 copy-start.3
  89.0 0.0 collective-permute-done.8.refs_8_
  89.0 0.8 copy-done.2
  89.7 0.2 copy-done.3
  89.9 0.0 copy-start.4
  89.9 0.8 copy-done.4
  90.7 0.0 copy-start
  90.7 2.8 %shard_map.124 = (bf16[128,1024]{1,0:T(8,128)(2,1)S(1)}, bf16[1024,1024]{1,0:T(8,128)(2,1)S(1)}) custom-call(s32[8]{0:T(128)S(1)} %fusion.1.order, bf16[128,1024]{1,0:T(8,128)(2,1)S(1)} %get-tuple-element.48.f_ref, bf16[128,1024]{1,0:T(8,128)(2,1)} %refs_0_.3, bf16[128,1024]{1,0:T(8,128)(2,1)} %refs_1_.3, bf16[256,1024]{1,0:T(8,128)(2,1)} %collective-permute-done.3.refs_2_, ...), custom_call_target="tpu_custom_call" | custom-call | flops 268435456 | bytes 4456480 | tf_op jit(solution)/shard_map/pallas_call | solution.py:303
  93.6 0.6 shard_map.121.y_ref
  94.2 2.3 %all-to-all-done.3 = bf16[8,64,128]{2,1,0:T(8,128)(2,1)S(1)} async-done(((bf16[8,64,128]{2,1,0:T(8,128)(2,1)}), bf16[8,64,128]{2,1,0:T(8,128)(2,1)S(1)}, u32[]{:S(2)}, u32[]{:S(2)}) %all-to-all-start.3) | async-done | bytes 131104 | tf_op jit(solution)/shard_map/all_to_all | solution.py:409
  96.6 0.0 copy-done
  96.6 2.2 %shard_map.125 = bf16[128,1024]{1,0:T(8,128)(2,1)} custom-call(s32[8]{0:T(128)S(1)} %fusion.1.order, f32[128,1024]{1,0:T(8,128)S(1)} %shard_map.121.y_ref, bf16[512,128]{1,0:T(8,128)(2,1)S(1)} %bitcast.8, bf16[128,128]{1,0:T(8,128)(2,1)S(1)} %get-tuple-element.41.bc_ref, f32[128,16]{1,0:T(8,128)S(1)} %get-tuple-element.43.cum_ref, ...), custom_call_target="tpu_custom_call" | custom-call | flops 268435456 | bytes 3059744 | tf_op jit(solution)/shard_map/pallas_call | solution.py:303
  (2 shorter events, 0.0 us)
Async XLA Ops:
  2.2 17.1 %copy-start.5 = (s32[8]{0:T(128)S(1)}, s32[8]{0:T(128)}, u32[]{:S(2)}) copy-start(s32[8]{0:T(128)} %constant.94) | copy-start | bytes 100
  2.2 17.1 %copy-start.6 = (s32[8]{0:T(128)S(1)}, s32[8]{0:T(128)}, u32[]{:S(2)}) copy-start(s32[8]{0:T(128)} %constant.80) | copy-start | bytes 100
  2.2 22.2 %all-to-all-start = ((bf16[4,160,1024]{2,1,0:T(8,128)(2,1)}), bf16[4,160,1024]{2,1,0:T(8,128)(2,1)S(1)}, u32[]{:S(2)}, u32[]{:S(2)}) async-start(bf16[4,160,1024]{2,1,0:T(8,128)(2,1)} %get-tuple-element.29), calls=%async_computation | async-start | bytes 2621440 | tf_op jit(solution)/shard_map/all_to_all | solution.py:348
  6.6 8.2 %collective-permute-start = (bf16[16,1024]{1,0:T(8,128)(2,1)S(1)}, bf16[16,1024]{1,0:T(8,128)(2,1)S(1)}, u32[]{:S(2)}, u32[]{:S(2)}) collective-permute-start(bf16[16,1024]{1,0:T(8,128)(2,1)S(1)} %get-tuple-element.30), channel_id=1, source_target_pairs={{0,8},{8,16},{16,24},{24,32},{32,40},{40,48},{48,56},{56,64},{64,7... | collective-permute-start | bytes 98312 | tf_op jit(solution)/shard_map/ppermute | solution.py:349
  17.4 4.0 %collective-permute-start.1 = (bf16[256,1024]{1,0:T(8,128)(2,1)}, bf16[256,1024]{1,0:T(8,128)(2,1)S(1)}, u32[]{:S(2)}, u32[]{:S(2)}) collective-permute-start(bf16[256,1024]{1,0:T(8,128)(2,1)} %get-tuple-element.49), channel_id=1, source_target_pairs={{0,1},{1,0},{2,3},{3,2},{4,5},{5,4},{6,7},{7,6},{8,9},{9,8},{10,11... | collective-permute-start | bytes 1572872 | tf_op jit(solution)/shard_map/ppermute | solution.py:346
  21.4 14.6 %copy-start.1 = (bf16[256,1024]{1,0:T(8,128)(2,1)}, bf16[256,1024]{1,0:T(8,128)(2,1)S(1)}, u32[]{:S(2)}) copy-start(bf16[256,1024]{1,0:T(8,128)(2,1)S(1)} %collective-permute-done.1.refs_5_) | copy-start | bytes 1572868
  24.5 11.5 %collective-permute-start.2 = (bf16[4,160,1024]{2,1,0:T(8,128)(2,1)S(1)}, bf16[4,160,1024]{2,1,0:T(8,128)(2,1)S(1)}, u32[]{:S(2)}, u32[]{:S(2)}) collective-permute-start(bf16[4,160,1024]{2,1,0:T(8,128)(2,1)S(1)} %all-to-all-done.wa), channel_id=1, source_target_pairs={{0,1},{1,0},{2,3},{3,2},{4,5},{5,4},{6,7},{7,6},{8,9},{9,8},{10,11... | collective-permute-start | bytes 3932168 | tf_op jit(solution)/shard_map/ppermute | solution.py:346
  26.4 19.8 %collective-permute-start.5 = (bf16[256,1024]{1,0:T(8,128)(2,1)}, bf16[256,1024]{1,0:T(8,128)(2,1)}, u32[]{:S(2)}, u32[]{:S(2)}) collective-permute-start(bf16[256,1024]{1,0:T(8,128)(2,1)} %get-tuple-element.49), channel_id=1, source_target_pairs={{0,4},{2,6},{4,0},{6,2},{1,5},{3,7},{5,1},{7,3},{8,12},{10,14},{12... | collective-permute-start | bytes 1572872 | tf_op jit(solution)/shard_map/ppermute | solution.py:366
  28.9 26.8 %collective-permute-start.3 = (bf16[256,1024]{1,0:T(8,128)(2,1)}, bf16[256,1024]{1,0:T(8,128)(2,1)}, u32[]{:S(2)}, u32[]{:S(2)}) collective-permute-start(bf16[256,1024]{1,0:T(8,128)(2,1)} %get-tuple-element.49), channel_id=1, source_target_pairs={{0,2},{2,4},{4,6},{6,0},{1,3},{3,5},{5,7},{7,1},{8,10},{10,12},{12... | collective-permute-start | bytes 1572872 | tf_op jit(solution)/shard_map/ppermute | solution.py:366
  32.2 25.4 %collective-permute-start.4 = (bf16[256,1024]{1,0:T(8,128)(2,1)}, bf16[256,1024]{1,0:T(8,128)(2,1)}, u32[]{:S(2)}, u32[]{:S(2)}) collective-permute-start(bf16[256,1024]{1,0:T(8,128)(2,1)} %get-tuple-element.49), channel_id=1, source_target_pairs={{0,6},{2,0},{4,2},{6,4},{1,7},{3,1},{5,3},{7,5},{8,14},{10,8},{12,... | collective-permute-start | bytes 1572872 | tf_op jit(solution)/shard_map/ppermute | solution.py:366
  38.6 21.4 %all-to-all-start.1 = ((bf16[8,72,128]{2,1,0:T(8,128)(2,1)}), bf16[8,72,128]{2,1,0:T(8,128)(2,1)S(1)}, u32[]{:S(2)}, u32[]{:S(2)}) async-start(bf16[8,72,128]{2,1,0:T(8,128)(2,1)} %get-tuple-element.44), calls=%async_computation.1 | async-start | bytes 294912 | tf_op jit(solution)/shard_map/all_to_all | solution.py:383
  46.2 42.8 %collective-permute-start.6 = (bf16[256,1024]{1,0:T(8,128)(2,1)}, bf16[256,1024]{1,0:T(8,128)(2,1)S(1)}, u32[]{:S(2)}, u32[]{:S(2)}) collective-permute-start(bf16[256,1024]{1,0:T(8,128)(2,1)} %collective-permute-done.5.refs_4_), channel_id=1, source_target_pairs={{0,1},{1,0},{2,3},{3,2},{4,5},{5,4},{6,7},{7,6},{8,9},{9,8},{10,11... | collective-permute-start | bytes 1572872 | tf_op jit(solution)/shard_map/ppermute | solution.py:346
  55.7 33.3 %collective-permute-start.7 = (bf16[256,1024]{1,0:T(8,128)(2,1)}, bf16[256,1024]{1,0:T(8,128)(2,1)S(1)}, u32[]{:S(2)}, u32[]{:S(2)}) collective-permute-start(bf16[256,1024]{1,0:T(8,128)(2,1)} %collective-permute-done.3.refs_2_), channel_id=1, source_target_pairs={{0,1},{1,0},{2,3},{3,2},{4,5},{5,4},{6,7},{7,6},{8,9},{9,8},{10,11... | collective-permute-start | bytes 1572872 | tf_op jit(solution)/shard_map/ppermute | solution.py:346
  57.6 31.4 %collective-permute-start.8 = (bf16[256,1024]{1,0:T(8,128)(2,1)}, bf16[256,1024]{1,0:T(8,128)(2,1)S(1)}, u32[]{:S(2)}, u32[]{:S(2)}) collective-permute-start(bf16[256,1024]{1,0:T(8,128)(2,1)} %collective-permute-done.4.refs_3_), channel_id=1, source_target_pairs={{0,1},{1,0},{2,3},{3,2},{4,5},{5,4},{6,7},{7,6},{8,9},{9,8},{10,11... | collective-permute-start | bytes 1572872 | tf_op jit(solution)/shard_map/ppermute | solution.py:346
  60.7 19.9 %all-to-all-start.2 = ((bf16[8,72,128]{2,1,0:T(8,128)(2,1)}), bf16[8,72,128]{2,1,0:T(8,128)(2,1)S(1)}, u32[]{:S(2)}, u32[]{:S(2)}) async-start(bf16[8,72,128]{2,1,0:T(8,128)(2,1)} %get-tuple-element.45), calls=%async_computation.2 | async-start | bytes 294912 | tf_op jit(solution)/shard_map/all_to_all | solution.py:401
  81.4 15.2 %all-to-all-start.3 = ((bf16[8,64,128]{2,1,0:T(8,128)(2,1)}), bf16[8,64,128]{2,1,0:T(8,128)(2,1)S(1)}, u32[]{:S(2)}, u32[]{:S(2)}) async-start(bf16[8,64,128]{2,1,0:T(8,128)(2,1)} %shard_map.123), calls=%async_computation.3 | async-start | bytes 262144 | tf_op jit(solution)/shard_map/all_to_all | solution.py:409
  88.9 0.8 copy-start.2
  89.0 1.0 copy-start.3
  89.9 0.8 copy-start.4
  90.7 5.8 %copy-start = (f32[1024]{0:T(1024)S(1)}, f32[1024]{0:T(1024)}, u32[]{:S(2)}) copy-start(f32[1024]{0:T(1024)} %param.21) | copy-start | bytes 12292

commit v4 on v3

--- a/solution.py
+++ b/solution.py
@@ -1,5 +1,3 @@
-import functools
-
 import jax
 import jax.numpy as jnp
 from jax import lax
@@ -18,6 +16,7 @@
 LANES = 128
 SUB = 8
 TILE = 256
+HELD = type(pltpu.HBM((8, 128), jnp.bfloat16))
 
 
 def dot(a, b, **kw):
@@ -212,6 +211,13 @@
         y_out[:, pair * LANES : (pair + 1) * LANES] = dot(jnp.concatenate(w, 1), both)
 
 
+def stack_kernel(*refs):
+    parts, (out, sems) = refs[:-2], refs[-2:]
+    size = parts[0].shape[0]
+    for c in fetch([(r, out.at[pl.ds(i * size, size)]) for i, r in enumerate(parts)], sems):
+        c.wait()
+
+
 def row_kernel(r_ref, before, decay, msg_out):
     state = jnp.zeros(before.shape[1:], F32)
     total = jnp.zeros((1, LANES), F32)
@@ -237,29 +243,24 @@
         e_out[b] = (before[b] + jnp.exp(decay[b : b + 1, :]) * state).astype(BF16)
 
 
-def gate_kernel(near, order, f_ref, *refs):
-    (out, w_out, w, sems) = refs[-4:]
-    near_refs, (z_ref, o_ref), far_refs = refs[:near], refs[near : near + 2], refs[near + 2 : -4]
-    k = z_ref.shape[0]
-    n = len(far_refs) + 1 + near
-    at = [pl.ds(i * k, k) for i in range(n)]
+def gate_kernel(order, f_ref, z_ref, o_ref, mine, other, others, out, w_out, w, sems):
+    k, width = z_ref.shape
+    n = w.shape[0] // k
+    shards = [(z_ref, o_ref)]
+    for ref in (mine, other, others):
+        for i in range(0, ref.shape[0], 2 * k):
+            shards.append((ref.at[pl.ds(i, k)], ref.at[pl.ds(i + k, k)]))
     copies = fetch(
-        [(z_ref, w.at[at[0]])]
-        + [(r.at[:k], w.at[at[i]]) for i, r in enumerate(far_refs, 1)]
-        + [(o_ref, w_out.at[at[0]])]
-        + [(r.at[k:], w_out.at[at[i]]) for i, r in enumerate(far_refs, 1)],
+        [(s[0], w.at[pl.ds(i * k, k)]) for i, s in enumerate(shards)]
+        + [(s[1], w_out.at[pl.ds(i * k, k)]) for i, s in enumerate(shards)],
         sems,
     )
-    for i, r in enumerate(near_refs, n - near):
-        w_out[i * k : (i + 1) * k, :] = r[k:, :]
     src = ordered(f_ref, order, n)
-    for c in copies[: n - near]:
+    for c in copies[:n]:
         c.wait()
-    for j in range(0, out.shape[1], TILE):
-        cut = slice(j, j + TILE)
-        tile = jnp.concatenate([w[: (n - near) * k, cut]] + [r[:k, cut] for r in near_refs], 0)
-        out[:, cut] = dot(src, tile).astype(BF16)
-    for c in copies[n - near :]:
+    for at in range(0, width, TILE):
+        out[:, at : at + TILE] = dot(src, w[:, at : at + TILE]).astype(BF16)
+    for c in copies[n:]:
         c.wait()
 
 
@@ -298,13 +299,16 @@
         pltpu.with_memory_space_constraint(a, pltpu.MemorySpace.HBM) if i >= len(args) - hbm else a
         for i, a in enumerate(args)
     ]
-    scratch = list(scratch) + ([pltpu.SemaphoreType.DMA((2 * hbm,))] if hbm else [])
+    scratch = list(scratch) + ([pltpu.SemaphoreType.DMA((16,))] if hbm else [])
     nbytes = sum(a.size * a.dtype.itemsize for a in args)
     return pl.pallas_call(
         body,
         out_shape=outs,
         in_specs=specs,
-        out_specs=jax.tree.map(lambda _: vmem, outs),
+        out_specs=jax.tree.map(
+            lambda o: pl.BlockSpec(memory_space=pltpu.MemorySpace.HBM) if isinstance(o, HELD) else vmem,
+            outs,
+        ),
         scratch_shapes=scratch,
         compiler_params=pltpu.CompilerParams(vmem_limit_bytes=16 * 2**20),
         cost_estimate=pl.CostEstimate(flops=flops, bytes_accessed=nbytes, transcendentals=0),
@@ -328,8 +332,7 @@
     x_at, c_at = lax.axis_index("x"), lax.axis_index("c")
     each = jnp.arange(2 * n_x)
     order = each % n_x * 2 + (c_at + each // n_x) % 2
-    late = jnp.array([0, 1, 3, 2, 4, 6, 5, 7])
-    order2 = (x_at - late + 2 * n_x) % n_x * 2 + (c_at + late // n_x) % 2
+    order2 = (x_at - each + 2 * n_x) % n_x * 2 + (c_at + each // n_x) % 2
     first, tail = call(
         pack_kernel,
         (sds((n_x, k + 2 * k * LANES // width, width), BF16), sds((HALO, depth), BF16)),
@@ -364,8 +367,15 @@
     w1b = across(w1a)
     for d in range(1, n_x):
         w2a.append(lax.ppermute(second, "x", [(i, (i + d) % n_x) for i in range(n_x)]))
-    for d in range(1, n_x):
-        w2b.append(across(w2a[d]))
+    size = (n_x - 1) * 2 * k
+    mine = call(
+        stack_kernel,
+        pltpu.HBM((size, width), BF16),
+        w2a[1:],
+        scratch=[pltpu.SemaphoreType.DMA((n_x - 1,))],
+        flops=10**6,
+    )
+    others = across(mine)
 
     x_act, bc_act, step, cum, msg = call(
         project_kernel,
@@ -408,13 +418,12 @@
     )
     incoming = lax.all_to_all(entering, "y", 0, 0)
     incoming = incoming.reshape(width // 2, LANES)
-    near = []
     gate, w_out = call(
-        functools.partial(gate_kernel, len(near)),
+        gate_kernel,
         (sds((rows, width), BF16), sds((width, depth), BF16)),
-        [order2, f, *near, proj_z, proj_out, w2a[1], w2a[3], w2a[2], w2b[0], w2b[2], w2b[1], w2b[3]],
+        [order2, f, proj_z, proj_out, mine, w2b[0], others],
         smem=1,
-        hbm=9,
+        hbm=5,
         scratch=[pltpu.VMEM((depth, width), BF16)],
         flops=2 * rows * depth * width,
     )

time: 99.5 us -> 112 us (1.13)
  blocking collectives: 0 us -> 15.9 us
  starting transfers between devices: 52.8 us -> 37 us
  waiting for transfers between devices: 29.4 us -> 43.7 us
  local copies, waits for them, and re-layouts: 1.79 us -> 0.01 us
    all_to_all x0 -> x1, blocking collectives: none -> 15.9 us  [local(): got = lax.all_to_all(msg, 'y', 0, 0)]
    ppermute x3, waiting for transfers between devices: 7.59 us -> 19.6 us  [local(): lax.ppermute(second, 'x', [(i, (i + d) % n_x) for i in range(n_x)])]
    all_to_all x1 -> x0, starting transfers between devices: 7.54 us -> none  [local(): got = lax.all_to_all(msg, 'y', 0, 0)]
    ppermute x5 -> x3, starting transfers between devices: 10.1 us -> 5.77 us  [across(): return lax.ppermute(block, 'c', [(0, 1), (1, 0)])]
    all_to_all x1, starting transfers between devices: 7.55 us -> 4.77 us  [local(): incoming = lax.all_to_all(entering, 'y', 0, 0)]
    all_to_all x1, waiting for transfers between devices: 2.35 us -> 4.17 us  [local(): incoming = lax.all_to_all(entering, 'y', 0, 0)]
    unnamed x14 -> x4, local copies, waits for them, and re-layouts: 1.79 us -> 0.01 us
    ppermute x3, starting transfers between devices: 9.53 us -> 8.36 us  [local(): lax.ppermute(second, 'x', [(i, (i + d) % n_x) for i in range(n_x)])]
  transfers between devices with their start and end apart: 13 -> 10, of which waited for: 6 -> 8; matrix products, arithmetic and copies ran while one was open for 0% -> 0% of each run, Pallas kernels for 10% -> 9%
where the time goes in v4:
time: 112 us; the launch traced here: 111 us
  waiting for transfers between devices  43.7 us (39%)
  starting transfers between devices  37 us (33%)
  blocking collectives  15.9 us (14%)
  Pallas kernels  14.3 us (13%)
    ppermute x3, waiting for transfers between devices, local(): lax.ppermute(second, 'x', [(i, (i + d) % n_x) for i in range(n_x)])  19.6 us
    all_to_all x1, blocking collectives, local(): got = lax.all_to_all(msg, 'y', 0, 0)  15.9 us
    pallas_call x9, Pallas kernels, call(): pl.pallas_call(body, out_shape=outs, in_specs=specs, out_specs=jax.tree.m...  14.3 us
    all_to_all x1, starting transfers between devices, local(): got = lax.all_to_all(msg, 'z', 0, 0)  10.3 us
    all_to_all x1, waiting for transfers between devices, local(): got = lax.all_to_all(msg, 'z', 0, 0)  9.25 us
    ppermute x3, starting transfers between devices, local(): lax.ppermute(second, 'x', [(i, (i + d) % n_x) for i in range(n_x)])  8.36 us
    ppermute x3, starting transfers between devices, across(): return lax.ppermute(block, 'c', [(0, 1), (1, 0)])  5.77 us
    all_to_all x1, starting transfers between devices, local(): incoming = lax.all_to_all(entering, 'y', 0, 0)  4.77 us
  transfers between devices with their start and end apart: 10, of which 8 were waited for; matrix products, arithmetic and copies ran while one was open for 0% of the time, Pallas kernels for 9%

profile of v4, /device:TPU:8, one launch (start us, length us, event | category | flops | bytes accessed | tf_op | source)
XLA Modules:
  0.0 111.2 jit_solution(2324736595464398397)
XLA Ops:
  0.0 2.3 %shard_map.109 = (bf16[4,160,1024]{2,1,0:T(8,128)(2,1)}, bf16[16,1024]{1,0:T(8,128)(2,1)S(1)}) custom-call(bf16[128,1024]{1,0:T(8,128)(2,1)} %x_ref.1, bf16[128,128]{1,0:T(8,128)(2,1)} %bc_ref.1, bf16[16,128]{1,0:T(8,128)(2,1)} %bitcast.12, bf16[128,1024]{1,0:T(8,128)(2,1)} %bitcast.10), custom_call_target="tpu_custom_call" | custom-call | bytes 561152 | tf_op jit(solution)/shard_map/pallas_call | solution.py:304
  2.3 4.3 %all-to-all-start = ((bf16[4,160,1024]{2,1,0:T(8,128)(2,1)}), bf16[4,160,1024]{2,1,0:T(8,128)(2,1)S(1)}, u32[]{:S(2)}, u32[]{:S(2)}) async-start(bf16[4,160,1024]{2,1,0:T(8,128)(2,1)} %get-tuple-element.29), calls=%async_computation | async-start | bytes 2621440 | tf_op jit(solution)/shard_map/all_to_all | solution.py:351
  6.6 3.5 %collective-permute-start = (bf16[16,1024]{1,0:T(8,128)(2,1)S(1)}, bf16[16,1024]{1,0:T(8,128)(2,1)S(1)}, u32[]{:S(2)}, u32[]{:S(2)}) collective-permute-start(bf16[16,1024]{1,0:T(8,128)(2,1)S(1)} %get-tuple-element.30), channel_id=1, source_target_pairs={{0,8},{8,16},{16,24},{24,32},{32,40},{40,48},{48,56},{56,64},{64,7... | collective-permute-start | bytes 98312 | tf_op jit(solution)/shard_map/ppermute | solution.py:352
  10.1 4.7 %collective-permute-done.halo_ref = bf16[16,1024]{1,0:T(8,128)(2,1)S(1)} collective-permute-done((bf16[16,1024]{1,0:T(8,128)(2,1)S(1)}, bf16[16,1024]{1,0:T(8,128)(2,1)S(1)}, u32[]{:S(2)}, u32[]{:S(2)}) %collective-permute-start) | collective-permute-done | bytes 32800 | tf_op jit(solution)/shard_map/ppermute | solution.py:352
  14.8 1.8 %shard_map.110 = (bf16[144,1024]{1,0:T(8,128)(2,1)S(1)}, bf16[256,1024]{1,0:T(8,128)(2,1)S(1)}, bf16[128,1024]{1,0:T(8,128)(2,1)S(1)}, f32[4,1024]{1,0:T(4,128)S...) custom-call(s32[8]{0:T(128)S(1)} %fusion.1.order, ...), custom_call_target="tpu_custom_call" | custom-call | flops 1000000 | bytes 837792 | tf_op jit(solution)/shard_map/pallas_call | solution.py:304
  16.6 1.9 %collective-permute-start.1 = (bf16[256,1024]{1,0:T(8,128)(2,1)S(1)}, bf16[256,1024]{1,0:T(8,128)(2,1)S(1)}, u32[]{:S(2)}, u32[]{:S(2)}) collective-permute-start(bf16[256,1024]{1,0:T(8,128)(2,1)S(1)} %get-tuple-element.49), channel_id=1, source_target_pairs={{0,1},{1,0},{2,3},{3,2},{4,5},{5,4},{6,7},{7,6},{8,9},{9,8},{10,11... | collective-permute-start | bytes 1572872 | tf_op jit(solution)/shard_map/ppermute | solution.py:349
  18.6 1.9 %collective-permute-done.1.other = bf16[256,1024]{1,0:T(8,128)(2,1)S(1)} collective-permute-done((bf16[256,1024]{1,0:T(8,128)(2,1)S(1)}, bf16[256,1024]{1,0:T(8,128)(2,1)S(1)}, u32[]{:S(2)}, u32[]{:S(2)}) %collective-permute-start.1) | collective-permute-done | bytes 524320 | tf_op jit(solution)/shard_map/ppermute | solution.py:349
  20.4 0.0 copy-start.1
  20.4 4.1 %all-to-all-done.wa = bf16[4,160,1024]{2,1,0:T(8,128)(2,1)S(1)} async-done(((bf16[4,160,1024]{2,1,0:T(8,128)(2,1)}), bf16[4,160,1024]{2,1,0:T(8,128)(2,1)S(1)}, u32[]{:S(2)}, u32[]{:S(2)}) %all-to-all-start) | async-done | bytes 1310752 | tf_op jit(solution)/shard_map/all_to_all | solution.py:351
  24.5 3.1 %collective-permute-start.5 = (bf16[256,1024]{1,0:T(8,128)(2,1)S(1)}, bf16[256,1024]{1,0:T(8,128)(2,1)S(1)}, u32[]{:S(2)}, u32[]{:S(2)}) collective-permute-start(bf16[256,1024]{1,0:T(8,128)(2,1)S(1)} %get-tuple-element.49), channel_id=1, source_target_pairs={{0,6},{2,0},{4,2},{6,4},{1,7},{3,1},{5,3},{7,5},{8,14},{10,8},{12,... | collective-permute-start | bytes 1572872 | tf_op jit(solution)/shard_map/ppermute | solution.py:369
  27.6 3.4 %collective-permute-start.4 = (bf16[256,1024]{1,0:T(8,128)(2,1)S(1)}, bf16[256,1024]{1,0:T(8,128)(2,1)S(1)}, u32[]{:S(2)}, u32[]{:S(2)}) collective-permute-start(bf16[256,1024]{1,0:T(8,128)(2,1)S(1)} %get-tuple-element.49), channel_id=1, source_target_pairs={{0,4},{2,6},{4,0},{6,2},{1,5},{3,7},{5,1},{7,3},{8,12},{10,14},{12... | collective-permute-start | bytes 1572872 | tf_op jit(solution)/shard_map/ppermute | solution.py:369
  30.9 1.9 %collective-permute-start.3 = (bf16[256,1024]{1,0:T(8,128)(2,1)S(1)}, bf16[256,1024]{1,0:T(8,128)(2,1)S(1)}, u32[]{:S(2)}, u32[]{:S(2)}) collective-permute-start(bf16[256,1024]{1,0:T(8,128)(2,1)S(1)} %get-tuple-element.49), channel_id=1, source_target_pairs={{0,2},{2,4},{4,6},{6,0},{1,3},{3,5},{5,7},{7,1},{8,10},{10,12},{12... | collective-permute-start | bytes 1572872 | tf_op jit(solution)/shard_map/ppermute | solution.py:369
  32.9 1.9 %collective-permute-start.2 = (bf16[4,160,1024]{2,1,0:T(8,128)(2,1)S(1)}, bf16[4,160,1024]{2,1,0:T(8,128)(2,1)S(1)}, u32[]{:S(2)}, u32[]{:S(2)}) collective-permute-start(bf16[4,160,1024]{2,1,0:T(8,128)(2,1)S(1)} %all-to-all-done.wa), channel_id=1, source_target_pairs={{0,1},{1,0},{2,3},{3,2},{4,5},{5,4},{6,7},{7,6},{8,9},{9,8},{10,11... | collective-permute-start | bytes 3932168 | tf_op jit(solution)/shard_map/ppermute | solution.py:349
  34.8 6.4 %collective-permute-done.5.refs_2_ = bf16[256,1024]{1,0:T(8,128)(2,1)S(1)} collective-permute-done((bf16[256,1024]{1,0:T(8,128)(2,1)S(1)}, bf16[256,1024]{1,0:T(8,128)(2,1)S(1)}, u32[]{:S(2)}, u32[]{:S(2)}) %collective-permute-start.5) | collective-permute-done | bytes 524320 | tf_op jit(solution)/shard_map/ppermute | solution.py:369
  41.2 4.6 %collective-permute-done.4.refs_1_ = bf16[256,1024]{1,0:T(8,128)(2,1)S(1)} collective-permute-done((bf16[256,1024]{1,0:T(8,128)(2,1)S(1)}, bf16[256,1024]{1,0:T(8,128)(2,1)S(1)}, u32[]{:S(2)}, u32[]{:S(2)}) %collective-permute-start.4) | collective-permute-done | bytes 524320 | tf_op jit(solution)/shard_map/ppermute | solution.py:369
  45.8 8.6 %collective-permute-done.3.refs_0_ = bf16[256,1024]{1,0:T(8,128)(2,1)S(1)} collective-permute-done((bf16[256,1024]{1,0:T(8,128)(2,1)S(1)}, bf16[256,1024]{1,0:T(8,128)(2,1)S(1)}, u32[]{:S(2)}, u32[]{:S(2)}) %collective-permute-start.3) | collective-permute-done | bytes 524320 | tf_op jit(solution)/shard_map/ppermute | solution.py:369
  54.5 1.2 %shard_map.115.mine = bf16[768,1024]{1,0:T(8,128)(2,1)} custom-call(bf16[256,1024]{1,0:T(8,128)(2,1)S(1)} %collective-permute-done.3.refs_0_, bf16[256,1024]{1,0:T(8,128)(2,1)S(1)} %collective-permute-done.4.refs_1_, bf16[256,1024]{1,0:T(8,128)(2,1)S(1)} %collective-permute-done.5.refs_2_), custom_call_target="tpu_custom_call" | custom-call | flops 1000000 | bytes 1572864 | tf_op jit(solution)/shard_map/pallas_call | solution.py:304
  55.7 0.0 copy-done.1
  55.7 1.9 %collective-permute-start.6 = (bf16[768,1024]{1,0:T(8,128)(2,1)}, bf16[768,1024]{1,0:T(8,128)(2,1)}, u32[]{:S(2)}, u32[]{:S(2)}) collective-permute-start(bf16[768,1024]{1,0:T(8,128)(2,1)} %shard_map.115.mine), channel_id=1, source_target_pairs={{0,1},{1,0},{2,3},{3,2},{4,5},{5,4},{6,7},{7,6},{8,9},{9,8},{10,11... | collective-permute-start | bytes 4718600 | tf_op jit(solution)/shard_map/ppermute | solution.py:349
  57.6 0.0 collective-permute-done.2.wb
  57.6 2.0 %shard_map.111 = (bf16[128,1024]{1,0:T(8,128)(2,1)S(1)}, bf16[128,128]{1,0:T(8,128)(2,1)S(1)}, f32[128,16]{1,0:T(8,128)S(1)}, f32[128,16]{1,0:T(8,128)S(1)}, bf16[8,72,128]{2,1,0:T(8,128)(2,1)S(1)}) custom-call(bf16[144,1024]{1,0:T(8,128)(2,1)S(1)} %get-tuple-element.34.src_ref, bf16[4,160,1024]{2,1,0:T(8,128)(2,1)S(1)} %all-to-all-done.wa, ...), custom_call_target="tpu_custom_call" | custom-call | flops 335544320 | bytes 2934912 | tf_op jit(solution)/shard_map/pallas_call | solution.py:304
  59.6 15.9 %all_to_all.20.r_ref = bf16[8,72,128]{2,1,0:T(8,128)(2,1)S(1)} all-to-all(bf16[8,72,128]{2,1,0:T(8,128)(2,1)S(1)} %get-tuple-element.44), channel_id=1, replica_groups=mesh['z'=8,'y'=8,'x'=4,'c'=2] {'y'}, dimensions={0} | all-to-all | bytes 294912 | tf_op jit(solution)/shard_map/all_to_all | solution.py:393
  75.6 0.7 shard_map.113
  76.3 10.3 %all-to-all-start.2 = ((bf16[8,72,128]{2,1,0:T(8,128)(2,1)}), bf16[8,72,128]{2,1,0:T(8,128)(2,1)S(1)}, u32[]{:S(2)}, u32[]{:S(2)}) async-start(bf16[8,72,128]{2,1,0:T(8,128)(2,1)} %get-tuple-element.45), calls=%async_computation.2 | async-start | bytes 294912 | tf_op jit(solution)/shard_map/all_to_all | solution.py:411
  86.6 9.3 %all-to-all-done.2.r_ref = bf16[8,72,128]{2,1,0:T(8,128)(2,1)S(1)} async-done(((bf16[8,72,128]{2,1,0:T(8,128)(2,1)}), bf16[8,72,128]{2,1,0:T(8,128)(2,1)S(1)}, u32[]{:S(2)}, u32[]{:S(2)}) %all-to-all-start.2) | async-done | bytes 147488 | tf_op jit(solution)/shard_map/all_to_all | solution.py:411
  95.8 0.7 shard_map.114
  96.6 4.8 %all-to-all-start.3 = ((bf16[8,64,128]{2,1,0:T(8,128)(2,1)}), bf16[8,64,128]{2,1,0:T(8,128)(2,1)S(1)}, u32[]{:S(2)}, u32[]{:S(2)}) async-start(bf16[8,64,128]{2,1,0:T(8,128)(2,1)} %shard_map.114), calls=%async_computation.3 | async-start | bytes 262144 | tf_op jit(solution)/shard_map/all_to_all | solution.py:419
  101.3 0.6 shard_map.112.y_ref
  102.0 0.0 collective-permute-done.6.others
  102.0 0.0 copy-start
  102.0 2.8 %shard_map.116 = (bf16[128,1024]{1,0:T(8,128)(2,1)S(1)}, bf16[1024,1024]{1,0:T(8,128)(2,1)S(1)}) custom-call(s32[8]{0:T(128)S(1)} %fusion.4.order, bf16[128,1024]{1,0:T(8,128)(2,1)S(1)} %get-tuple-element.48.f_ref, bf16[128,1024]{1,0:T(8,128)(2,1)} %z_ref.1, bf16[128,1024]{1,0:T(8,128)(2,1)} %o_ref.1, bf16[768,1024]{1,0:T(8,128)(2,1)} %shard_map.115.mine, ...), custom_call_target="tpu_custom_call" | custom-call | flops 268435456 | bytes 4456480 | tf_op jit(solution)/shard_map/pallas_call | solution.py:304
  104.8 4.2 %all-to-all-done.3 = bf16[8,64,128]{2,1,0:T(8,128)(2,1)S(1)} async-done(((bf16[8,64,128]{2,1,0:T(8,128)(2,1)}), bf16[8,64,128]{2,1,0:T(8,128)(2,1)S(1)}, u32[]{:S(2)}, u32[]{:S(2)}) %all-to-all-start.3) | async-done | bytes 131104 | tf_op jit(solution)/shard_map/all_to_all | solution.py:419
  109.0 0.0 copy-done
  109.0 2.2 %shard_map.117 = bf16[128,1024]{1,0:T(8,128)(2,1)} custom-call(s32[8]{0:T(128)S(1)} %fusion.4.order, f32[128,1024]{1,0:T(8,128)S(1)} %shard_map.112.y_ref, bf16[512,128]{1,0:T(8,128)(2,1)S(1)} %bitcast.8, bf16[128,128]{1,0:T(8,128)(2,1)S(1)} %get-tuple-element.41.bc_ref, f32[128,16]{1,0:T(8,128)S(1)} %get-tuple-element.43.cum_ref, ...), custom_call_target="tpu_custom_call" | custom-call | flops 268435456 | bytes 3059744 | tf_op jit(solution)/shard_map/pallas_call | solution.py:304
  (2 shorter events, 0.0 us)
Async XLA Ops:
  2.3 22.2 %all-to-all-start = ((bf16[4,160,1024]{2,1,0:T(8,128)(2,1)}), bf16[4,160,1024]{2,1,0:T(8,128)(2,1)S(1)}, u32[]{:S(2)}, u32[]{:S(2)}) async-start(bf16[4,160,1024]{2,1,0:T(8,128)(2,1)} %get-tuple-element.29), calls=%async_computation | async-start | bytes 2621440 | tf_op jit(solution)/shard_map/all_to_all | solution.py:351
  6.6 8.2 %collective-permute-start = (bf16[16,1024]{1,0:T(8,128)(2,1)S(1)}, bf16[16,1024]{1,0:T(8,128)(2,1)S(1)}, u32[]{:S(2)}, u32[]{:S(2)}) collective-permute-start(bf16[16,1024]{1,0:T(8,128)(2,1)S(1)} %get-tuple-element.30), channel_id=1, source_target_pairs={{0,8},{8,16},{16,24},{24,32},{32,40},{40,48},{48,56},{56,64},{64,7... | collective-permute-start | bytes 98312 | tf_op jit(solution)/shard_map/ppermute | solution.py:352
  16.6 3.8 %collective-permute-start.1 = (bf16[256,1024]{1,0:T(8,128)(2,1)S(1)}, bf16[256,1024]{1,0:T(8,128)(2,1)S(1)}, u32[]{:S(2)}, u32[]{:S(2)}) collective-permute-start(bf16[256,1024]{1,0:T(8,128)(2,1)S(1)} %get-tuple-element.49), channel_id=1, source_target_pairs={{0,1},{1,0},{2,3},{3,2},{4,5},{5,4},{6,7},{7,6},{8,9},{9,8},{10,11... | collective-permute-start | bytes 1572872 | tf_op jit(solution)/shard_map/ppermute | solution.py:349
  20.4 35.2 %copy-start.1 = (bf16[256,1024]{1,0:T(8,128)(2,1)}, bf16[256,1024]{1,0:T(8,128)(2,1)S(1)}, u32[]{:S(2)}) copy-start(bf16[256,1024]{1,0:T(8,128)(2,1)S(1)} %collective-permute-done.1.other) | copy-start | bytes 1572868
  24.5 16.7 %collective-permute-start.5 = (bf16[256,1024]{1,0:T(8,128)(2,1)S(1)}, bf16[256,1024]{1,0:T(8,128)(2,1)S(1)}, u32[]{:S(2)}, u32[]{:S(2)}) collective-permute-start(bf16[256,1024]{1,0:T(8,128)(2,1)S(1)} %get-tuple-element.49), channel_id=1, source_target_pairs={{0,6},{2,0},{4,2},{6,4},{1,7},{3,1},{5,3},{7,5},{8,14},{10,8},{12,... | collective-permute-start | bytes 1572872 | tf_op jit(solution)/shard_map/ppermute | solution.py:369
  27.6 18.2 %collective-permute-start.4 = (bf16[256,1024]{1,0:T(8,128)(2,1)S(1)}, bf16[256,1024]{1,0:T(8,128)(2,1)S(1)}, u32[]{:S(2)}, u32[]{:S(2)}) collective-permute-start(bf16[256,1024]{1,0:T(8,128)(2,1)S(1)} %get-tuple-element.49), channel_id=1, source_target_pairs={{0,4},{2,6},{4,0},{6,2},{1,5},{3,7},{5,1},{7,3},{8,12},{10,14},{12... | collective-permute-start | bytes 1572872 | tf_op jit(solution)/shard_map/ppermute | solution.py:369
  30.9 23.5 %collective-permute-start.3 = (bf16[256,1024]{1,0:T(8,128)(2,1)S(1)}, bf16[256,1024]{1,0:T(8,128)(2,1)S(1)}, u32[]{:S(2)}, u32[]{:S(2)}) collective-permute-start(bf16[256,1024]{1,0:T(8,128)(2,1)S(1)} %get-tuple-element.49), channel_id=1, source_target_pairs={{0,2},{2,4},{4,6},{6,0},{1,3},{3,5},{5,7},{7,1},{8,10},{10,12},{12... | collective-permute-start | bytes 1572872 | tf_op jit(solution)/shard_map/ppermute | solution.py:369
  32.9 24.7 %collective-permute-start.2 = (bf16[4,160,1024]{2,1,0:T(8,128)(2,1)S(1)}, bf16[4,160,1024]{2,1,0:T(8,128)(2,1)S(1)}, u32[]{:S(2)}, u32[]{:S(2)}) collective-permute-start(bf16[4,160,1024]{2,1,0:T(8,128)(2,1)S(1)} %all-to-all-done.wa), channel_id=1, source_target_pairs={{0,1},{1,0},{2,3},{3,2},{4,5},{5,4},{6,7},{7,6},{8,9},{9,8},{10,11... | collective-permute-start | bytes 3932168 | tf_op jit(solution)/shard_map/ppermute | solution.py:349
  55.7 46.3 %collective-permute-start.6 = (bf16[768,1024]{1,0:T(8,128)(2,1)}, bf16[768,1024]{1,0:T(8,128)(2,1)}, u32[]{:S(2)}, u32[]{:S(2)}) collective-permute-start(bf16[768,1024]{1,0:T(8,128)(2,1)} %shard_map.115.mine), channel_id=1, source_target_pairs={{0,1},{1,0},{2,3},{3,2},{4,5},{5,4},{6,7},{7,6},{8,9},{9,8},{10,11... | collective-permute-start | bytes 4718600 | tf_op jit(solution)/shard_map/ppermute | solution.py:349
  76.3 19.6 %all-to-all-start.2 = ((bf16[8,72,128]{2,1,0:T(8,128)(2,1)}), bf16[8,72,128]{2,1,0:T(8,128)(2,1)S(1)}, u32[]{:S(2)}, u32[]{:S(2)}) async-start(bf16[8,72,128]{2,1,0:T(8,128)(2,1)} %get-tuple-element.45), calls=%async_computation.2 | async-start | bytes 294912 | tf_op jit(solution)/shard_map/all_to_all | solution.py:411
  96.6 12.4 %all-to-all-start.3 = ((bf16[8,64,128]{2,1,0:T(8,128)(2,1)}), bf16[8,64,128]{2,1,0:T(8,128)(2,1)S(1)}, u32[]{:S(2)}, u32[]{:S(2)}) async-start(bf16[8,64,128]{2,1,0:T(8,128)(2,1)} %shard_map.114), calls=%async_computation.3 | async-start | bytes 262144 | tf_op jit(solution)/shard_map/all_to_all | solution.py:419
  102.0 7.0 %copy-start = (f32[1024]{0:T(1024)S(1)}, f32[1024]{0:T(1024)}, u32[]{:S(2)}) copy-start(f32[1024]{0:T(1024)} %param.20) | copy-start | bytes 12292

commit v5 on v4

--- a/solution.py
+++ b/solution.py
@@ -92,8 +92,8 @@
 def source_kernel(order, halo_ref, *refs):
     z_ref, o_ref, f_ref = refs[:3]
     small_refs = refs[3:7]
-    out, second, fields = refs[7:10]
-    small, sems = refs[10:14], refs[14]
+    out, second = refs[7:9]
+    small, fields, sems = refs[9:13], refs[13], refs[14]
     k = z_ref.shape[0]
     copies = fetch(
         [(f_ref, fields), (z_ref, second.at[:k]), (o_ref, second.at[k:])]
@@ -148,8 +148,8 @@
     log_step = -jnp.exp(rate[...]) * step
     lower = (iota((rows, rows), 0) >= iota((rows, rows), 1)).astype(F32)
     cum = dot(lower, log_step, precision=HIGHEST)
-    dt_out[...] = step
-    cum_out[...] = cum
+    dt_out[...] = step.T
+    cum_out[...] = cum.T
     last = cum[rows - 1 : rows, :]
     weight = spread(jnp.exp(last - cum) * step, width)
 
@@ -192,13 +192,13 @@
 
 def within_kernel(x_ref, bc_ref, dt_ref, cum_ref, y_out):
     rows, _ = x_ref.shape
-    heads = dt_ref.shape[1]
+    heads = dt_ref.shape[0]
     state = bc_ref.shape[1] // 2
     scores = dot_nt(bc_ref[:, state:], bc_ref[:, :state])
     causal = iota((rows, rows), 0) >= iota((rows, rows), 1)
-    cum = cum_ref[...]
-    cum_t = cum.T
-    dt_t = dt_ref[...].T
+    cum_t = cum_ref[...]
+    cum = cum_t.T
+    dt_t = dt_ref[...]
     left = iota((rows, LANES), 1) < LANES // 2
     for pair in range(heads // 2):
         w = []
@@ -243,7 +243,7 @@
         e_out[b] = (before[b] + jnp.exp(decay[b : b + 1, :]) * state).astype(BF16)
 
 
-def gate_kernel(order, f_ref, z_ref, o_ref, mine, other, others, out, w_out, w, sems):
+def gate_kernel(order, f_ref, z_ref, o_ref, mine, other, others, out, w_out, w, fields, sems):
     k, width = z_ref.shape
     n = w.shape[0] // k
     shards = [(z_ref, o_ref)]
@@ -251,16 +251,17 @@
         for i in range(0, ref.shape[0], 2 * k):
             shards.append((ref.at[pl.ds(i, k)], ref.at[pl.ds(i + k, k)]))
     copies = fetch(
-        [(s[0], w.at[pl.ds(i * k, k)]) for i, s in enumerate(shards)]
+        [(f_ref, fields)]
+        + [(s[0], w.at[pl.ds(i * k, k)]) for i, s in enumerate(shards)]
         + [(s[1], w_out.at[pl.ds(i * k, k)]) for i, s in enumerate(shards)],
         sems,
     )
-    src = ordered(f_ref, order, n)
-    for c in copies[:n]:
+    for c in copies[: n + 1]:
         c.wait()
+    src = ordered(fields, order, n)
     for at in range(0, width, TILE):
         out[:, at : at + TILE] = dot(src, w[:, at : at + TILE]).astype(BF16)
-    for c in copies[n:]:
+    for c in copies[n + 1 :]:
         c.wait()
 
 
@@ -271,7 +272,7 @@
     left = iota((rows, LANES), 1) < LANES // 2
     c1 = jnp.where(left, 0.0, bc)
     c = (pltpu.roll(c1, LANES // 2, 1).astype(BF16), c1.astype(BF16))
-    grown = spread(jnp.exp(cum_ref[...]), width)
+    grown = spread(jnp.exp(cum_ref[...]).T, width)
     square = jnp.zeros((rows, 1), F32)
     parts = []
     for at in range(0, width, TILE):
@@ -299,7 +300,7 @@
         pltpu.with_memory_space_constraint(a, pltpu.MemorySpace.HBM) if i >= len(args) - hbm else a
         for i, a in enumerate(args)
     ]
-    scratch = list(scratch) + ([pltpu.SemaphoreType.DMA((16,))] if hbm else [])
+    scratch = list(scratch) + ([pltpu.SemaphoreType.DMA((24,))] if hbm else [])
     nbytes = sum(a.size * a.dtype.itemsize for a in args)
     return pl.pallas_call(
         body,
@@ -351,13 +352,14 @@
     w1a = lax.all_to_all(first, "x", 0, 0)
     halo = lax.ppermute(tail, LAT, [(i, i + 1) for i in range(bands - 1)])
     small = [conv_x, conv_bc, dt_bias[None], log_rate[None]]
-    src, second, f, *small = call(
+    src, second, *small = call(
         source_kernel,
-        [sds((HALO + rows, depth), BF16), sds((2 * k, width), BF16), sds((rows, depth), BF16)]
+        [sds((HALO + rows, depth), BF16), sds((2 * k, width), BF16)]
         + [sds(a.shape, F32) for a in small],
         [order, halo, proj_z, proj_out, f, *small],
         smem=1,
         hbm=7,
+        scratch=[pltpu.VMEM((rows, depth), BF16)],
         flops=10**6,
     )
     w2a, w2b = [second], [across(second)]
@@ -382,8 +384,8 @@
         (
             sds((rows, width), BF16),
             sds((rows, 2 * state), BF16),
-            sds((rows, heads), F32),
-            sds((rows, heads), F32),
+            sds((heads, rows), F32),
+            sds((heads, rows), F32),
             sds((n_y, width // heads + SUB, LANES), BF16),
         ),
         [src, w1a, w1b, *small],
@@ -423,8 +425,8 @@
         (sds((rows, width), BF16), sds((width, depth), BF16)),
         [order2, f, proj_z, proj_out, mine, w2b[0], others],
         smem=1,
-        hbm=5,
-        scratch=[pltpu.VMEM((depth, width), BF16)],
+        hbm=6,
+        scratch=[pltpu.VMEM((depth, width), BF16), pltpu.VMEM((rows, depth), BF16)],
         flops=2 * rows * depth * width,
     )
     out = call(

time: 112 us -> 112 us (level)
  no operation moved by 1% of the time
where the time goes in v5:
time: 112 us; the launch traced here: 111 us
  waiting for transfers between devices  43.4 us (39%)
  starting transfers between devices  37 us (33%)
  blocking collectives  15.9 us (14%)
  Pallas kernels  14.8 us (13%)
    ppermute x3, waiting for transfers between devices, local(): lax.ppermute(second, 'x', [(i, (i + d) % n_x) for i in range(n_x)])  19.6 us
    all_to_all x1, blocking collectives, local(): got = lax.all_to_all(msg, 'y', 0, 0)  15.9 us
    pallas_call x9, Pallas kernels, call(): pl.pallas_call(body, out_shape=outs, in_specs=specs, out_specs=jax.tree.m...  14.8 us
    all_to_all x1, starting transfers between devices, local(): got = lax.all_to_all(msg, 'z', 0, 0)  10.3 us
    all_to_all x1, waiting for transfers between devices, local(): got = lax.all_to_all(msg, 'z', 0, 0)  9.25 us
    ppermute x3, starting transfers between devices, local(): lax.ppermute(second, 'x', [(i, (i + d) % n_x) for i in range(n_x)])  8.36 us
    ppermute x3, starting transfers between devices, across(): return lax.ppermute(block, 'c', [(0, 1), (1, 0)])  5.77 us
    all_to_all x1, starting transfers between devices, local(): incoming = lax.all_to_all(entering, 'y', 0, 0)  4.77 us
  transfers between devices with their start and end apart: 10, of which 8 were waited for; matrix products, arithmetic and copies ran while one was open for 0% of the time, Pallas kernels for 9%

profile of v5, /device:TPU:8, one launch (start us, length us, event | category | flops | bytes accessed | tf_op | source)
XLA Modules:
  0.0 111.3 jit_solution(2695938020430947839)
XLA Ops:
  0.0 2.4 %shard_map.109 = (bf16[4,160,1024]{2,1,0:T(8,128)(2,1)}, bf16[16,1024]{1,0:T(8,128)(2,1)S(1)}) custom-call(bf16[128,1024]{1,0:T(8,128)(2,1)} %x_ref.1, bf16[128,128]{1,0:T(8,128)(2,1)} %bc_ref.1, bf16[16,128]{1,0:T(8,128)(2,1)} %bitcast.13, bf16[128,1024]{1,0:T(8,128)(2,1)} %bitcast.10), custom_call_target="tpu_custom_call" | custom-call | bytes 561152 | tf_op jit(solution)/shard_map/pallas_call | solution.py:305
  2.4 4.3 %all-to-all-start = ((bf16[4,160,1024]{2,1,0:T(8,128)(2,1)}), bf16[4,160,1024]{2,1,0:T(8,128)(2,1)S(1)}, u32[]{:S(2)}, u32[]{:S(2)}) async-start(bf16[4,160,1024]{2,1,0:T(8,128)(2,1)} %get-tuple-element.28), calls=%async_computation | async-start | bytes 2621440 | tf_op jit(solution)/shard_map/all_to_all | solution.py:352
  6.7 3.5 %collective-permute-start = (bf16[16,1024]{1,0:T(8,128)(2,1)S(1)}, bf16[16,1024]{1,0:T(8,128)(2,1)S(1)}, u32[]{:S(2)}, u32[]{:S(2)}) collective-permute-start(bf16[16,1024]{1,0:T(8,128)(2,1)S(1)} %get-tuple-element.29), channel_id=1, source_target_pairs={{0,8},{8,16},{16,24},{24,32},{32,40},{40,48},{48,56},{56,64},{64,7... | collective-permute-start | bytes 98312 | tf_op jit(solution)/shard_map/ppermute | solution.py:353
  10.2 4.7 %collective-permute-done.halo_ref = bf16[16,1024]{1,0:T(8,128)(2,1)S(1)} collective-permute-done((bf16[16,1024]{1,0:T(8,128)(2,1)S(1)}, bf16[16,1024]{1,0:T(8,128)(2,1)S(1)}, u32[]{:S(2)}, u32[]{:S(2)}) %collective-permute-start) | collective-permute-done | bytes 32800 | tf_op jit(solution)/shard_map/ppermute | solution.py:353
  14.9 1.9 %shard_map.110 = (bf16[144,1024]{1,0:T(8,128)(2,1)S(1)}, bf16[256,1024]{1,0:T(8,128)(2,1)S(1)}, f32[4,1024]{1,0:T(4,128)S(1)}, f32[4,128]{1,0:T(4,128)S(1)}, f32[1,16]{1,0:T(1,128)S(1)}, /*index=5*/f32[1,16]{1,0:T(1,128)S(1)}) custom-call(s32[8]{0:T(128)S(1)} %fusion.1.order, bf16[16,1024]{1,0:T(8,128)(2,1)S(1)} %collective-permute-done.halo_ref, ...), custom_call_target="tpu_custom_call" | custom-call | flops 1000000 | bytes 837792 | tf_op jit(solution)/shard_map/pallas_call | solution.py:305
  16.8 1.9 %collective-permute-start.1 = (bf16[256,1024]{1,0:T(8,128)(2,1)S(1)}, bf16[256,1024]{1,0:T(8,128)(2,1)S(1)}, u32[]{:S(2)}, u32[]{:S(2)}) collective-permute-start(bf16[256,1024]{1,0:T(8,128)(2,1)S(1)} %get-tuple-element.47), channel_id=1, source_target_pairs={{0,1},{1,0},{2,3},{3,2},{4,5},{5,4},{6,7},{7,6},{8,9},{9,8},{10,11... | collective-permute-start | bytes 1572872 | tf_op jit(solution)/shard_map/ppermute | solution.py:350
  18.7 1.9 %collective-permute-done.1.other = bf16[256,1024]{1,0:T(8,128)(2,1)S(1)} collective-permute-done((bf16[256,1024]{1,0:T(8,128)(2,1)S(1)}, bf16[256,1024]{1,0:T(8,128)(2,1)S(1)}, u32[]{:S(2)}, u32[]{:S(2)}) %collective-permute-start.1) | collective-permute-done | bytes 524320 | tf_op jit(solution)/shard_map/ppermute | solution.py:350
  20.6 0.0 copy-start.1
  20.6 4.0 %all-to-all-done.wa = bf16[4,160,1024]{2,1,0:T(8,128)(2,1)S(1)} async-done(((bf16[4,160,1024]{2,1,0:T(8,128)(2,1)}), bf16[4,160,1024]{2,1,0:T(8,128)(2,1)S(1)}, u32[]{:S(2)}, u32[]{:S(2)}) %all-to-all-start) | async-done | bytes 1310752 | tf_op jit(solution)/shard_map/all_to_all | solution.py:352
  24.6 3.1 %collective-permute-start.5 = (bf16[256,1024]{1,0:T(8,128)(2,1)S(1)}, bf16[256,1024]{1,0:T(8,128)(2,1)S(1)}, u32[]{:S(2)}, u32[]{:S(2)}) collective-permute-start(bf16[256,1024]{1,0:T(8,128)(2,1)S(1)} %get-tuple-element.47), channel_id=1, source_target_pairs={{0,6},{2,0},{4,2},{6,4},{1,7},{3,1},{5,3},{7,5},{8,14},{10,8},{12,... | collective-permute-start | bytes 1572872 | tf_op jit(solution)/shard_map/ppermute | solution.py:371
  27.6 3.4 %collective-permute-start.4 = (bf16[256,1024]{1,0:T(8,128)(2,1)S(1)}, bf16[256,1024]{1,0:T(8,128)(2,1)S(1)}, u32[]{:S(2)}, u32[]{:S(2)}) collective-permute-start(bf16[256,1024]{1,0:T(8,128)(2,1)S(1)} %get-tuple-element.47), channel_id=1, source_target_pairs={{0,4},{2,6},{4,0},{6,2},{1,5},{3,7},{5,1},{7,3},{8,12},{10,14},{12... | collective-permute-start | bytes 1572872 | tf_op jit(solution)/shard_map/ppermute | solution.py:371
  31.0 1.9 %collective-permute-start.3 = (bf16[256,1024]{1,0:T(8,128)(2,1)S(1)}, bf16[256,1024]{1,0:T(8,128)(2,1)S(1)}, u32[]{:S(2)}, u32[]{:S(2)}) collective-permute-start(bf16[256,1024]{1,0:T(8,128)(2,1)S(1)} %get-tuple-element.47), channel_id=1, source_target_pairs={{0,2},{2,4},{4,6},{6,0},{1,3},{3,5},{5,7},{7,1},{8,10},{10,12},{12... | collective-permute-start | bytes 1572872 | tf_op jit(solution)/shard_map/ppermute | solution.py:371
  32.9 1.9 %collective-permute-start.2 = (bf16[4,160,1024]{2,1,0:T(8,128)(2,1)S(1)}, bf16[4,160,1024]{2,1,0:T(8,128)(2,1)S(1)}, u32[]{:S(2)}, u32[]{:S(2)}) collective-permute-start(bf16[4,160,1024]{2,1,0:T(8,128)(2,1)S(1)} %all-to-all-done.wa), channel_id=1, source_target_pairs={{0,1},{1,0},{2,3},{3,2},{4,5},{5,4},{6,7},{7,6},{8,9},{9,8},{10,11... | collective-permute-start | bytes 3932168 | tf_op jit(solution)/shard_map/ppermute | solution.py:350
  34.9 6.4 %collective-permute-done.5.refs_2_ = bf16[256,1024]{1,0:T(8,128)(2,1)S(1)} collective-permute-done((bf16[256,1024]{1,0:T(8,128)(2,1)S(1)}, bf16[256,1024]{1,0:T(8,128)(2,1)S(1)}, u32[]{:S(2)}, u32[]{:S(2)}) %collective-permute-start.5) | collective-permute-done | bytes 524320 | tf_op jit(solution)/shard_map/ppermute | solution.py:371
  41.2 4.6 %collective-permute-done.4.refs_1_ = bf16[256,1024]{1,0:T(8,128)(2,1)S(1)} collective-permute-done((bf16[256,1024]{1,0:T(8,128)(2,1)S(1)}, bf16[256,1024]{1,0:T(8,128)(2,1)S(1)}, u32[]{:S(2)}, u32[]{:S(2)}) %collective-permute-start.4) | collective-permute-done | bytes 524320 | tf_op jit(solution)/shard_map/ppermute | solution.py:371
  45.9 8.6 %collective-permute-done.3.refs_0_ = bf16[256,1024]{1,0:T(8,128)(2,1)S(1)} collective-permute-done((bf16[256,1024]{1,0:T(8,128)(2,1)S(1)}, bf16[256,1024]{1,0:T(8,128)(2,1)S(1)}, u32[]{:S(2)}, u32[]{:S(2)}) %collective-permute-start.3) | collective-permute-done | bytes 524320 | tf_op jit(solution)/shard_map/ppermute | solution.py:371
  54.5 1.2 %shard_map.115.mine = bf16[768,1024]{1,0:T(8,128)(2,1)} custom-call(bf16[256,1024]{1,0:T(8,128)(2,1)S(1)} %collective-permute-done.3.refs_0_, bf16[256,1024]{1,0:T(8,128)(2,1)S(1)} %collective-permute-done.4.refs_1_, bf16[256,1024]{1,0:T(8,128)(2,1)S(1)} %collective-permute-done.5.refs_2_), custom_call_target="tpu_custom_call" | custom-call | flops 1000000 | bytes 1572864 | tf_op jit(solution)/shard_map/pallas_call | solution.py:305
  55.7 0.0 copy-done.1
  55.7 1.9 %collective-permute-start.6 = (bf16[768,1024]{1,0:T(8,128)(2,1)}, bf16[768,1024]{1,0:T(8,128)(2,1)}, u32[]{:S(2)}, u32[]{:S(2)}) collective-permute-start(bf16[768,1024]{1,0:T(8,128)(2,1)} %shard_map.115.mine), channel_id=1, source_target_pairs={{0,1},{1,0},{2,3},{3,2},{4,5},{5,4},{6,7},{7,6},{8,9},{9,8},{10,11... | collective-permute-start | bytes 4718600 | tf_op jit(solution)/shard_map/ppermute | solution.py:350
  57.7 0.0 collective-permute-done.2.wb
  57.7 2.0 %shard_map.111 = (bf16[128,1024]{1,0:T(8,128)(2,1)S(1)}, bf16[128,128]{1,0:T(8,128)(2,1)S(1)}, f32[16,128]{1,0:T(8,128)S(1)}, f32[16,128]{1,0:T(8,128)S(1)}, bf16[8,72,128]{2,1,0:T(8,128)(2,1)S(1)}) custom-call(bf16[144,1024]{1,0:T(8,128)(2,1)S(1)} %get-tuple-element.33.src_ref, bf16[4,160,1024]{2,1,0:T(8,128)(2,1)S(1)} %all-to-all-done.wa, ...), custom_call_target="tpu_custom_call" | custom-call | flops 335544320 | bytes 2934912 | tf_op jit(solution)/shard_map/pallas_call | solution.py:305
  59.7 15.9 %all_to_all.20.r_ref = bf16[8,72,128]{2,1,0:T(8,128)(2,1)S(1)} all-to-all(bf16[8,72,128]{2,1,0:T(8,128)(2,1)S(1)} %get-tuple-element.43), channel_id=1, replica_groups=mesh['z'=8,'y'=8,'x'=4,'c'=2] {'y'}, dimensions={0} | all-to-all | bytes 294912 | tf_op jit(solution)/shard_map/all_to_all | solution.py:395
  75.6 0.7 shard_map.113
  76.3 10.3 %all-to-all-start.2 = ((bf16[8,72,128]{2,1,0:T(8,128)(2,1)}), bf16[8,72,128]{2,1,0:T(8,128)(2,1)S(1)}, u32[]{:S(2)}, u32[]{:S(2)}) async-start(bf16[8,72,128]{2,1,0:T(8,128)(2,1)} %get-tuple-element.44), calls=%async_computation.2 | async-start | bytes 294912 | tf_op jit(solution)/shard_map/all_to_all | solution.py:413
  86.6 9.3 %all-to-all-done.2.r_ref = bf16[8,72,128]{2,1,0:T(8,128)(2,1)S(1)} async-done(((bf16[8,72,128]{2,1,0:T(8,128)(2,1)}), bf16[8,72,128]{2,1,0:T(8,128)(2,1)S(1)}, u32[]{:S(2)}, u32[]{:S(2)}) %all-to-all-start.2) | async-done | bytes 147488 | tf_op jit(solution)/shard_map/all_to_all | solution.py:413
  95.9 0.7 shard_map.114
  96.6 4.8 %all-to-all-start.3 = ((bf16[8,64,128]{2,1,0:T(8,128)(2,1)}), bf16[8,64,128]{2,1,0:T(8,128)(2,1)S(1)}, u32[]{:S(2)}, u32[]{:S(2)}) async-start(bf16[8,64,128]{2,1,0:T(8,128)(2,1)} %shard_map.114), calls=%async_computation.3 | async-start | bytes 262144 | tf_op jit(solution)/shard_map/all_to_all | solution.py:421
  101.4 0.7 shard_map.112.y_ref
  102.1 0.0 copy-start
  102.1 0.0 collective-permute-done.6.others
  102.1 3.0 %shard_map.116 = (bf16[128,1024]{1,0:T(8,128)(2,1)S(1)}, bf16[1024,1024]{1,0:T(8,128)(2,1)S(1)}) custom-call(s32[8]{0:T(128)S(1)} %fusion.4.order, bf16[128,1024]{1,0:T(8,128)(2,1)} %bitcast.12, bf16[128,1024]{1,0:T(8,128)(2,1)} %z_ref.1, bf16[128,1024]{1,0:T(8,128)(2,1)} %o_ref.1, bf16[768,1024]{1,0:T(8,128)(2,1)} %shard_map.115.mine, ...), custom_call_target="tpu_custom_call" | custom-call | flops 268435456 | bytes 4456480 | tf_op jit(solution)/shard_map/pallas_call | solution.py:305
  105.1 4.0 %all-to-all-done.3 = bf16[8,64,128]{2,1,0:T(8,128)(2,1)S(1)} async-done(((bf16[8,64,128]{2,1,0:T(8,128)(2,1)}), bf16[8,64,128]{2,1,0:T(8,128)(2,1)S(1)}, u32[]{:S(2)}, u32[]{:S(2)}) %all-to-all-start.3) | async-done | bytes 131104 | tf_op jit(solution)/shard_map/all_to_all | solution.py:421
  109.0 0.0 copy-done
  109.0 2.3 %shard_map.117 = bf16[128,1024]{1,0:T(8,128)(2,1)} custom-call(s32[8]{0:T(128)S(1)} %fusion.4.order, f32[128,1024]{1,0:T(8,128)S(1)} %shard_map.112.y_ref, bf16[512,128]{1,0:T(8,128)(2,1)S(1)} %bitcast.8, bf16[128,128]{1,0:T(8,128)(2,1)S(1)} %get-tuple-element.40.bc_ref, f32[16,128]{1,0:T(8,128)S(1)} %get-tuple-element.42.cum_ref, ...), custom_call_target="tpu_custom_call" | custom-call | flops 268435456 | bytes 3059744 | tf_op jit(solution)/shard_map/pallas_call | solution.py:305
  (2 shorter events, 0.0 us)
Async XLA Ops:
  2.4 22.2 %all-to-all-start = ((bf16[4,160,1024]{2,1,0:T(8,128)(2,1)}), bf16[4,160,1024]{2,1,0:T(8,128)(2,1)S(1)}, u32[]{:S(2)}, u32[]{:S(2)}) async-start(bf16[4,160,1024]{2,1,0:T(8,128)(2,1)} %get-tuple-element.28), calls=%async_computation | async-start | bytes 2621440 | tf_op jit(solution)/shard_map/all_to_all | solution.py:352
  6.7 8.2 %collective-permute-start = (bf16[16,1024]{1,0:T(8,128)(2,1)S(1)}, bf16[16,1024]{1,0:T(8,128)(2,1)S(1)}, u32[]{:S(2)}, u32[]{:S(2)}) collective-permute-start(bf16[16,1024]{1,0:T(8,128)(2,1)S(1)} %get-tuple-element.29), channel_id=1, source_target_pairs={{0,8},{8,16},{16,24},{24,32},{32,40},{40,48},{48,56},{56,64},{64,7... | collective-permute-start | bytes 98312 | tf_op jit(solution)/shard_map/ppermute | solution.py:353
  16.8 3.8 %collective-permute-start.1 = (bf16[256,1024]{1,0:T(8,128)(2,1)S(1)}, bf16[256,1024]{1,0:T(8,128)(2,1)S(1)}, u32[]{:S(2)}, u32[]{:S(2)}) collective-permute-start(bf16[256,1024]{1,0:T(8,128)(2,1)S(1)} %get-tuple-element.47), channel_id=1, source_target_pairs={{0,1},{1,0},{2,3},{3,2},{4,5},{5,4},{6,7},{7,6},{8,9},{9,8},{10,11... | collective-permute-start | bytes 1572872 | tf_op jit(solution)/shard_map/ppermute | solution.py:350
  20.6 35.2 %copy-start.1 = (bf16[256,1024]{1,0:T(8,128)(2,1)}, bf16[256,1024]{1,0:T(8,128)(2,1)S(1)}, u32[]{:S(2)}) copy-start(bf16[256,1024]{1,0:T(8,128)(2,1)S(1)} %collective-permute-done.1.other) | copy-start | bytes 1572868
  24.6 16.7 %collective-permute-start.5 = (bf16[256,1024]{1,0:T(8,128)(2,1)S(1)}, bf16[256,1024]{1,0:T(8,128)(2,1)S(1)}, u32[]{:S(2)}, u32[]{:S(2)}) collective-permute-start(bf16[256,1024]{1,0:T(8,128)(2,1)S(1)} %get-tuple-element.47), channel_id=1, source_target_pairs={{0,6},{2,0},{4,2},{6,4},{1,7},{3,1},{5,3},{7,5},{8,14},{10,8},{12,... | collective-permute-start | bytes 1572872 | tf_op jit(solution)/shard_map/ppermute | solution.py:371
  27.6 18.2 %collective-permute-start.4 = (bf16[256,1024]{1,0:T(8,128)(2,1)S(1)}, bf16[256,1024]{1,0:T(8,128)(2,1)S(1)}, u32[]{:S(2)}, u32[]{:S(2)}) collective-permute-start(bf16[256,1024]{1,0:T(8,128)(2,1)S(1)} %get-tuple-element.47), channel_id=1, source_target_pairs={{0,4},{2,6},{4,0},{6,2},{1,5},{3,7},{5,1},{7,3},{8,12},{10,14},{12... | collective-permute-start | bytes 1572872 | tf_op jit(solution)/shard_map/ppermute | solution.py:371
  31.0 23.5 %collective-permute-start.3 = (bf16[256,1024]{1,0:T(8,128)(2,1)S(1)}, bf16[256,1024]{1,0:T(8,128)(2,1)S(1)}, u32[]{:S(2)}, u32[]{:S(2)}) collective-permute-start(bf16[256,1024]{1,0:T(8,128)(2,1)S(1)} %get-tuple-element.47), channel_id=1, source_target_pairs={{0,2},{2,4},{4,6},{6,0},{1,3},{3,5},{5,7},{7,1},{8,10},{10,12},{12... | collective-permute-start | bytes 1572872 | tf_op jit(solution)/shard_map/ppermute | solution.py:371
  32.9 24.7 %collective-permute-start.2 = (bf16[4,160,1024]{2,1,0:T(8,128)(2,1)S(1)}, bf16[4,160,1024]{2,1,0:T(8,128)(2,1)S(1)}, u32[]{:S(2)}, u32[]{:S(2)}) collective-permute-start(bf16[4,160,1024]{2,1,0:T(8,128)(2,1)S(1)} %all-to-all-done.wa), channel_id=1, source_target_pairs={{0,1},{1,0},{2,3},{3,2},{4,5},{5,4},{6,7},{7,6},{8,9},{9,8},{10,11... | collective-permute-start | bytes 3932168 | tf_op jit(solution)/shard_map/ppermute | solution.py:350
  55.7 46.4 %collective-permute-start.6 = (bf16[768,1024]{1,0:T(8,128)(2,1)}, bf16[768,1024]{1,0:T(8,128)(2,1)}, u32[]{:S(2)}, u32[]{:S(2)}) collective-permute-start(bf16[768,1024]{1,0:T(8,128)(2,1)} %shard_map.115.mine), channel_id=1, source_target_pairs={{0,1},{1,0},{2,3},{3,2},{4,5},{5,4},{6,7},{7,6},{8,9},{9,8},{10,11... | collective-permute-start | bytes 4718600 | tf_op jit(solution)/shard_map/ppermute | solution.py:350
  76.3 19.6 %all-to-all-start.2 = ((bf16[8,72,128]{2,1,0:T(8,128)(2,1)}), bf16[8,72,128]{2,1,0:T(8,128)(2,1)S(1)}, u32[]{:S(2)}, u32[]{:S(2)}) async-start(bf16[8,72,128]{2,1,0:T(8,128)(2,1)} %get-tuple-element.44), calls=%async_computation.2 | async-start | bytes 294912 | tf_op jit(solution)/shard_map/all_to_all | solution.py:413
  96.6 12.4 %all-to-all-start.3 = ((bf16[8,64,128]{2,1,0:T(8,128)(2,1)}), bf16[8,64,128]{2,1,0:T(8,128)(2,1)S(1)}, u32[]{:S(2)}, u32[]{:S(2)}) async-start(bf16[8,64,128]{2,1,0:T(8,128)(2,1)} %shard_map.114), calls=%async_computation.3 | async-start | bytes 262144 | tf_op jit(solution)/shard_map/all_to_all | solution.py:421
  102.1 7.0 %copy-start = (f32[1024]{0:T(1024)S(1)}, f32[1024]{0:T(1024)}, u32[]{:S(2)}) copy-start(f32[1024]{0:T(1024)} %param.20) | copy-start | bytes 12292

commit v6 on v3

--- a/solution.py
+++ b/solution.py
@@ -149,8 +149,8 @@
     log_step = -jnp.exp(rate[...]) * step
     lower = (iota((rows, rows), 0) >= iota((rows, rows), 1)).astype(F32)
     cum = dot(lower, log_step, precision=HIGHEST)
-    dt_out[...] = step
-    cum_out[...] = cum
+    dt_out[...] = step.T
+    cum_out[...] = cum.T
     last = cum[rows - 1 : rows, :]
     weight = spread(jnp.exp(last - cum) * step, width)
 
@@ -193,13 +193,13 @@
 
 def within_kernel(x_ref, bc_ref, dt_ref, cum_ref, y_out):
     rows, _ = x_ref.shape
-    heads = dt_ref.shape[1]
+    heads = dt_ref.shape[0]
     state = bc_ref.shape[1] // 2
     scores = dot_nt(bc_ref[:, state:], bc_ref[:, :state])
     causal = iota((rows, rows), 0) >= iota((rows, rows), 1)
-    cum = cum_ref[...]
-    cum_t = cum.T
-    dt_t = dt_ref[...].T
+    cum_t = cum_ref[...]
+    cum = cum_t.T
+    dt_t = dt_ref[...]
     left = iota((rows, LANES), 1) < LANES // 2
     for pair in range(heads // 2):
         w = []
@@ -270,7 +270,7 @@
     left = iota((rows, LANES), 1) < LANES // 2
     c1 = jnp.where(left, 0.0, bc)
     c = (pltpu.roll(c1, LANES // 2, 1).astype(BF16), c1.astype(BF16))
-    grown = spread(jnp.exp(cum_ref[...]), width)
+    grown = spread(jnp.exp(cum_ref[...]).T, width)
     square = jnp.zeros((rows, 1), F32)
     parts = []
     for at in range(0, width, TILE):
@@ -358,9 +358,7 @@
         flops=10**6,
     )
     w2a, w2b = [second], [across(second)]
-    w1a, src, second, order2, w2b[0] = lax.optimization_barrier(
-        (w1a, src, second, order2, w2b[0])
-    )
+    w1a, src, second, order2 = lax.optimization_barrier((w1a, src, second, order2))
     w1b = across(w1a)
     for d in range(1, n_x):
         w2a.append(lax.ppermute(second, "x", [(i, (i + d) % n_x) for i in range(n_x)]))
@@ -372,8 +370,8 @@
         (
             sds((rows, width), BF16),
             sds((rows, 2 * state), BF16),
-            sds((rows, heads), F32),
-            sds((rows, heads), F32),
+            sds((heads, rows), F32),
+            sds((heads, rows), F32),
             sds((n_y, width // heads + SUB, LANES), BF16),
         ),
         [src, w1a, w1b, *small],

time: 99.5 us -> 99.5 us (level)
    all_to_all x1, waiting for transfers between devices: 3.08 us -> 7.1 us  [local(): w1a = lax.all_to_all(first, 'x', 0, 0)]
    ppermute x3, waiting for transfers between devices: 7.59 us -> 5.17 us  [local(): lax.ppermute(second, 'x', [(i, (i + d) % n_x) for i in range(n_x)])]
    ppermute x5, waiting for transfers between devices: 2.05 us -> 0.01 us  [across(): return lax.ppermute(block, 'c', [(0, 1), (1, 0)])]
  transfers between devices with their start and end apart: 13 -> 13, of which waited for: 6 -> 5; matrix products, arithmetic and copies ran while one was open for 0% -> 0% of each run, Pallas kernels for 10% -> 10%
where the time goes in v6:
time: 99.5 us; the launch traced here: 98.8 us
  starting transfers between devices  53.3 us (54%)
  waiting for transfers between devices  29.5 us (30%)
  Pallas kernels  14.7 us (15%)
  local copies, waits for them, and re-layouts  1.1 us (1%)
    pallas_call x8, Pallas kernels, call(): pl.pallas_call(body, out_shape=outs, in_specs=specs, out_specs=jax.tree.m...  14.7 us
    ppermute x5, starting transfers between devices, across(): return lax.ppermute(block, 'c', [(0, 1), (1, 0)])  10.5 us
    all_to_all x1, starting transfers between devices, local(): got = lax.all_to_all(msg, 'z', 0, 0)  10.3 us
    all_to_all x1, waiting for transfers between devices, local(): got = lax.all_to_all(msg, 'z', 0, 0)  9.63 us
    ppermute x3, starting transfers between devices, local(): lax.ppermute(second, 'x', [(i, (i + d) % n_x) for i in range(n_x)])  9.53 us
    all_to_all x1, starting transfers between devices, local(): got = lax.all_to_all(msg, 'y', 0, 0)  7.56 us
    all_to_all x1, starting transfers between devices, local(): incoming = lax.all_to_all(entering, 'y', 0, 0)  7.55 us
    all_to_all x1, waiting for transfers between devices, local(): w1a = lax.all_to_all(first, 'x', 0, 0)  7.1 us
  transfers between devices with their start and end apart: 13, of which 5 were waited for; matrix products, arithmetic and copies ran while one was open for 0% of the time, Pallas kernels for 10%

profile of v6, /device:TPU:8, one launch (start us, length us, event | category | flops | bytes accessed | tf_op | source)
XLA Modules:
  0.0 98.8 jit_solution(16423529863167110055)
XLA Ops:
  0.0 2.2 %shard_map.118 = (bf16[4,160,1024]{2,1,0:T(8,128)(2,1)}, bf16[16,1024]{1,0:T(8,128)(2,1)S(1)}) custom-call(bf16[128,1024]{1,0:T(8,128)(2,1)} %x_ref.1, bf16[128,128]{1,0:T(8,128)(2,1)} %bc_ref.1, bf16[16,128]{1,0:T(8,128)(2,1)} %bitcast.12, bf16[128,1024]{1,0:T(8,128)(2,1)} %bitcast.10), custom_call_target="tpu_custom_call" | custom-call | bytes 561152 | tf_op jit(solution)/shard_map/pallas_call | solution.py:303
  2.2 0.0 copy-start.4
  2.2 0.0 copy-start.5
  2.2 4.3 %all-to-all-start = ((bf16[4,160,1024]{2,1,0:T(8,128)(2,1)}), bf16[4,160,1024]{2,1,0:T(8,128)(2,1)S(1)}, u32[]{:S(2)}, u32[]{:S(2)}) async-start(bf16[4,160,1024]{2,1,0:T(8,128)(2,1)} %get-tuple-element.28), calls=%async_computation | async-start | bytes 2621440 | tf_op jit(solution)/shard_map/all_to_all | solution.py:348
  6.5 3.5 %collective-permute-start = (bf16[16,1024]{1,0:T(8,128)(2,1)S(1)}, bf16[16,1024]{1,0:T(8,128)(2,1)S(1)}, u32[]{:S(2)}, u32[]{:S(2)}) collective-permute-start(bf16[16,1024]{1,0:T(8,128)(2,1)S(1)} %get-tuple-element.29), channel_id=1, source_target_pairs={{0,8},{8,16},{16,24},{24,32},{32,40},{40,48},{48,56},{56,64},{64,7... | collective-permute-start | bytes 98312 | tf_op jit(solution)/shard_map/ppermute | solution.py:349
  10.0 0.0 copy-done.4
  10.0 0.0 copy-done.5
  10.1 4.7 %collective-permute-done.halo_ref = bf16[16,1024]{1,0:T(8,128)(2,1)S(1)} collective-permute-done((bf16[16,1024]{1,0:T(8,128)(2,1)S(1)}, bf16[16,1024]{1,0:T(8,128)(2,1)S(1)}, u32[]{:S(2)}, u32[]{:S(2)}) %collective-permute-start) | collective-permute-done | bytes 32800 | tf_op jit(solution)/shard_map/ppermute | solution.py:349
  14.7 2.6 %shard_map.119 = (bf16[144,1024]{1,0:T(8,128)(2,1)S(1)}, bf16[256,1024]{1,0:T(8,128)(2,1)}, bf16[128,1024]{1,0:T(8,128)(2,1)S(1)}, f32[4,1024]{1,0:T(4,128)S(1)}...) custom-call(s32[8]{0:T(128)S(1)} %fusion.order, ...), custom_call_target="tpu_custom_call" | custom-call | flops 1000000 | bytes 837792 | tf_op jit(solution)/shard_map/pallas_call | solution.py:303
  17.3 7.1 %all-to-all-done.wa = bf16[4,160,1024]{2,1,0:T(8,128)(2,1)S(1)} async-done(((bf16[4,160,1024]{2,1,0:T(8,128)(2,1)}), bf16[4,160,1024]{2,1,0:T(8,128)(2,1)S(1)}, u32[]{:S(2)}, u32[]{:S(2)}) %all-to-all-start) | async-done | bytes 1310752 | tf_op jit(solution)/shard_map/all_to_all | solution.py:348
  24.4 1.9 %collective-permute-start.1 = (bf16[4,160,1024]{2,1,0:T(8,128)(2,1)S(1)}, bf16[4,160,1024]{2,1,0:T(8,128)(2,1)S(1)}, u32[]{:S(2)}, u32[]{:S(2)}) collective-permute-start(bf16[4,160,1024]{2,1,0:T(8,128)(2,1)S(1)} %all-to-all-done.wa), channel_id=1, source_target_pairs={{0,1},{1,0},{2,3},{3,2},{4,5},{5,4},{6,7},{7,6},{8,9},{9,8},{10,11... | collective-permute-start | bytes 3932168 | tf_op jit(solution)/shard_map/ppermute | solution.py:346
  26.3 2.5 %collective-permute-start.4 = (bf16[256,1024]{1,0:T(8,128)(2,1)}, bf16[256,1024]{1,0:T(8,128)(2,1)}, u32[]{:S(2)}, u32[]{:S(2)}) collective-permute-start(bf16[256,1024]{1,0:T(8,128)(2,1)} %get-tuple-element.48), channel_id=1, source_target_pairs={{0,4},{2,6},{4,0},{6,2},{1,5},{3,7},{5,1},{7,3},{8,12},{10,14},{12... | collective-permute-start | bytes 1572872 | tf_op jit(solution)/shard_map/ppermute | solution.py:364
  28.8 3.4 %collective-permute-start.2 = (bf16[256,1024]{1,0:T(8,128)(2,1)}, bf16[256,1024]{1,0:T(8,128)(2,1)}, u32[]{:S(2)}, u32[]{:S(2)}) collective-permute-start(bf16[256,1024]{1,0:T(8,128)(2,1)} %get-tuple-element.48), channel_id=1, source_target_pairs={{0,2},{2,4},{4,6},{6,0},{1,3},{3,5},{5,7},{7,1},{8,10},{10,12},{12... | collective-permute-start | bytes 1572872 | tf_op jit(solution)/shard_map/ppermute | solution.py:364
  32.2 3.7 %collective-permute-start.3 = (bf16[256,1024]{1,0:T(8,128)(2,1)}, bf16[256,1024]{1,0:T(8,128)(2,1)}, u32[]{:S(2)}, u32[]{:S(2)}) collective-permute-start(bf16[256,1024]{1,0:T(8,128)(2,1)} %get-tuple-element.48), channel_id=1, source_target_pairs={{0,6},{2,0},{4,2},{6,4},{1,7},{3,1},{5,3},{7,5},{8,14},{10,8},{12,... | collective-permute-start | bytes 1572872 | tf_op jit(solution)/shard_map/ppermute | solution.py:364
  35.9 0.0 collective-permute-done.1.wb
  35.9 2.7 %shard_map.120 = (bf16[128,1024]{1,0:T(8,128)(2,1)S(1)}, bf16[128,128]{1,0:T(8,128)(2,1)S(1)}, f32[16,128]{1,0:T(8,128)S(1)}, f32[16,128]{1,0:T(8,128)S(1)}, bf16[8,72,128]{2,1,0:T(8,128)(2,1)}) custom-call(bf16[144,1024]{1,0:T(8,128)(2,1)S(1)} %get-tuple-element.33.src_ref, bf16[4,160,1024]{2,1,0:T(8,128)(2,1)S(1)} %all-to-all-done.wa, ...), custom_call_target="tpu_custom_call" | custom-call | flops 335544320 | bytes 2934912 | tf_op jit(solution)/shard_map/pallas_call | solution.py:303
  38.6 7.6 %all-to-all-start.1 = ((bf16[8,72,128]{2,1,0:T(8,128)(2,1)}), bf16[8,72,128]{2,1,0:T(8,128)(2,1)S(1)}, u32[]{:S(2)}, u32[]{:S(2)}) async-start(bf16[8,72,128]{2,1,0:T(8,128)(2,1)} %get-tuple-element.43), calls=%async_computation.1 | async-start | bytes 294912 | tf_op jit(solution)/shard_map/all_to_all | solution.py:381
  46.1 1.9 %collective-permute-start.5 = (bf16[256,1024]{1,0:T(8,128)(2,1)}, bf16[256,1024]{1,0:T(8,128)(2,1)S(1)}, u32[]{:S(2)}, u32[]{:S(2)}) collective-permute-start(bf16[256,1024]{1,0:T(8,128)(2,1)} %get-tuple-element.48), channel_id=1, source_target_pairs={{0,1},{1,0},{2,3},{3,2},{4,5},{5,4},{6,7},{7,6},{8,9},{9,8},{10,11... | collective-permute-start | bytes 1572872 | tf_op jit(solution)/shard_map/ppermute | solution.py:346
  48.0 0.0 collective-permute-done.4.refs_4_
  48.0 2.4 %collective-permute-start.6 = (bf16[256,1024]{1,0:T(8,128)(2,1)}, bf16[256,1024]{1,0:T(8,128)(2,1)S(1)}, u32[]{:S(2)}, u32[]{:S(2)}) collective-permute-start(bf16[256,1024]{1,0:T(8,128)(2,1)} %collective-permute-done.4.refs_4_), channel_id=1, source_target_pairs={{0,1},{1,0},{2,3},{3,2},{4,5},{5,4},{6,7},{7,6},{8,9},{9,8},{10,11... | collective-permute-start | bytes 1572872 | tf_op jit(solution)/shard_map/ppermute | solution.py:346
  50.5 5.2 %collective-permute-done.2.refs_2_ = bf16[256,1024]{1,0:T(8,128)(2,1)} collective-permute-done((bf16[256,1024]{1,0:T(8,128)(2,1)}, bf16[256,1024]{1,0:T(8,128)(2,1)}, u32[]{:S(2)}, u32[]{:S(2)}) %collective-permute-start.2) | collective-permute-done | bytes 524320 | tf_op jit(solution)/shard_map/ppermute | solution.py:364
  55.6 1.9 %collective-permute-start.7 = (bf16[256,1024]{1,0:T(8,128)(2,1)}, bf16[256,1024]{1,0:T(8,128)(2,1)S(1)}, u32[]{:S(2)}, u32[]{:S(2)}) collective-permute-start(bf16[256,1024]{1,0:T(8,128)(2,1)} %collective-permute-done.2.refs_2_), channel_id=1, source_target_pairs={{0,1},{1,0},{2,3},{3,2},{4,5},{5,4},{6,7},{7,6},{8,9},{9,8},{10,11... | collective-permute-start | bytes 1572872 | tf_op jit(solution)/shard_map/ppermute | solution.py:346
  57.6 0.0 collective-permute-done.3.refs_3_
  57.6 2.4 %collective-permute-start.8 = (bf16[256,1024]{1,0:T(8,128)(2,1)}, bf16[256,1024]{1,0:T(8,128)(2,1)}, u32[]{:S(2)}, u32[]{:S(2)}) collective-permute-start(bf16[256,1024]{1,0:T(8,128)(2,1)} %collective-permute-done.3.refs_3_), channel_id=1, source_target_pairs={{0,1},{1,0},{2,3},{3,2},{4,5},{5,4},{6,7},{7,6},{8,9},{9,8},{10,11... | collective-permute-start | bytes 1572872 | tf_op jit(solution)/shard_map/ppermute | solution.py:346
  60.0 0.0 all-to-all-done.1.r_ref
  60.0 0.7 shard_map.122
  60.7 10.3 %all-to-all-start.2 = ((bf16[8,72,128]{2,1,0:T(8,128)(2,1)}), bf16[8,72,128]{2,1,0:T(8,128)(2,1)S(1)}, u32[]{:S(2)}, u32[]{:S(2)}) async-start(bf16[8,72,128]{2,1,0:T(8,128)(2,1)} %get-tuple-element.44), calls=%async_computation.2 | async-start | bytes 294912 | tf_op jit(solution)/shard_map/all_to_all | solution.py:399
  71.0 9.6 %all-to-all-done.2.r_ref = bf16[8,72,128]{2,1,0:T(8,128)(2,1)S(1)} async-done(((bf16[8,72,128]{2,1,0:T(8,128)(2,1)}), bf16[8,72,128]{2,1,0:T(8,128)(2,1)S(1)}, u32[]{:S(2)}, u32[]{:S(2)}) %all-to-all-start.2) | async-done | bytes 147488 | tf_op jit(solution)/shard_map/all_to_all | solution.py:399
  80.6 0.7 shard_map.123
  81.4 7.5 %all-to-all-start.3 = ((bf16[8,64,128]{2,1,0:T(8,128)(2,1)}), bf16[8,64,128]{2,1,0:T(8,128)(2,1)S(1)}, u32[]{:S(2)}, u32[]{:S(2)}) async-start(bf16[8,64,128]{2,1,0:T(8,128)(2,1)} %shard_map.123), calls=%async_computation.3 | async-start | bytes 262144 | tf_op jit(solution)/shard_map/all_to_all | solution.py:407
  88.9 0.0 collective-permute-done.5.refs_5_
  88.9 0.0 copy-start.1
  88.9 0.0 collective-permute-done.6.refs_6_
  88.9 0.0 copy-start.2
  88.9 0.0 collective-permute-done.7.refs_7_
  89.0 0.0 copy-start.3
  89.0 0.0 collective-permute-done.8.refs_8_
  89.0 0.7 copy-done.1
  89.7 0.2 copy-done.2
  89.9 0.1 copy-done.3
  90.0 0.0 copy-start
  90.0 2.8 %shard_map.124 = (bf16[128,1024]{1,0:T(8,128)(2,1)S(1)}, bf16[1024,1024]{1,0:T(8,128)(2,1)S(1)}) custom-call(s32[8]{0:T(128)S(1)} %fusion.1.order, bf16[128,1024]{1,0:T(8,128)(2,1)S(1)} %get-tuple-element.47.f_ref, bf16[128,1024]{1,0:T(8,128)(2,1)} %refs_0_.3, bf16[128,1024]{1,0:T(8,128)(2,1)} %refs_1_.3, bf16[256,1024]{1,0:T(8,128)(2,1)} %collective-permute-done.2.refs_2_, ...), custom_call_target="tpu_custom_call" | custom-call | flops 268435456 | bytes 4456480 | tf_op jit(solution)/shard_map/pallas_call | solution.py:303
  92.9 0.7 shard_map.121.y_ref
  93.6 3.0 %all-to-all-done.3 = bf16[8,64,128]{2,1,0:T(8,128)(2,1)S(1)} async-done(((bf16[8,64,128]{2,1,0:T(8,128)(2,1)}), bf16[8,64,128]{2,1,0:T(8,128)(2,1)S(1)}, u32[]{:S(2)}, u32[]{:S(2)}) %all-to-all-start.3) | async-done | bytes 131104 | tf_op jit(solution)/shard_map/all_to_all | solution.py:407
  96.5 0.0 copy-done
  96.5 2.3 %shard_map.125 = bf16[128,1024]{1,0:T(8,128)(2,1)} custom-call(s32[8]{0:T(128)S(1)} %fusion.1.order, f32[128,1024]{1,0:T(8,128)S(1)} %shard_map.121.y_ref, bf16[512,128]{1,0:T(8,128)(2,1)S(1)} %bitcast.8, bf16[128,128]{1,0:T(8,128)(2,1)S(1)} %get-tuple-element.40.bc_ref, f32[16,128]{1,0:T(8,128)S(1)} %get-tuple-element.42.cum_ref, ...), custom_call_target="tpu_custom_call" | custom-call | flops 268435456 | bytes 3059744 | tf_op jit(solution)/shard_map/pallas_call | solution.py:303
  (2 shorter events, 0.0 us)
Async XLA Ops:
  2.2 7.8 %copy-start.4 = (s32[8]{0:T(128)S(1)}, s32[8]{0:T(128)}, u32[]{:S(2)}) copy-start(s32[8]{0:T(128)} %constant.94) | copy-start | bytes 100
  2.2 7.8 %copy-start.5 = (s32[8]{0:T(128)S(1)}, s32[8]{0:T(128)}, u32[]{:S(2)}) copy-start(s32[8]{0:T(128)} %constant.80) | copy-start | bytes 100
  2.2 22.2 %all-to-all-start = ((bf16[4,160,1024]{2,1,0:T(8,128)(2,1)}), bf16[4,160,1024]{2,1,0:T(8,128)(2,1)S(1)}, u32[]{:S(2)}, u32[]{:S(2)}) async-start(bf16[4,160,1024]{2,1,0:T(8,128)(2,1)} %get-tuple-element.28), calls=%async_computation | async-start | bytes 2621440 | tf_op jit(solution)/shard_map/all_to_all | solution.py:348
  6.5 8.2 %collective-permute-start = (bf16[16,1024]{1,0:T(8,128)(2,1)S(1)}, bf16[16,1024]{1,0:T(8,128)(2,1)S(1)}, u32[]{:S(2)}, u32[]{:S(2)}) collective-permute-start(bf16[16,1024]{1,0:T(8,128)(2,1)S(1)} %get-tuple-element.29), channel_id=1, source_target_pairs={{0,8},{8,16},{16,24},{24,32},{32,40},{40,48},{48,56},{56,64},{64,7... | collective-permute-start | bytes 98312 | tf_op jit(solution)/shard_map/ppermute | solution.py:349
  24.4 11.5 %collective-permute-start.1 = (bf16[4,160,1024]{2,1,0:T(8,128)(2,1)S(1)}, bf16[4,160,1024]{2,1,0:T(8,128)(2,1)S(1)}, u32[]{:S(2)}, u32[]{:S(2)}) collective-permute-start(bf16[4,160,1024]{2,1,0:T(8,128)(2,1)S(1)} %all-to-all-done.wa), channel_id=1, source_target_pairs={{0,1},{1,0},{2,3},{3,2},{4,5},{5,4},{6,7},{7,6},{8,9},{9,8},{10,11... | collective-permute-start | bytes 3932168 | tf_op jit(solution)/shard_map/ppermute | solution.py:346
  26.3 21.7 %collective-permute-start.4 = (bf16[256,1024]{1,0:T(8,128)(2,1)}, bf16[256,1024]{1,0:T(8,128)(2,1)}, u32[]{:S(2)}, u32[]{:S(2)}) collective-permute-start(bf16[256,1024]{1,0:T(8,128)(2,1)} %get-tuple-element.48), channel_id=1, source_target_pairs={{0,4},{2,6},{4,0},{6,2},{1,5},{3,7},{5,1},{7,3},{8,12},{10,14},{12... | collective-permute-start | bytes 1572872 | tf_op jit(solution)/shard_map/ppermute | solution.py:364
  28.8 26.8 %collective-permute-start.2 = (bf16[256,1024]{1,0:T(8,128)(2,1)}, bf16[256,1024]{1,0:T(8,128)(2,1)}, u32[]{:S(2)}, u32[]{:S(2)}) collective-permute-start(bf16[256,1024]{1,0:T(8,128)(2,1)} %get-tuple-element.48), channel_id=1, source_target_pairs={{0,2},{2,4},{4,6},{6,0},{1,3},{3,5},{5,7},{7,1},{8,10},{10,12},{12... | collective-permute-start | bytes 1572872 | tf_op jit(solution)/shard_map/ppermute | solution.py:364
  32.2 25.4 %collective-permute-start.3 = (bf16[256,1024]{1,0:T(8,128)(2,1)}, bf16[256,1024]{1,0:T(8,128)(2,1)}, u32[]{:S(2)}, u32[]{:S(2)}) collective-permute-start(bf16[256,1024]{1,0:T(8,128)(2,1)} %get-tuple-element.48), channel_id=1, source_target_pairs={{0,6},{2,0},{4,2},{6,4},{1,7},{3,1},{5,3},{7,5},{8,14},{10,8},{12,... | collective-permute-start | bytes 1572872 | tf_op jit(solution)/shard_map/ppermute | solution.py:364
  38.6 21.4 %all-to-all-start.1 = ((bf16[8,72,128]{2,1,0:T(8,128)(2,1)}), bf16[8,72,128]{2,1,0:T(8,128)(2,1)S(1)}, u32[]{:S(2)}, u32[]{:S(2)}) async-start(bf16[8,72,128]{2,1,0:T(8,128)(2,1)} %get-tuple-element.43), calls=%async_computation.1 | async-start | bytes 294912 | tf_op jit(solution)/shard_map/all_to_all | solution.py:381
  46.1 42.8 %collective-permute-start.5 = (bf16[256,1024]{1,0:T(8,128)(2,1)}, bf16[256,1024]{1,0:T(8,128)(2,1)S(1)}, u32[]{:S(2)}, u32[]{:S(2)}) collective-permute-start(bf16[256,1024]{1,0:T(8,128)(2,1)} %get-tuple-element.48), channel_id=1, source_target_pairs={{0,1},{1,0},{2,3},{3,2},{4,5},{5,4},{6,7},{7,6},{8,9},{9,8},{10,11... | collective-permute-start | bytes 1572872 | tf_op jit(solution)/shard_map/ppermute | solution.py:346
  48.0 40.9 %collective-permute-start.6 = (bf16[256,1024]{1,0:T(8,128)(2,1)}, bf16[256,1024]{1,0:T(8,128)(2,1)S(1)}, u32[]{:S(2)}, u32[]{:S(2)}) collective-permute-start(bf16[256,1024]{1,0:T(8,128)(2,1)} %collective-permute-done.4.refs_4_), channel_id=1, source_target_pairs={{0,1},{1,0},{2,3},{3,2},{4,5},{5,4},{6,7},{7,6},{8,9},{9,8},{10,11... | collective-permute-start | bytes 1572872 | tf_op jit(solution)/shard_map/ppermute | solution.py:346
  55.6 33.3 %collective-permute-start.7 = (bf16[256,1024]{1,0:T(8,128)(2,1)}, bf16[256,1024]{1,0:T(8,128)(2,1)S(1)}, u32[]{:S(2)}, u32[]{:S(2)}) collective-permute-start(bf16[256,1024]{1,0:T(8,128)(2,1)} %collective-permute-done.2.refs_2_), channel_id=1, source_target_pairs={{0,1},{1,0},{2,3},{3,2},{4,5},{5,4},{6,7},{7,6},{8,9},{9,8},{10,11... | collective-permute-start | bytes 1572872 | tf_op jit(solution)/shard_map/ppermute | solution.py:346
  57.6 31.4 %collective-permute-start.8 = (bf16[256,1024]{1,0:T(8,128)(2,1)}, bf16[256,1024]{1,0:T(8,128)(2,1)}, u32[]{:S(2)}, u32[]{:S(2)}) collective-permute-start(bf16[256,1024]{1,0:T(8,128)(2,1)} %collective-permute-done.3.refs_3_), channel_id=1, source_target_pairs={{0,1},{1,0},{2,3},{3,2},{4,5},{5,4},{6,7},{7,6},{8,9},{9,8},{10,11... | collective-permute-start | bytes 1572872 | tf_op jit(solution)/shard_map/ppermute | solution.py:346
  60.7 19.9 %all-to-all-start.2 = ((bf16[8,72,128]{2,1,0:T(8,128)(2,1)}), bf16[8,72,128]{2,1,0:T(8,128)(2,1)S(1)}, u32[]{:S(2)}, u32[]{:S(2)}) async-start(bf16[8,72,128]{2,1,0:T(8,128)(2,1)} %get-tuple-element.44), calls=%async_computation.2 | async-start | bytes 294912 | tf_op jit(solution)/shard_map/all_to_all | solution.py:399
  81.4 15.2 %all-to-all-start.3 = ((bf16[8,64,128]{2,1,0:T(8,128)(2,1)}), bf16[8,64,128]{2,1,0:T(8,128)(2,1)S(1)}, u32[]{:S(2)}, u32[]{:S(2)}) async-start(bf16[8,64,128]{2,1,0:T(8,128)(2,1)} %shard_map.123), calls=%async_computation.3 | async-start | bytes 262144 | tf_op jit(solution)/shard_map/all_to_all | solution.py:407
  88.9 0.8 copy-start.1
  88.9 1.0 copy-start.2
  89.0 1.1 %copy-start.3 = (bf16[256,1024]{1,0:T(8,128)(2,1)}, bf16[256,1024]{1,0:T(8,128)(2,1)S(1)}, u32[]{:S(2)}) copy-start(bf16[256,1024]{1,0:T(8,128)(2,1)S(1)} %collective-permute-done.7.refs_7_) | copy-start | bytes 1572868
  90.0 6.5 %copy-start = (f32[1024]{0:T(1024)S(1)}, f32[1024]{0:T(1024)}, u32[]{:S(2)}) copy-start(f32[1024]{0:T(1024)} %param.21) | copy-start | bytes 12292
